TPU v7x, 128 devices: a whole 4x4x4 slice. The times are simulated.
128 devices in a mesh: group: 4 (over y), tm: 32 (over x, z, core).
Axes of the slice: x: 4, y: 4, z: 4, core: 2. Of those that a mesh axis runs over, the one named last changes fastest.
Arguments:
- precip: bfloat16 [4, 128, 1440, 720], P('group', 'tm'), may hold values from 0.099609375 to 4
- day_bins: int32 [128], replicated, may hold values from 0 to 15
- family_of: int32 [4], replicated, may hold values from 0 to 2
Outputs:
- day_mean: bfloat16 [4, 16, 1440, 720], P('group', None, 'tm')
- day_second: bfloat16 [4, 16, 1440, 720], P('group', None, 'tm')
- day_third: bfloat16 [4, 16, 1440, 720], P('group', None, 'tm')
- family_mean: bfloat16 [3, 16, 1440, 720], P(None, None, 'tm')
- anomaly_norm: float32 [4, 128], replicated
All inputs are finite; a program needn't handle non-finite values.
Results may differ from a plain program's by a relative error of at most 0.001.
The roundings to bfloat16 on the way count: a program that leaves them out, or rounds other values in their place, can miss the bound.
Values may be sent and summed in bfloat16 or wider, within the bound.
No kernel may reach another device: no remote copies, remote signals or barrier semaphores. Data moves between devices by JAX's collectives and lax.ppermute only.
A program may use at most 192 MiB of HBM per device.

v0:
```python
import math

import jax
import jax.numpy as jnp
from jax import lax
from jax.sharding import PartitionSpec as P

LON = 1440
DAYS = 16
FAM = 3


def from_everyone(array, axis):
    copies = jnp.broadcast_to(array, (lax.axis_size(axis), *array.shape))
    return lax.all_to_all(copies, axis, split_axis=0, concat_axis=0, tiled=True)


def of_everyone(array, axis):
    return from_everyone(array, axis).sum(axis=0)


def joined_along(tiles, dim):
    tiles = jnp.moveaxis(tiles, 0, dim)
    lengths = tiles.shape
    return tiles.reshape(*lengths[:dim], lengths[dim] * lengths[dim + 1], *lengths[dim + 2 :])


def collect(array, axis, dim):
    return joined_along(from_everyone(array, axis), dim)


def lat_weight(count):
    rows_idx = jnp.arange(count, dtype=jnp.float32)
    return jnp.cos((-90.0 + (rows_idx + 0.5) * 180.0 / count) * (math.pi / 180.0))


def local(precip, day_bins, family_of):
    lat_count = precip.shape[3]
    onehot = day_bins[None, :] == jnp.arange(DAYS, dtype=jnp.int32)[:, None]
    onehot_f = onehot.astype(jnp.float32)
    onehot_b = onehot.astype(jnp.bfloat16)
    divisor = jnp.maximum(jnp.sum(onehot_f, axis=1), 1.0)
    weight = lat_weight(lat_count)
    total_weight = LON * jnp.sum(weight)
    fields = lax.all_to_all(precip, "tm", split_axis=2, concat_axis=1, tiled=True)
    items, steps, band, lats = fields.shape
    flat_cells = fields.reshape(items, steps, band * lats)
    bin_sums = jnp.einsum("dt,ktc->kdc", onehot_b, flat_cells, preferred_element_type=jnp.float32)
    means = bin_sums / divisor[None, :, None]
    anomaly = flat_cells.astype(jnp.float32) - jnp.take(means, day_bins, axis=1)
    square = anomaly * anomaly
    second = (
        jnp.einsum("dt,ktc->kdc", onehot_f, square, precision=lax.Precision.HIGHEST)
        / divisor[None, :, None]
    )
    third = (
        jnp.einsum("dt,ktc->kdc", onehot_f, square * anomaly, precision=lax.Precision.HIGHEST)
        / divisor[None, :, None]
    )
    weighted = jnp.sum(
        square.reshape(items, steps, band, lats) * weight[None, None, None, :], axis=(2, 3)
    )
    shape = (items, DAYS, band, lats)
    day_mean, day_second, day_third, weighted = (
        means.astype(jnp.bfloat16).reshape(shape),
        second.astype(jnp.bfloat16).reshape(shape),
        third.astype(jnp.bfloat16).reshape(shape),
        weighted,
    )
    family_hot = (family_of[None, :] == jnp.arange(FAM, dtype=jnp.int32)[:, None]).astype(
        jnp.float32
    )
    family_count = jnp.maximum(jnp.sum(family_hot, axis=1), 1.0)
    every_mean = lax.all_gather(day_mean, "group", axis=0, tiled=True)
    summed = jnp.einsum(
        "fm,mdbl->fdbl",
        family_hot.astype(jnp.bfloat16),
        every_mean,
        preferred_element_type=jnp.float32,
    )
    family_mean = (summed / family_count[:, None, None, None]).astype(jnp.bfloat16)
    band_total = of_everyone(weighted, "tm")
    norm_value = jnp.sqrt(band_total / total_weight)
    anomaly_norm = collect(norm_value, "group", 0)
    return (day_mean, day_second, day_third, family_mean, anomaly_norm)


def solution(mesh):
    in_specs = (P("group", "tm", None, None), P(), P())
    out_specs = (
        P("group", None, "tm", None),
        P("group", None, "tm", None),
        P("group", None, "tm", None),
        P(None, None, "tm", None),
        P(),
    )
    return jax.shard_map(local, mesh=mesh, in_specs=in_specs, out_specs=out_specs, check_vma=False)
```

profile of v0, /device:TPU:1, one launch (start us, length us, event | category | flops | bytes accessed | tf_op | source)
XLA Modules:
  0.0 329.1 jit_solution(11827919619380598518)
XLA Ops:
  7.2 24.5 %copy.40 = bf16[1,4,1440,720]{3,1,0,2:T(4,128)(2,1)} copy(bf16[1,4,1440,720]{3,2,1,0:T(8,128)(2,1)} %param.3) | data formatting | bytes 16588800 | tf_op args[0]
  31.7 0.0 copy-start
  31.7 9.6 %all-to-all-start = ((bf16[1,4,1440,720]{3,1,0,2:T(4,128)(2,1)}), bf16[1,4,1440,720]{3,1,0,2:T(4,128)(2,1)}, u32[]{:S(2)}, u32[]{:S(2)}) async-start(bf16[1,4,1440,720]{3,1,0,2:T(4,128)(2,1)} %copy.40), calls=%async_computation | async-start | bytes 17694720 | tf_op jit(solution)/shard_map/all_to_all | solution.py:45
  41.3 0.0 all-gather.2.cloned.1.call-start
  41.4 0.0 copy-done
  41.4 0.1 convert_reduce_fusion
  41.5 114.9 %all-to-all-done = bf16[1,4,1440,720]{3,1,0,2:T(4,128)(2,1)} async-done(((bf16[1,4,1440,720]{3,1,0,2:T(4,128)(2,1)}), bf16[1,4,1440,720]{3,1,0,2:T(4,128)(2,1)}, u32[]{:S(2)}, u32[]{:S(2)}) %all-to-all-start) | async-done | bytes 8294432 | tf_op jit(solution)/shard_map/all_to_all | solution.py:45
  156.4 9.0 %copy.41 = bf16[1,32,4,45,720]{4,3,2,1,0:T(8,128)(2,1)} copy(bf16[1,32,4,45,720]{4,2,3,1,0:T(4,128)(2,1)} %bitcast.1) | data formatting | bytes 16588800 | tf_op jit(solution)/shard_map/all_to_all | solution.py:45
  165.4 18.3 %reshape.118 = bf16[128,32400]{1,0:T(8,128)(2,1)} reshape(bf16[1,32,4,45,720]{4,3,2,1,0:T(8,128)(2,1)} %copy.41) | data formatting | bytes 16588800 | tf_op jit(solution)/shard_map/reshape.1
  183.7 0.0 copy-start.1
  183.7 5.5 %bitcast_convert_fusion = (bf16[1,16,32400]{2,1,0:T(8,128)(2,1)}, f32[1,32400,16]{1,2,0:T(8,128)S(1)}) fusion(f32[16]{0:T(128)S(1)} %broadcast_maximum_fusion.1, bf16[128,32400]{1,0:T(8,128)(2,1)} %reshape.118, s32[128]{0:T(128)S(1)} %copy-done), kind=kOutput, calls=%fused_computation.25 | convolution fusion | flops 133749248 | bytes 11405376 | tf_op jit(solution)/shard_map/dt,ktc->kdc/dot_general | solution.py:48
  189.2 3.3 %reshape.119 = bf16[1,16,45,720]{3,2,1,0:T(8,128)(2,1)S(1)} reshape(bf16[1,16,32400]{2,1,0:T(8,128)(2,1)} %get-tuple-element.30) | data formatting | bytes 2073600 | tf_op jit(solution)/shard_map/reshape | solution.py:65
  192.5 1.3 copy.46
  193.9 0.0 all-gather.2.cloned.1.call-update
  193.9 0.0 copy-done.1
  193.9 0.1 convert_reduce_fusion.1
  194.0 0.1 broadcast_in_dim.36
  194.1 0.7 fusion.20
  195.5 10.7 %gather_fusion = f32[128,32400]{1,0:T(8,128)} fusion(f32[16,32400]{1,0:T(8,128)S(1)} %bitcast.41, s32[1024]{0:T(1024)S(1)} %pad_clamp_fusion), kind=kCustom, calls=%fused_computation | custom fusion | bytes 33178112 | tf_op jit(solution)/shard_map/jit(_take)/gather | solution.py:50
  206.2 23.4 %gather.10 = f32[1,32,4,45,720]{4,3,2,1,0:T(8,128)} reshape(f32[128,32400]{1,0:T(8,128)} %gather_fusion) | data formatting | bytes 33177600 | tf_op jit(solution)/shard_map/jit(_take)/gather | solution.py:50
  229.6 21.3 %fusion.11 = f32[32,4]{1,0:T(8,128)S(1)} fusion(f32[1,32,4,45,720]{4,3,2,1,0:T(8,128)} %gather.10, bf16[1,32,4,45,720]{4,2,3,1,0:T(4,128)(2,1)} %bitcast.1, f32[720]{0:T(1024)S(1)} %multiply_cosine_fusion, pred[32,4]{1,0:T(8,128)(4,1)S(1)} %broadcast_in_dim.36), kind=kLoop, calls=%fused_computation.17 | loop fusion | flops 24883072 | bytes 24886720 | tf_op jit(solution)/shard_map/reduce_sum | solution.py:60
  250.9 0.1 reduce_sum.50
  251.0 0.6 broadcast_in_dim.39
  251.6 24.8 %all-to-all-start.1 = ((f32[32,1,128]{2,1,0:T(1,128)}), f32[32,1,128]{2,1,0:T(1,128)S(1)}, u32[]{:S(2)}, u32[]{:S(2)}) async-start(f32[32,1,128]{2,1,0:T(1,128)} %broadcast_in_dim.39), calls=%async_computation.1 | async-start | bytes 32768 | tf_op jit(solution)/shard_map/all_to_all | solution.py:15
  276.4 12.8 %fusion.6 = bf16[1,16,32400]{2,1,0:T(8,128)(2,1)S(1)} fusion(f32[128,32400]{1,0:T(8,128)} %gather_fusion, bf16[128,32400]{1,0:T(8,128)(2,1)} %reshape.118, pred[128]{0:T(512)(128)(4,1)S(1)} %compare_and_fusion, f32[16]{0:T(128)S(1)} %broadcast_maximum_fusion.1, s32[128]{0:T(128)S(1)} %copy-done), kind=kOutput, calls=%fused_computation.10 | convolution fusion | flops 818037248 | bytes 25920704 | tf_op jit(solution)/shard_map/dt,ktc->kdc/dot_general | solution.py:57
  289.2 0.0 all-to-all-done.1
  289.3 0.6 broadcast_in_dim.40
  289.9 4.2 %all-to-all-start.2 = ((f32[4,1,128]{2,1,0:T(1,128)}), f32[4,1,128]{2,1,0:T(1,128)S(1)}, u32[]{:S(2)}, u32[]{:S(2)}) async-start(f32[4,1,128]{2,1,0:T(1,128)} %broadcast_in_dim.40), calls=%async_computation.2 | async-start | bytes 4096 | tf_op jit(solution)/shard_map/all_to_all | solution.py:15
  294.0 12.3 %fusion.3 = bf16[1,16,32400]{2,1,0:T(8,128)(2,1)S(1)} fusion(f32[128,32400]{1,0:T(8,128)} %gather_fusion, bf16[128,32400]{1,0:T(8,128)(2,1)} %reshape.118, pred[128]{0:T(512)(128)(4,1)S(1)} %compare_and_fusion, f32[16]{0:T(128)S(1)} %broadcast_maximum_fusion.1, s32[128]{0:T(128)S(1)} %copy-done), kind=kOutput, calls=%fused_computation.7 | convolution fusion | flops 813890048 | bytes 25920704 | tf_op jit(solution)/shard_map/dt,ktc->kdc/dot_general | solution.py:53
  306.4 2.2 reshape.121
  308.6 1.3 copy.48
  309.9 2.2 reshape.120
  312.2 1.3 copy.47
  313.5 0.0 all-to-all-done.2
  313.5 0.0 all-gather.2.cloned.1.call-done
  313.5 6.0 %divide_convert_fusion = bf16[3,16,45,720]{3,0,2,1:T(4,128)(2,1)S(1)} fusion(bf16[4,16,45,720]{3,1,2,0:T(8,128)(2,1)} %all-gather.2.cloned.1.call-done, f32[3]{0:T(128)S(1)} %broadcast_maximum_fusion, s32[4]{0:T(128)S(1)} %copy-done.1), kind=kOutput, calls=%fused_computation.19 | convolution fusion | flops 15552036 | bytes 7257628 | tf_op jit(solution)/shard_map/fm,mdbl->fdbl/dot_general | solution.py:75
  319.5 2.2 copy.49
  321.7 0.6 copy.63
  (8 shorter events, 0.1 us)
Async XLA Ops:
  31.7 9.7 %copy-start = (s32[128]{0:T(128)S(1)}, s32[128]{0:T(128)}, u32[]{:S(2)}) copy-start(s32[128]{0:T(128)} %param.4) | copy-start | bytes 1540
  31.7 124.7 %all-to-all-start = ((bf16[1,4,1440,720]{3,1,0,2:T(4,128)(2,1)}), bf16[1,4,1440,720]{3,1,0,2:T(4,128)(2,1)}, u32[]{:S(2)}, u32[]{:S(2)}) async-start(bf16[1,4,1440,720]{3,1,0,2:T(4,128)(2,1)} %copy.40), calls=%async_computation | async-start | bytes 17694720 | tf_op jit(solution)/shard_map/all_to_all | solution.py:45
  41.3 272.2 %all-gather.2.cloned.1.call-start = ((), (), s32[]{:S(2)}) async-start(), calls=%async_computation.3 | async-start | bytes 5529600 | tf_op jit(solution)/shard_map/all_gather | solution.py:74
  183.7 10.2 %copy-start.1 = (s32[4]{0:T(128)S(1)}, s32[4]{0:T(128)}, u32[]{:S(2)}) copy-start(s32[4]{0:T(128)} %param.5) | copy-start | bytes 52
  251.6 37.7 %all-to-all-start.1 = ((f32[32,1,128]{2,1,0:T(1,128)}), f32[32,1,128]{2,1,0:T(1,128)S(1)}, u32[]{:S(2)}, u32[]{:S(2)}) async-start(f32[32,1,128]{2,1,0:T(1,128)} %broadcast_in_dim.39), calls=%async_computation.1 | async-start | bytes 32768 | tf_op jit(solution)/shard_map/all_to_all | solution.py:15
  289.9 23.6 %all-to-all-start.2 = ((f32[4,1,128]{2,1,0:T(1,128)}), f32[4,1,128]{2,1,0:T(1,128)S(1)}, u32[]{:S(2)}, u32[]{:S(2)}) async-start(f32[4,1,128]{2,1,0:T(1,128)} %broadcast_in_dim.40), calls=%async_computation.2 | async-start | bytes 4096 | tf_op jit(solution)/shard_map/all_to_all | solution.py:15
Sparse Core Ops, SparseCore 0:
  194.0 67.7 all-gather.1
where the time goes:
time: 330 us; the launch traced here: 329 us
  waiting for transfers between devices  115 us (35%)
  local copies, waits for them, and re-layouts  102 us (31%)
  starting transfers between devices  38.6 us (12%)
  matrix products  36.6 us (11%)
  other arithmetic  22.3 us (7%)
  between operations  14.8 us (4%)
    all_to_all x1, waiting for transfers between devices, local(): lax.all_to_all(precip, 'tm', split_axis=2, concat_axis=1, tiled=True)  115 us
    gather x2, local copies, waits for them, and re-layouts, local(): anomaly = flat_cells.astype(jnp.float32) - jnp.take(means, day_bins, axis=1)  34.1 us
    unnamed x10, local copies, waits for them, and re-layouts  31.2 us
    all_to_all x2, starting transfers between devices, from_everyone(): return lax.all_to_all(copies, axis, split_axis=0, concat_axis=0, tiled=True)  29 us
    reduce_sum x1, other arithmetic, local(): jnp.sum(square.reshape(items, steps, band, lats) * weight[None, None, Non...  21.3 us
    another operation x1, local copies, waits for them, and re-layouts  18.3 us
    dot_general x1, matrix products, local(): jnp.einsum('dt,ktc->kdc', onehot_f, square * anomaly, precision=lax.Preci...  12.8 us
    dot_general x1, matrix products, local(): jnp.einsum('dt,ktc->kdc', onehot_f, square, precision=lax.Precision.HIGHEST)  12.3 us
  transfers between devices with their start and end apart: 4, of which 1 were waited for; matrix products, arithmetic and copies ran while one was open for 27% of the time, Pallas kernels for 0%

commit v1 on v0

v1 whole, which is shorter than its diff:
```python
import functools
import math

import jax
import jax.numpy as jnp
import numpy as np
from jax import lax
from jax.experimental import pallas as pl
from jax.experimental.pallas import tpu as pltpu
from jax.sharding import PartitionSpec as P

LON = 1440
LAT = 720
DAYS = 16
FAM = 3
MODELS = 4
TIME = 128
LANES = 128
FULL = LAT // LANES
TAIL = LAT - FULL * LANES
HALF = TAIL // 2
PEERS = 32
BAND = LON // PEERS
BLOCK = 8 * BAND
CHUNKS = (8, 5, 2)

F32 = jnp.float32
BF16 = jnp.bfloat16


def rows_of(triples):
    return -(-17 * triples // 8) * 8


def packed_weight(triples):
    lat = np.arange(LAT, dtype=np.float64)
    weight = np.cos((-90.0 + (lat + 0.5) * 180.0 / LAT) * (math.pi / 180.0))
    count = 3 * triples
    rows = np.zeros((rows_of(triples), LANES))
    for j in range(FULL):
        rows[j * count : (j + 1) * count] = weight[j * LANES : (j + 1) * LANES]
    tail = weight[FULL * LANES :]
    for half in range(2):
        part = rows[FULL * count + half * triples : FULL * count + (half + 1) * triples]
        part[:, :TAIL] = tail
        part[:, TAIL : TAIL + HALF] = tail[half * HALF : (half + 1) * HALF]
    return rows.astype(np.float32), float(weight.sum() * LON)


def pack_kernel(first, triples, x_ref, out_ref, wide, rows):
    count = 3 * triples
    used = 17 * triples
    total = rows_of(triples)
    for j in range(FULL):
        wide[j] = x_ref[0, :, j * LANES : (j + 1) * LANES].astype(F32)
    wide[FULL, :, :TAIL] = x_ref[0, :, FULL * LANES :].astype(F32)
    if total > used:
        rows[total - 8 :, :] = jnp.zeros((8, LANES), F32)
    lane = lax.broadcasted_iota(jnp.int32, (triples, LANES), 1)
    for r in range(8):
        s = BAND * r + first
        for j in range(FULL):
            rows[j * count : (j + 1) * count, :] = wide[j, s : s + count, :]
        third = wide[FULL, s + 2 * triples : s + 3 * triples, :]
        for half in range(2):
            own = wide[FULL, s + half * triples : s + (half + 1) * triples, :]
            moved = pltpu.roll(third, TAIL - half * HALF, 1)
            rows[FULL * count + half * triples : FULL * count + (half + 1) * triples, :] = jnp.where(
                lane < TAIL, own, jnp.where(lane < TAIL + HALF, moved, 0.0)
            )
        out_ref[r, 0] = rows[...].astype(BF16)


def pack(x, first, triples):
    steps = x.shape[0]
    total = rows_of(triples)
    return pl.pallas_call(
        functools.partial(pack_kernel, first, triples),
        grid=(LON // BLOCK, steps),
        in_specs=[pl.BlockSpec((1, BLOCK, LAT), lambda q, t: (t, q, 0))],
        out_specs=pl.BlockSpec((8, 1, total, LANES), lambda q, t: (q, t, 0, 0)),
        out_shape=jax.ShapeDtypeStruct((PEERS, steps, total, LANES), BF16),
        scratch_shapes=[pltpu.VMEM((FULL + 1, BLOCK, LANES), F32), pltpu.VMEM((total, LANES), F32)],
        cost_estimate=pl.CostEstimate(flops=10_000_000, bytes_accessed=12_000_000, transcendentals=0),
        name=f"pack{first}",
    )(x)


def spread(value, day, total, table):
    table[pl.ds(day, total, stride=DAYS), :] = value


def unpack(table, out, triples):
    count = 3 * triples
    lane = lax.broadcasted_iota(jnp.int32, (DAYS, LANES), 1)

    def row(index):
        return table[pl.ds(pl.multiple_of(index * DAYS, DAYS), DAYS), :]

    def whole(lon, carry):
        for j in range(FULL):
            out[lon, :, j * LANES : (j + 1) * LANES] = row(j * count + lon).astype(BF16)
        return carry

    def tail(lon, carry):
        out[lon, :, FULL * LANES :] = row(FULL * count + lon)[:, :TAIL].astype(BF16)
        return carry

    def last(k, carry):
        low = pltpu.roll(row(FULL * count + k), LANES - TAIL, 1)
        high = pltpu.roll(row(FULL * count + triples + k), LANES - TAIL + HALF, 1)
        joined = jnp.where(lane < HALF, low, high)
        out[2 * triples + k, :, FULL * LANES :] = joined[:, :TAIL].astype(BF16)
        return carry

    lax.fori_loop(0, count, whole, 0)
    lax.fori_loop(0, 2 * triples, tail, 0)
    lax.fori_loop(0, triples, last, 0)


def moment_kernel(first, triples, chained, *refs):
    bins, inverse, x, weight, before = refs[:5]
    refs = refs[5 + (3 if chained else 0) :]
    day_mean, day_second, day_third, packed, after, mean, second, third, norm, table, wide, sem = refs
    total = rows_of(triples)
    count = 3 * triples
    tiles = total // 8

    zero = jnp.zeros((total, LANES), F32)
    for d in range(DAYS):
        mean[d] = zero
        second[d] = zero
        third[d] = zero

    def add(t, carry):
        d = bins[t]
        mean[d] = mean[d] + x[t].astype(F32)
        return carry

    lax.fori_loop(0, TIME, add, 0, unroll=4)

    for d in range(DAYS):
        value = mean[d] * inverse[d]
        mean[d] = value
        packed[d] = value.astype(BF16)
        spread(value, d, total, table)
    unpack(table, wide.at[0], triples)

    def moments(t, carry):
        d = bins[t]
        sums = None
        for k in range(tiles):
            at = slice(8 * k, 8 * k + 8)
            a = x[t, at].astype(F32) - mean[d, at]
            q = a * a
            second[d, at] = second[d, at] + q
            third[d, at] = third[d, at] + q * a
            w = q * weight[at]
            sums = w if sums is None else sums + w
        norm[t] = sums
        return carry

    lax.fori_loop(0, TIME, moments, 0, unroll=2)

    for slot, ref in ((1, second), (2, third)):
        for d in range(DAYS):
            spread(ref[d] * inverse[d], d, total, table)
        unpack(table, wide.at[slot], triples)

    by_time = jnp.sum(norm[...], axis=1)
    after[...] = before[...] + jnp.sum(by_time.T, axis=0, keepdims=True)

    copies = [
        pltpu.make_async_copy(wide.at[i], out.at[pl.ds(first, count)], sem.at[i])
        for i, out in enumerate((day_mean, day_second, day_third))
    ]
    for copy in copies:
        copy.start()
    for copy in copies:
        copy.wait()


def moments(bins, inverse, x, weight, before, outs, first, triples):
    total = rows_of(triples)
    count = 3 * triples
    smem = pl.BlockSpec(memory_space=pltpu.SMEM)
    vmem = pl.BlockSpec(memory_space=pltpu.VMEM)
    anywhere = pl.BlockSpec(memory_space=pl.ANY)
    chained = outs is not None
    field = jax.ShapeDtypeStruct((BAND, DAYS, LAT), BF16)
    result = pl.pallas_call(
        functools.partial(moment_kernel, first, triples, chained),
        in_specs=[smem, smem, vmem, vmem, vmem] + [anywhere] * (3 if chained else 0),
        out_specs=[anywhere] * 3 + [vmem, vmem],
        out_shape=[
            field,
            field,
            field,
            jax.ShapeDtypeStruct((DAYS, total, LANES), BF16),
            jax.ShapeDtypeStruct((1, TIME), F32),
        ],
        input_output_aliases={5: 0, 6: 1, 7: 2} if chained else {},
        scratch_shapes=[
            pltpu.VMEM((DAYS, total, LANES), F32),
            pltpu.VMEM((DAYS, total, LANES), F32),
            pltpu.VMEM((DAYS, total, LANES), F32),
            pltpu.VMEM((TIME, 8, LANES), F32),
            pltpu.VMEM((total * DAYS, LANES), F32),
            pltpu.VMEM((3, count, DAYS, LAT), BF16),
            pltpu.SemaphoreType.DMA((3,)),
        ],
        cost_estimate=pl.CostEstimate(flops=40_000_000 * triples, bytes_accessed=1_000_000 * triples, transcendentals=0),
        name=f"moments{first}",
    )(bins, inverse, x, weight, before, *(outs or ()))
    return result[:3], result[3], result[4]


def family_kernel(first, triples, chained, *refs):
    share = refs[0]
    own = refs[1:5]
    out, table, wide, sem = refs[5 + (1 if chained else 0) :]
    total = rows_of(triples)
    count = 3 * triples
    copies = []
    for f in range(FAM):
        for d in range(DAYS):
            value = own[0][d].astype(F32) * share[f, 0]
            for k in range(1, MODELS):
                value = value + own[k][d].astype(F32) * share[f, k]
            spread(value * share[f, MODELS], d, total, table)
        unpack(table, wide.at[f], triples)
        copies.append(pltpu.make_async_copy(wide.at[f], out.at[f, pl.ds(first, count)], sem.at[f]))
        copies[-1].start()
    for copy in copies:
        copy.wait()


def families(share, means, out, first, triples):
    total = rows_of(triples)
    count = 3 * triples
    vmem = pl.BlockSpec(memory_space=pltpu.VMEM)
    anywhere = pl.BlockSpec(memory_space=pl.ANY)
    chained = out is not None
    return pl.pallas_call(
        functools.partial(family_kernel, first, triples, chained),
        in_specs=[pl.BlockSpec(memory_space=pltpu.SMEM)] + [vmem] * MODELS + [anywhere] * (1 if chained else 0),
        out_specs=anywhere,
        out_shape=jax.ShapeDtypeStruct((FAM, BAND, DAYS, LAT), BF16),
        input_output_aliases={5: 0} if chained else {},
        scratch_shapes=[
            pltpu.VMEM((total * DAYS, LANES), F32),
            pltpu.VMEM((FAM, count, DAYS, LAT), BF16),
            pltpu.SemaphoreType.DMA((FAM,)),
        ],
        cost_estimate=pl.CostEstimate(flops=10_000_000 * triples, bytes_accessed=500_000 * triples, transcendentals=0),
        name=f"families{first}",
    )(share, *means, *(() if out is None else (out,)))


def local(precip, day_bins, family_of):
    days = jnp.arange(DAYS, dtype=jnp.int32)
    counts = jnp.sum((day_bins[None, :] == days[:, None]).astype(F32), axis=1)
    inverse = 1.0 / jnp.maximum(counts, 1.0)

    group = lax.axis_index("group")
    turned = (group - jnp.arange(MODELS, dtype=jnp.int32)) % MODELS
    hot = (family_of[None, :] == jnp.arange(FAM, dtype=jnp.int32)[:, None]).astype(F32)
    members = jnp.maximum(jnp.sum(hot, axis=1, keepdims=True), 1.0)
    picked = jnp.sum(
        hot[:, None, :] * (turned[:, None] == jnp.arange(MODELS, dtype=jnp.int32)[None, :]).astype(F32)[None],
        axis=2,
    )
    share = jnp.concatenate([picked, 1.0 / members], axis=1)

    x = precip[0]
    first = 0
    starts = []
    for triples in CHUNKS:
        starts.append(first)
        first += 3 * triples
    sent = [pack(x, s, n) for s, n in zip(starts, CHUNKS)]
    got = [lax.all_to_all(p, "tm", split_axis=0, concat_axis=0, tiled=True) for p in sent]

    outs, fam = None, None
    norm = jnp.zeros((1, TIME), F32)
    for s, n, g in zip(starts, CHUNKS, got):
        weight, total_weight = packed_weight(n)
        outs, mean, norm = moments(
            day_bins, inverse, g.reshape(TIME, rows_of(n), LANES), jnp.asarray(weight), norm, outs, s, n
        )
        means = [mean] + [
            lax.ppermute(mean, "group", [(i, (i + k) % MODELS) for i in range(MODELS)]) for k in range(1, MODELS)
        ]
        fam = families(share, means, fam, s, n)

    mine = jnp.where(jnp.arange(MODELS, dtype=jnp.int32)[:, None] == group, norm, 0.0)
    anomaly_norm = jnp.sqrt(lax.psum(mine, ("group", "tm")) / total_weight)
    fields = [o[None].transpose(0, 2, 1, 3) for o in outs]
    return (*fields, fam.transpose(0, 2, 1, 3), anomaly_norm)


def solution(mesh):
    in_specs = (P("group", "tm", None, None), P(), P())
    out_specs = (
        P("group", None, "tm", None),
        P("group", None, "tm", None),
        P("group", None, "tm", None),
        P(None, None, "tm", None),
        P(),
    )
    return jax.shard_map(local, mesh=mesh, in_specs=in_specs, out_specs=out_specs, check_vma=False)
```

time: 330 us -> 277 us (0.84)
  local copies, waits for them, and re-layouts: 102 us -> 5.37 us
  blocking collectives: 0 us -> 87 us
  Pallas kernels: 0 us -> 77.1 us
  waiting for transfers between devices: 115 us -> 68.8 us
  matrix products: 36.6 us -> 0 us
  other arithmetic: 22.3 us -> 2.84 us
  between operations: 14.8 us -> 1.01 us
  starting transfers between devices: 38.6 us -> 33.2 us
    psum x0 -> x1, blocking collectives: none -> 87 us  [local(): anomaly_norm = jnp.sqrt(lax.psum(mine, ('group', 'tm')) / total_weight)]
    pallas_call x0 -> x9, Pallas kernels: none -> 77.1 us  [the longest x3 34.6 us: pack(): pl.pallas_call(functools.partial(pack_kernel, first, triples), grid=(LON...]
    all_to_all x3, waiting for transfers between devices: 115 us -> 68.8 us  [local(): lax.all_to_all(p, 'tm', split_axis=0, concat_axis=0, tiled=True)]
    dot_general x4 -> x0, matrix products: 36.6 us -> none  [the longest x1 12.8 us: local(): jnp.einsum('dt,ktc->kdc', onehot_f, square * anomaly, precision=lax.Preci...]
    gather x2 -> x0, local copies, waits for them, and re-layouts: 34.1 us -> none  [local(): anomaly = flat_cells.astype(jnp.float32) - jnp.take(means, day_bins, axis=1)]
    unnamed x10 -> x24, local copies, waits for them, and re-layouts: 31.2 us -> 4.76 us
    reduce_sum x5 -> x3, other arithmetic: 22.2 us -> 0.32 us  [the longest x1 0.12 us: local(): members = jnp.maximum(jnp.sum(hot, axis=1, keepdims=True), 1.0)]
    another operation x1 -> x0, local copies, waits for them, and re-layouts: 18.3 us -> none
  transfers between devices with their start and end apart: 4 -> 12, of which waited for: 1 -> 2; matrix products, arithmetic and copies ran while one was open for 27% -> 1% of each run, Pallas kernels for 0% -> 23%
where the time goes in v1:
time: 277 us; the launch traced here: 275 us
  blocking collectives  87 us (31%)
  Pallas kernels  77.1 us (28%)
  waiting for transfers between devices  68.8 us (25%)
  starting transfers between devices  33.2 us (12%)
  local copies, waits for them, and re-layouts  5.37 us (2%)
  other arithmetic  2.84 us (1%)
    psum x1, blocking collectives, local(): anomaly_norm = jnp.sqrt(lax.psum(mine, ('group', 'tm')) / total_weight)  87 us
    all_to_all x3, waiting for transfers between devices, local(): lax.all_to_all(p, 'tm', split_axis=0, concat_axis=0, tiled=True)  68.8 us
    pallas_call x3, Pallas kernels, pack(): pl.pallas_call(functools.partial(pack_kernel, first, triples), grid=(LON...  34.6 us
    pallas_call x3, Pallas kernels, moments(): pl.pallas_call(functools.partial(moment_kernel, first, triples, chained),...  28 us
    all_to_all x3, starting transfers between devices, local(): lax.all_to_all(p, 'tm', split_axis=0, concat_axis=0, tiled=True)  22 us
    pallas_call x3, Pallas kernels, families(): pl.pallas_call(functools.partial(family_kernel, first, triples, chained),...  14.5 us
    ppermute x9, starting transfers between devices, local(): lax.ppermute(mean, 'group', [(i, (i + k) % MODELS) for i in range(MODELS)])  11.2 us
  transfers between devices with their start and end apart: 12, of which 2 were waited for; matrix products, arithmetic and copies ran while one was open for 1% of the time, Pallas kernels for 23%

profile of v1, /device:TPU:1, one launch (start us, length us, event | category | flops | bytes accessed | tf_op | source)
XLA Modules:
  0.0 275.4 jit_solution(9463796170715480667)
XLA Ops:
  0.6 11.7 %pack24.1 = bf16[32,4,88,128]{3,2,1,0:T(8,128)(2,1)} custom-call(bf16[4,1440,720]{2,1,0:T(8,128)(2,1)} %bitcast.17), custom_call_target="tpu_custom_call" | custom-call | flops 10000000 | bytes 12000000 | tf_op jit(solution)/shard_map/pack24/pallas_call | solution.py:77
  12.3 9.4 %all-to-all-start.1 = ((bf16[32,4,88,128]{3,2,1,0:T(8,128)(2,1)}), bf16[32,4,88,128]{3,2,1,0:T(8,128)(2,1)S(1)}, u32[]{:S(2)}, u32[]{:S(2)}) async-start(bf16[32,4,88,128]{3,2,1,0:T(8,128)(2,1)} %pack24.1), calls=%async_computation.1 | async-start | bytes 5767168 | tf_op jit(solution)/shard_map/all_to_all | solution.py:282
  21.7 11.7 %pack0.1 = bf16[32,4,136,128]{3,2,1,0:T(8,128)(2,1)} custom-call(bf16[4,1440,720]{2,1,0:T(8,128)(2,1)} %bitcast.18), custom_call_target="tpu_custom_call" | custom-call | flops 10000000 | bytes 12000000 | tf_op jit(solution)/shard_map/pack0/pallas_call | solution.py:77
  33.4 25.0 %all-to-all-done.1 = bf16[32,4,88,128]{3,2,1,0:T(8,128)(2,1)S(1)} async-done(((bf16[32,4,88,128]{3,2,1,0:T(8,128)(2,1)}), bf16[32,4,88,128]{3,2,1,0:T(8,128)(2,1)S(1)}, u32[]{:S(2)}, u32[]{:S(2)}) %all-to-all-start.1) | async-done | bytes 2883616 | tf_op jit(solution)/shard_map/all_to_all | solution.py:282
  58.4 1.6 copy-done
  60.0 5.4 %all-to-all-start.2 = ((bf16[32,4,136,128]{3,2,1,0:T(8,128)(2,1)}), bf16[32,4,136,128]{3,2,1,0:T(8,128)(2,1)}, u32[]{:S(2)}, u32[]{:S(2)}) async-start(bf16[32,4,136,128]{3,2,1,0:T(8,128)(2,1)} %pack0.1), calls=%async_computation.2 | async-start | bytes 8912896 | tf_op jit(solution)/shard_map/all_to_all | solution.py:282
  65.4 0.0 copy-start.11
  65.4 0.0 copy-start.10
  65.4 11.3 %pack39.1 = bf16[32,4,40,128]{3,2,1,0:T(8,128)(2,1)} custom-call(bf16[4,1440,720]{2,1,0:T(8,128)(2,1)} %bitcast.19), custom_call_target="tpu_custom_call" | custom-call | flops 10000000 | bytes 12000000 | tf_op jit(solution)/shard_map/pack39/pallas_call | solution.py:77
  76.7 0.1 fusion.3
  76.8 0.1 convert_reduce_fusion
  77.0 43.8 %all-to-all-done.2 = bf16[32,4,136,128]{3,2,1,0:T(8,128)(2,1)} async-done(((bf16[32,4,136,128]{3,2,1,0:T(8,128)(2,1)}), bf16[32,4,136,128]{3,2,1,0:T(8,128)(2,1)}, u32[]{:S(2)}, u32[]{:S(2)}) %all-to-all-start.2) | async-done | bytes 4456480 | tf_op jit(solution)/shard_map/all_to_all | solution.py:282
  120.7 7.2 %all-to-all-start = ((bf16[32,4,40,128]{3,2,1,0:T(8,128)(2,1)}), bf16[32,4,40,128]{3,2,1,0:T(8,128)(2,1)S(1)}, u32[]{:S(2)}, u32[]{:S(2)}) async-start(bf16[32,4,40,128]{3,2,1,0:T(8,128)(2,1)} %pack39.1), calls=%async_computation | async-start | bytes 2621440 | tf_op jit(solution)/shard_map/all_to_all | solution.py:282
  127.9 0.5 maximum_divide_fusion.refs_1_
  128.5 0.1 fusion.1
  128.5 0.5 broadcast_in_dim.44.refs_4_
  129.1 12.8 %moments0.1 = (bf16[45,16,720]{2,1,0:T(8,128)(2,1)}, bf16[45,16,720]{2,1,0:T(8,128)(2,1)}, bf16[45,16,720]{2,1,0:T(8,128)(2,1)}, bf16[16,136,128]{2,1,0:T(8,128)(2,1)}, f32[1,128]{1,0:T(1,128)}) custom-call(s32[128]{0:T(128)} %refs_0_.5, f32[16]{0:T(128)} %maximum_divide_fusion.refs_1_, bf16[128,136,128]{2,1,0:T(8,128)(2,1)} %bitcast.3.refs_2_, ...), custom_call_target="tpu_custom_call" | custom-call | flops 320000000 | bytes 8000000 | tf_op jit(solution)/shard_map/moments0/pallas_call | solution.py:191
  141.9 9.3 %moments24.1 = (bf16[45,16,720]{2,1,0:T(8,128)(2,1)}, bf16[45,16,720]{2,1,0:T(8,128)(2,1)}, bf16[45,16,720]{2,1,0:T(8,128)(2,1)}, bf16[16,88,128]{2,1,0:T(8,128)(2,1)}, f32[1,128]{1,0:T(1,128)}) custom-call(s32[128]{0:T(128)} %refs_0_.5, f32[16]{0:T(128)} %maximum_divide_fusion.refs_1_, ...), custom_call_target="tpu_custom_call", output_to_operand_aliasing={{0}: (5, {}), {1}: (6, {}), {2}: (7, {})} | custom-call | flops 200000000 | bytes 5000000 | tf_op jit(solution)/shard_map/moments24/pallas_call | solution.py:191
  151.2 1.4 collective-permute-start.3
  152.6 0.1 copy.20
  152.7 1.3 collective-permute-start.6
  154.0 1.4 collective-permute-start.7
  155.4 2.0 collective-permute-start.8
  157.4 0.1 multiply_reduce_fusion
  157.5 0.6 pad_maximum_fusion.refs_0_
  158.1 0.3 collective-permute-start.4
  158.5 1.1 copy-done.1
  159.6 5.8 %moments39.1 = (bf16[45,16,720]{2,1,0:T(8,128)(2,1)}, bf16[45,16,720]{2,1,0:T(8,128)(2,1)}, bf16[45,16,720]{2,1,0:T(8,128)(2,1)}, bf16[16,40,128]{2,1,0:T(8,128)(2,1)}, f32[1,128]{1,0:T(1,128)}) custom-call(s32[128]{0:T(128)} %refs_0_.5, f32[16]{0:T(128)} %maximum_divide_fusion.refs_1_, ...), custom_call_target="tpu_custom_call", output_to_operand_aliasing={{0}: (5, {}), {1}: (6, {}), {2}: (7, {})} | custom-call | flops 80000000 | bytes 2000000 | tf_op jit(solution)/shard_map/moments39/pallas_call | solution.py:191
  165.4 1.6 collective-permute-start.5
  167.0 0.7 broadcast_select_fusion
  167.7 87.0 %psum.7 = f32[4,128]{1,0:T(4,128)S(1)} all-reduce(f32[4,128]{1,0:T(4,128)S(1)} %broadcast_select_fusion), channel_id=1, replica_groups=mesh['group'=4,'tm'=32] {'group','tm'}, use_global_device_ids=true, to_apply=%region_3.4 | all-reduce | flops 512 | bytes 4096 | tf_op jit(solution)/shard_map/psum | solution.py:297
  254.7 0.0 collective-permute-done.6.refs_2_
  254.7 0.1 collective-permute-start
  254.8 0.0 collective-permute-done.7.refs_3_
  254.8 1.7 collective-permute-start.1
  256.5 0.0 collective-permute-done.8.refs_4_
  256.5 1.4 collective-permute-start.2
  257.9 0.6 multiply_sqrt_fusion
  258.5 6.7 %families0.1.refs_5_ = bf16[3,45,16,720]{3,2,1,0:T(8,128)(2,1)} custom-call(f32[3,5]{1,0:T(4,128)} %pad_maximum_fusion.refs_0_, bf16[16,136,128]{2,1,0:T(8,128)(2,1)} %get-tuple-element.33.refs_1_, bf16[16,136,128]{2,1,0:T(8,128)(2,1)} %copy-done.3, bf16[16,136,128]{2,1,0:T(8,128)(2,1)} %copy-done.4, bf16[16,136,128]{2,1,0:T(8,128)(2,1)} %copy-done.5), custom_call_target="tpu_custom_call" | custom-call | flops 80000000 | bytes 4000000 | tf_op jit(solution)/shard_map/families0/pallas_call | solution.py:244
  265.3 0.0 collective-permute-done.5.refs_4_
  265.3 0.7 copy-done.6
  266.1 4.8 %families24.1.refs_5_ = bf16[3,45,16,720]{3,2,1,0:T(8,128)(2,1)} custom-call(f32[3,5]{1,0:T(4,128)} %pad_maximum_fusion.refs_0_, bf16[16,88,128]{2,1,0:T(8,128)(2,1)} %get-tuple-element.32.refs_1_, bf16[16,88,128]{2,1,0:T(8,128)(2,1)} %collective-permute-done.3.refs_2_, ...), custom_call_target="tpu_custom_call", output_to_operand_aliasing={{}: (5, {})} | custom-call | flops 50000000 | bytes 2500000 | tf_op jit(solution)/shard_map/families24/pallas_call | solution.py:244
  270.9 0.0 collective-permute-done.refs_2_
  270.9 0.0 collective-permute-done.1.refs_3_
  270.9 0.6 copy-done.7
  271.5 0.1 copy-done.8
  271.6 0.7 copy-done.9
  272.3 2.9 %families39.1 = bf16[3,45,16,720]{3,2,1,0:T(8,128)(2,1)} custom-call(f32[3,5]{1,0:T(4,128)} %pad_maximum_fusion.refs_0_, bf16[16,40,128]{2,1,0:T(8,128)(2,1)} %get-tuple-element.31.refs_1_, bf16[16,40,128]{2,1,0:T(8,128)(2,1)} %copy-done.7, bf16[16,40,128]{2,1,0:T(8,128)(2,1)} %copy-done.8, ...), custom_call_target="tpu_custom_call", output_to_operand_aliasing={{}: (5, {})} | custom-call | flops 20000000 | bytes 1000000 | tf_op jit(solution)/shard_map/families39/pallas_call | solution.py:244
  (24 shorter events, 0.1 us)
Async XLA Ops:
  12.3 46.1 %all-to-all-start.1 = ((bf16[32,4,88,128]{3,2,1,0:T(8,128)(2,1)}), bf16[32,4,88,128]{3,2,1,0:T(8,128)(2,1)S(1)}, u32[]{:S(2)}, u32[]{:S(2)}) async-start(bf16[32,4,88,128]{3,2,1,0:T(8,128)(2,1)} %pack24.1), calls=%async_computation.1 | async-start | bytes 5767168 | tf_op jit(solution)/shard_map/all_to_all | solution.py:282
  58.4 1.6 copy-start
  60.0 60.7 %all-to-all-start.2 = ((bf16[32,4,136,128]{3,2,1,0:T(8,128)(2,1)}), bf16[32,4,136,128]{3,2,1,0:T(8,128)(2,1)}, u32[]{:S(2)}, u32[]{:S(2)}) async-start(bf16[32,4,136,128]{3,2,1,0:T(8,128)(2,1)} %pack0.1), calls=%async_computation.2 | async-start | bytes 8912896 | tf_op jit(solution)/shard_map/all_to_all | solution.py:282
  65.4 11.3 %copy-start.11 = (s32[4]{0:T(128)S(1)}, s32[4]{0:T(128)}, u32[]{:S(2)}) copy-start(s32[4]{0:T(128)} %param.8) | copy-start | bytes 52
  65.4 11.4 %copy-start.10 = (s32[128]{0:T(128)S(1)}, s32[128]{0:T(128)}, u32[]{:S(2)}) copy-start(s32[128]{0:T(128)} %refs_0_.5) | copy-start | bytes 1540
  120.7 37.8 %all-to-all-start = ((bf16[32,4,40,128]{3,2,1,0:T(8,128)(2,1)}), bf16[32,4,40,128]{3,2,1,0:T(8,128)(2,1)S(1)}, u32[]{:S(2)}, u32[]{:S(2)}) async-start(bf16[32,4,40,128]{3,2,1,0:T(8,128)(2,1)} %pack39.1), calls=%async_computation | async-start | bytes 2621440 | tf_op jit(solution)/shard_map/all_to_all | solution.py:282
  141.9 10.8 %copy-start.2 = (bf16[16,136,128]{2,1,0:T(8,128)(2,1)S(1)}, bf16[16,136,128]{2,1,0:T(8,128)(2,1)}, u32[]{:S(2)}) copy-start(bf16[16,136,128]{2,1,0:T(8,128)(2,1)} %get-tuple-element.33.refs_1_) | copy-start | bytes 1671172
  151.2 14.2 %collective-permute-start.3 = (bf16[16,88,128]{2,1,0:T(8,128)(2,1)}, bf16[16,88,128]{2,1,0:T(8,128)(2,1)}, u32[]{:S(2)}, u32[]{:S(2)}) collective-permute-start(bf16[16,88,128]{2,1,0:T(8,128)(2,1)} %get-tuple-element.32.refs_1_), channel_id=1, source_target_pairs={{0,32},{32,64},{64,96},{96,0},{1,33},{33,65},{65,97},{97,1},{2,34}... | collective-permute-start | bytes 1081352 | tf_op jit(solution)/shard_map/ppermute | solution.py:292
  152.7 102.0 %collective-permute-start.6 = (bf16[16,136,128]{2,1,0:T(8,128)(2,1)S(1)}, bf16[16,136,128]{2,1,0:T(8,128)(2,1)S(1)}, u32[]{:S(2)}, u32[]{:S(2)}) collective-permute-start(bf16[16,136,128]{2,1,0:T(8,128)(2,1)S(1)} %copy-done.2), channel_id=1, source_target_pairs={{0,32},{32,64},{64,96},{96,0},{1,33},{33,65},{65,97},{97,1},{2,34}... | collective-permute-start | bytes 1671176 | tf_op jit(solution)/shard_map/ppermute | solution.py:292
  154.0 100.8 %collective-permute-start.7 = (bf16[16,136,128]{2,1,0:T(8,128)(2,1)S(1)}, bf16[16,136,128]{2,1,0:T(8,128)(2,1)S(1)}, u32[]{:S(2)}, u32[]{:S(2)}) collective-permute-start(bf16[16,136,128]{2,1,0:T(8,128)(2,1)S(1)} %copy-done.2), channel_id=1, source_target_pairs={{0,64},{32,96},{64,0},{96,32},{1,65},{33,97},{65,1},{97,33},{2,66}... | collective-permute-start | bytes 1671176 | tf_op jit(solution)/shard_map/ppermute | solution.py:292
  155.4 101.1 %collective-permute-start.8 = (bf16[16,136,128]{2,1,0:T(8,128)(2,1)S(1)}, bf16[16,136,128]{2,1,0:T(8,128)(2,1)S(1)}, u32[]{:S(2)}, u32[]{:S(2)}) collective-permute-start(bf16[16,136,128]{2,1,0:T(8,128)(2,1)S(1)} %copy-done.2), channel_id=1, source_target_pairs={{0,96},{32,0},{64,32},{96,64},{1,97},{33,1},{65,33},{97,65},{2,98}... | collective-permute-start | bytes 1671176 | tf_op jit(solution)/shard_map/ppermute | solution.py:292
  158.1 107.1 %collective-permute-start.4 = (bf16[16,88,128]{2,1,0:T(8,128)(2,1)}, bf16[16,88,128]{2,1,0:T(8,128)(2,1)}, u32[]{:S(2)}, u32[]{:S(2)}) collective-permute-start(bf16[16,88,128]{2,1,0:T(8,128)(2,1)} %get-tuple-element.32.refs_1_), channel_id=1, source_target_pairs={{0,64},{32,96},{64,0},{96,32},{1,65},{33,97},{65,1},{97,33},{2,66}... | collective-permute-start | bytes 1081352 | tf_op jit(solution)/shard_map/ppermute | solution.py:292
  158.5 1.1 copy-start.1
  165.4 99.9 %collective-permute-start.5 = (bf16[16,88,128]{2,1,0:T(8,128)(2,1)}, bf16[16,88,128]{2,1,0:T(8,128)(2,1)S(1)}, u32[]{:S(2)}, u32[]{:S(2)}) collective-permute-start(bf16[16,88,128]{2,1,0:T(8,128)(2,1)} %get-tuple-element.32.refs_1_), channel_id=1, source_target_pairs={{0,96},{32,0},{64,32},{96,64},{1,97},{33,1},{65,33},{97,65},{2,98}... | collective-permute-start | bytes 1081352 | tf_op jit(solution)/shard_map/ppermute | solution.py:292
  254.7 3.8 %copy-start.3 = (bf16[16,136,128]{2,1,0:T(8,128)(2,1)}, bf16[16,136,128]{2,1,0:T(8,128)(2,1)S(1)}, u32[]{:S(2)}) copy-start(bf16[16,136,128]{2,1,0:T(8,128)(2,1)S(1)} %collective-permute-done.6.refs_2_) | copy-start | bytes 1671172
  254.7 16.2 %collective-permute-start = (bf16[16,40,128]{2,1,0:T(8,128)(2,1)}, bf16[16,40,128]{2,1,0:T(8,128)(2,1)S(1)}, u32[]{:S(2)}, u32[]{:S(2)}) collective-permute-start(bf16[16,40,128]{2,1,0:T(8,128)(2,1)} %get-tuple-element.31.refs_1_), channel_id=1, source_target_pairs={{0,32},{32,64},{64,96},{96,0},{1,33},{33,65},{65,97},{97,1},{2,34}... | collective-permute-start | bytes 491528 | tf_op jit(solution)/shard_map/ppermute | solution.py:292
  254.8 3.7 %copy-start.4 = (bf16[16,136,128]{2,1,0:T(8,128)(2,1)}, bf16[16,136,128]{2,1,0:T(8,128)(2,1)S(1)}, u32[]{:S(2)}) copy-start(bf16[16,136,128]{2,1,0:T(8,128)(2,1)S(1)} %collective-permute-done.7.refs_3_) | copy-start | bytes 1671172
  254.8 16.1 %collective-permute-start.1 = (bf16[16,40,128]{2,1,0:T(8,128)(2,1)}, bf16[16,40,128]{2,1,0:T(8,128)(2,1)S(1)}, u32[]{:S(2)}, u32[]{:S(2)}) collective-permute-start(bf16[16,40,128]{2,1,0:T(8,128)(2,1)} %get-tuple-element.31.refs_1_), channel_id=1, source_target_pairs={{0,64},{32,96},{64,0},{96,32},{1,65},{33,97},{65,1},{97,33},{2,66}... | collective-permute-start | bytes 491528 | tf_op jit(solution)/shard_map/ppermute | solution.py:292
  256.5 2.0 copy-start.5
  256.5 14.4 %collective-permute-start.2 = (bf16[16,40,128]{2,1,0:T(8,128)(2,1)}, bf16[16,40,128]{2,1,0:T(8,128)(2,1)S(1)}, u32[]{:S(2)}, u32[]{:S(2)}) collective-permute-start(bf16[16,40,128]{2,1,0:T(8,128)(2,1)} %get-tuple-element.31.refs_1_), channel_id=1, source_target_pairs={{0,96},{32,0},{64,32},{96,64},{1,97},{33,1},{65,33},{97,65},{2,98}... | collective-permute-start | bytes 491528 | tf_op jit(solution)/shard_map/ppermute | solution.py:292
  265.3 0.8 copy-start.6
  270.9 0.7 copy-start.7
  270.9 0.7 copy-start.8
  271.6 0.7 copy-start.9

commit v2 on v1

v2 whole, which is shorter than its diff:
```python
import functools
import math

import jax
import jax.numpy as jnp
import numpy as np
from jax import lax
from jax.experimental import pallas as pl
from jax.experimental.pallas import tpu as pltpu
from jax.sharding import PartitionSpec as P

LON = 1440
LAT = 720
DAYS = 16
FAM = 3
MODELS = 4
TIME = 128
LANES = 128
FULL = LAT // LANES
TAIL = LAT - FULL * LANES
HALF = TAIL // 2
PEERS = 32
BAND = LON // PEERS
BLOCK = 8 * BAND
CHUNKS = (11, 4)

F32 = jnp.float32
BF16 = jnp.bfloat16


def rows_of(triples):
    return -(-17 * triples // 8) * 8


def packed_weight(triples):
    lat = np.arange(LAT, dtype=np.float64)
    weight = np.cos((-90.0 + (lat + 0.5) * 180.0 / LAT) * (math.pi / 180.0))
    count = 3 * triples
    rows = np.zeros((rows_of(triples), LANES))
    for j in range(FULL):
        rows[j * count : (j + 1) * count] = weight[j * LANES : (j + 1) * LANES]
    tail = weight[FULL * LANES :]
    for half in range(2):
        part = rows[FULL * count + half * triples : FULL * count + (half + 1) * triples]
        part[:, :TAIL] = tail
        part[:, TAIL : TAIL + HALF] = tail[half * HALF : (half + 1) * HALF]
    return rows.astype(np.float32), float(weight.sum() * LON)


def pack_kernel(first, triples, steps, x, out, held, ready, wide, rows, got, put):
    count = 3 * triples
    used = 17 * triples
    total = rows_of(triples)
    pieces = LON // BLOCK * steps
    lane = lax.broadcasted_iota(jnp.int32, (triples, LANES), 1)

    def enter(i):
        q, t = i // steps, i % steps
        return pltpu.make_async_copy(x.at[t, pl.ds(pl.multiple_of(q * BLOCK, 8), BLOCK)], held.at[i], got.at[i])

    def leave(i):
        q, t = i // steps, i % steps
        return pltpu.make_async_copy(ready.at[i], out.at[pl.ds(q * 8, 8), t], put.at[i])

    for i in range(pieces):
        enter(i).start()
    if total > used:
        rows[total - 8 :, :] = jnp.zeros((8, LANES), F32)

    def piece(i, carry):
        enter(i).wait()
        for j in range(FULL):
            wide[j] = held[i, :, j * LANES : (j + 1) * LANES].astype(F32)
        wide[FULL, :, :TAIL] = held[i, :, FULL * LANES :].astype(F32)
        for r in range(8):
            s = BAND * r + first
            for j in range(FULL):
                rows[j * count : (j + 1) * count, :] = wide[j, s : s + count, :]
            third = wide[FULL, s + 2 * triples : s + 3 * triples, :]
            for half in range(2):
                own = wide[FULL, s + half * triples : s + (half + 1) * triples, :]
                moved = pltpu.roll(third, TAIL - half * HALF, 1)
                rows[FULL * count + half * triples : FULL * count + (half + 1) * triples, :] = jnp.where(
                    lane < TAIL, own, jnp.where(lane < TAIL + HALF, moved, 0.0)
                )
            ready[i, r] = rows[...].astype(BF16)
        leave(i).start()
        return carry

    lax.fori_loop(0, pieces, piece, 0)
    for i in range(pieces):
        leave(i).wait()


def pack(x, first, triples):
    steps = x.shape[0]
    total = rows_of(triples)
    pieces = LON // BLOCK * steps
    return pl.pallas_call(
        functools.partial(pack_kernel, first, triples, steps),
        in_specs=[pl.BlockSpec(memory_space=pl.ANY)],
        out_specs=pl.BlockSpec(memory_space=pl.ANY),
        out_shape=jax.ShapeDtypeStruct((PEERS, steps, total, LANES), BF16),
        scratch_shapes=[
            pltpu.VMEM((pieces, BLOCK, LAT), BF16),
            pltpu.VMEM((pieces, 8, total, LANES), BF16),
            pltpu.VMEM((FULL + 1, BLOCK, LANES), F32),
            pltpu.VMEM((total, LANES), F32),
            pltpu.SemaphoreType.DMA((pieces,)),
            pltpu.SemaphoreType.DMA((pieces,)),
        ],
        cost_estimate=pl.CostEstimate(flops=10_000_000, bytes_accessed=12_000_000, transcendentals=0),
        name=f"pack{first}",
    )(x)


def unpack(table, scale, out, triples):
    stride = rows_of(triples) + 1
    count = 3 * triples
    lane = lax.broadcasted_iota(jnp.int32, (DAYS, LANES), 1)

    def row(index):
        halves = [table[pl.ds(8 * h * stride + index, 8, stride=stride), :] for h in range(DAYS // 8)]
        value = jnp.concatenate(halves, axis=0)
        return value if scale is None else value * scale

    def whole(lon, carry):
        for j in range(FULL):
            out[lon, :, j * LANES : (j + 1) * LANES] = row(j * count + lon).astype(BF16)
        return carry

    def tail(lon, carry):
        out[lon, :, FULL * LANES :] = row(FULL * count + lon)[:, :TAIL].astype(BF16)
        return carry

    def last(k, carry):
        low = pltpu.roll(row(FULL * count + k), LANES - TAIL, 1)
        high = pltpu.roll(row(FULL * count + triples + k), LANES - TAIL + HALF, 1)
        joined = jnp.where(lane < HALF, low, high)
        out[2 * triples + k, :, FULL * LANES :] = joined[:, :TAIL].astype(BF16)
        return carry

    lax.fori_loop(0, count, whole, 0)
    lax.fori_loop(0, 2 * triples, tail, 0)
    lax.fori_loop(0, triples, last, 0)


SMEM = pl.BlockSpec(memory_space=pltpu.SMEM)
VMEM = pl.BlockSpec(memory_space=pltpu.VMEM)
ANY = pl.BlockSpec(memory_space=pl.ANY)
STEPS = 4
SPAN = TIME // STEPS


def sum_kernel(triples, bins, inverse, x, mean, packed):
    total = rows_of(triples)
    stride = total + 1
    step = pl.program_id(0)

    @pl.when(step == 0)
    def _():
        for d in range(DAYS):
            mean[d * stride : (d + 1) * stride, :] = jnp.zeros((stride, LANES), F32)

    def add(t, carry):
        at = bins[step * SPAN + t] * stride
        for k in range(total // 8):
            rows = pl.ds(at + 8 * k, 8)
            mean[rows, :] = mean[rows, :] + x[t, 8 * k : 8 * k + 8].astype(F32)
        return carry

    lax.fori_loop(0, SPAN, add, 0, unroll=4)

    @pl.when(step == STEPS - 1)
    def _():
        for d in range(DAYS):
            rows = slice(d * stride, d * stride + total)
            value = mean[rows, :] * inverse[d]
            mean[rows, :] = value
            packed[d] = value.astype(BF16)


def sums(bins, inverse, x, triples):
    total = rows_of(triples)
    return pl.pallas_call(
        functools.partial(sum_kernel, triples),
        grid=(STEPS,),
        in_specs=[SMEM, SMEM, pl.BlockSpec((SPAN, total, LANES), lambda i: (i, 0, 0))],
        out_specs=[
            pl.BlockSpec((DAYS * (total + 1), LANES), lambda i: (0, 0)),
            pl.BlockSpec((DAYS, total, LANES), lambda i: (0, 0, 0)),
        ],
        out_shape=[
            jax.ShapeDtypeStruct((DAYS * (total + 1), LANES), F32),
            jax.ShapeDtypeStruct((DAYS, total, LANES), BF16),
        ],
        cost_estimate=pl.CostEstimate(flops=10_000_000 * triples, bytes_accessed=700_000 * triples, transcendentals=0),
        name=f"sums{triples}",
    )(bins, inverse, x)


def moment_kernel(first, triples, chained, *refs):
    bins, x, mean, inverse, weight, before = refs[:6]
    refs = refs[6 + (3 if chained else 0) :]
    day_mean, day_second, day_third, after, second, third, norm, wide, sem = refs
    total = rows_of(triples)
    stride = total + 1
    count = 3 * triples
    step = pl.program_id(0)
    outs = (day_mean, day_second, day_third)

    def leave(i):
        return pltpu.make_async_copy(wide.at[i], outs[i].at[pl.ds(first, count)], sem.at[i])

    @pl.when(step == 0)
    def _():
        for d in range(DAYS):
            second[d * stride : (d + 1) * stride, :] = jnp.zeros((stride, LANES), F32)
            third[d * stride : (d + 1) * stride, :] = jnp.zeros((stride, LANES), F32)
        unpack(mean, None, wide.at[0], triples)
        leave(0).start()

    def moments(t, carry):
        at = bins[step * SPAN + t] * stride
        sums = None
        for k in range(total // 8):
            rows = pl.ds(at + 8 * k, 8)
            tile = slice(8 * k, 8 * k + 8)
            a = x[t, tile].astype(F32) - mean[rows, :]
            q = a * a
            second[rows, :] = second[rows, :] + q
            third[rows, :] = third[rows, :] + q * a
            w = q * weight[tile, :]
            sums = w if sums is None else sums + w
        norm[step * SPAN + t] = sums
        return carry

    lax.fori_loop(0, SPAN, moments, 0, unroll=2)

    @pl.when(step == STEPS - 1)
    def _():
        by_time = jnp.sum(norm[...], axis=1)
        after[...] = before[...] + jnp.sum(by_time.T, axis=0, keepdims=True)
        scale = inverse[...]
        unpack(second, scale, wide.at[1], triples)
        leave(1).start()
        unpack(third, scale, wide.at[2], triples)
        leave(2).start()
        for i in range(3):
            leave(i).wait()


def moments(bins, inverse, x, mean, weight, before, outs, first, triples):
    total = rows_of(triples)
    count = 3 * triples
    chained = outs is not None
    field = jax.ShapeDtypeStruct((BAND, DAYS, LAT), BF16)
    result = pl.pallas_call(
        functools.partial(moment_kernel, first, triples, chained),
        grid=(STEPS,),
        in_specs=[SMEM, pl.BlockSpec((SPAN, total, LANES), lambda i: (i, 0, 0))]
        + [VMEM] * 4
        + [ANY] * (3 if chained else 0),
        out_specs=[ANY] * 3 + [VMEM],
        out_shape=[field, field, field, jax.ShapeDtypeStruct((1, TIME), F32)],
        input_output_aliases={6: 0, 7: 1, 8: 2} if chained else {},
        scratch_shapes=[
            pltpu.VMEM((DAYS * (total + 1), LANES), F32),
            pltpu.VMEM((DAYS * (total + 1), LANES), F32),
            pltpu.VMEM((TIME, 8, LANES), F32),
            pltpu.VMEM((3, count, DAYS, LAT), BF16),
            pltpu.SemaphoreType.DMA((3,)),
        ],
        cost_estimate=pl.CostEstimate(flops=40_000_000 * triples, bytes_accessed=1_000_000 * triples, transcendentals=0),
        name=f"moments{first}",
    )(bins, x, mean, inverse, weight, before, *(outs or ()))
    return result[:3], result[3]


def family_kernel(first, triples, chained, *refs):
    share, own, right, left, low, high = refs[:6]
    out, table, wide, sem = refs[6 + (1 if chained else 0) :]
    total = rows_of(triples)
    stride = total + 1
    count = 3 * triples
    for d in range(DAYS):
        across = low[d] if d < DAYS // 2 else high[d - DAYS // 2]
        values = [v.astype(F32) for v in (own[d], right[d], left[d], across)]
        for f in range(FAM):
            value = values[0] * share[f, 0]
            for k in range(1, MODELS):
                value = value + values[k] * share[f, k]
            table[f, d * stride : d * stride + total, :] = value
    copies = []
    for f in range(FAM):
        unpack(table.at[f], None, wide.at[f], triples)
        copies.append(pltpu.make_async_copy(wide.at[f], out.at[f, pl.ds(first, count)], sem.at[f]))
        copies[-1].start()
    for copy in copies:
        copy.wait()


def families(share, means, out, first, triples):
    total = rows_of(triples)
    count = 3 * triples
    chained = out is not None
    return pl.pallas_call(
        functools.partial(family_kernel, first, triples, chained),
        in_specs=[SMEM] + [VMEM] * 5 + [ANY] * (1 if chained else 0),
        out_specs=ANY,
        out_shape=jax.ShapeDtypeStruct((FAM, BAND, DAYS, LAT), BF16),
        input_output_aliases={6: 0} if chained else {},
        scratch_shapes=[
            pltpu.VMEM((FAM, DAYS * (total + 1), LANES), F32),
            pltpu.VMEM((FAM, count, DAYS, LAT), BF16),
            pltpu.SemaphoreType.DMA((FAM,)),
        ],
        cost_estimate=pl.CostEstimate(flops=10_000_000 * triples, bytes_accessed=500_000 * triples, transcendentals=0),
        name=f"families{first}",
    )(share, *means, *(() if out is None else (out,)))


def from_others(mean):
    up = [(i, (i + 1) % MODELS) for i in range(MODELS)]
    down = [(i, (i - 1) % MODELS) for i in range(MODELS)]
    behind = lax.ppermute(mean, "group", up)
    ahead = lax.ppermute(mean, "group", down)
    low = lax.ppermute(behind[: DAYS // 2], "group", up)
    high = lax.ppermute(ahead[DAYS // 2 :], "group", down)
    return behind, ahead, low, high


def local(precip, day_bins, family_of):
    days = jnp.arange(DAYS, dtype=jnp.int32)
    counts = jnp.sum((day_bins[None, :] == days[:, None]).astype(F32), axis=1)
    inverse = 1.0 / jnp.maximum(counts, 1.0)
    inverse_rows = jnp.broadcast_to(inverse[:, None], (DAYS, LANES))

    group = lax.axis_index("group")
    turned = (group + jnp.array([0, MODELS - 1, 1, 2], dtype=jnp.int32)) % MODELS
    models = jnp.arange(MODELS, dtype=jnp.int32)
    hot = (family_of[None, :] == jnp.arange(FAM, dtype=jnp.int32)[:, None]).astype(F32)
    members = jnp.maximum(jnp.sum(hot, axis=1), 1.0)
    at = (turned[:, None] == models[None, :]).astype(F32)
    share = jnp.sum(hot[:, None, :] * at[None], axis=2) / members[:, None]

    x = precip[0]
    first = 0
    starts = []
    for triples in CHUNKS:
        starts.append(first)
        first += 3 * triples
    sent = [pack(x, s, n) for s, n in zip(starts, CHUNKS)]
    got = [lax.all_to_all(p, "tm", split_axis=0, concat_axis=0, tiled=True) for p in sent]

    outs, fam = None, None
    norm = jnp.zeros((1, TIME), F32)
    for s, n, g in zip(starts, CHUNKS, got):
        weight, total_weight = packed_weight(n)
        g = g.reshape(TIME, rows_of(n), LANES)
        mean, packed = sums(day_bins, inverse, g, n)
        means = (packed, *from_others(packed))
        outs, norm = moments(day_bins, inverse_rows, g, mean, jnp.asarray(weight), norm, outs, s, n)
        fam = families(share, means, fam, s, n)

    everyone = MODELS * PEERS
    parts = lax.all_to_all(
        jnp.broadcast_to(norm, (everyone, 1, TIME)), ("group", "tm"), split_axis=0, concat_axis=0, tiled=True
    )
    anomaly_norm = jnp.sqrt(jnp.sum(parts.reshape(MODELS, PEERS, TIME), axis=1) / total_weight)
    fields = [o[None].transpose(0, 2, 1, 3) for o in outs]
    return (*fields, fam.transpose(0, 2, 1, 3), anomaly_norm)


def solution(mesh):
    in_specs = (P("group", "tm", None, None), P(), P())
    out_specs = (
        P("group", None, "tm", None),
        P("group", None, "tm", None),
        P("group", None, "tm", None),
        P(None, None, "tm", None),
        P(),
    )
    return jax.shard_map(local, mesh=mesh, in_specs=in_specs, out_specs=out_specs, check_vma=False)
```

time: 277 us -> 202 us (0.73)
  blocking collectives: 87 us -> 0 us
  waiting for transfers between devices: 68.8 us -> 98.3 us
  Pallas kernels: 77.1 us -> 51.5 us
  starting transfers between devices: 33.2 us -> 40.6 us
    psum x1 -> x0, blocking collectives: 87 us -> none  [local(): anomaly_norm = jnp.sqrt(lax.psum(mine, ('group', 'tm')) / total_weight)]
    all_to_all x3 -> x2, waiting for transfers between devices: 68.8 us -> 93.8 us  [local(): lax.all_to_all(p, 'tm', split_axis=0, concat_axis=0, tiled=True)]
    pallas_call x3 -> x4, Pallas kernels: 34.6 us -> 21 us  [the longest x2 11.3 us: pack(): pl.pallas_call(functools.partial(pack_kernel, first, triples, steps), in_...]
    pallas_call x3 -> x2, Pallas kernels: 28 us -> 19.1 us  [moments(): pl.pallas_call(functools.partial(moment_kernel, first, triples, chained),...]
    all_to_all x0 -> x1, starting transfers between devices: none -> 5.15 us  [local(): lax.all_to_all(jnp.broadcast_to(norm, (everyone, 1, TIME)), ('group', 'tm...]
    pallas_call x3 -> x2, Pallas kernels: 14.5 us -> 11.4 us  [families(): pl.pallas_call(functools.partial(family_kernel, first, triples, chained),...]
    all_to_all x3 -> x2, starting transfers between devices: 22 us -> 24.1 us  [local(): lax.all_to_all(p, 'tm', split_axis=0, concat_axis=0, tiled=True)]
    ppermute x9 -> x8, starting transfers between devices: 11.2 us -> 11.3 us  [the longest x2 4.22 us: from_others(): high = lax.ppermute(ahead[DAYS // 2:], 'group', down)]
  transfers between devices with their start and end apart: 12 -> 11, of which waited for: 2 -> 5; matrix products, arithmetic and copies ran while one was open for 1% -> 3% of each run, Pallas kernels for 23% -> 21%
where the time goes in v2:
time: 202 us; the launch traced here: 200 us
  waiting for transfers between devices  98.3 us (49%)
  Pallas kernels  51.5 us (25%)
  starting transfers between devices  40.6 us (20%)
  local copies, waits for them, and re-layouts  6.42 us (3%)
  other arithmetic  2.21 us (1%)
    all_to_all x2, waiting for transfers between devices, local(): lax.all_to_all(p, 'tm', split_axis=0, concat_axis=0, tiled=True)  93.8 us
    all_to_all x2, starting transfers between devices, local(): lax.all_to_all(p, 'tm', split_axis=0, concat_axis=0, tiled=True)  24.1 us
    pallas_call x2, Pallas kernels, moments(): pl.pallas_call(functools.partial(moment_kernel, first, triples, chained),...  19.1 us
    pallas_call x2, Pallas kernels, families(): pl.pallas_call(functools.partial(family_kernel, first, triples, chained),...  11.4 us
    pallas_call x2, Pallas kernels, pack(): pl.pallas_call(functools.partial(pack_kernel, first, triples, steps), in_...  11.3 us
    pallas_call x2, Pallas kernels, sums(): pl.pallas_call(functools.partial(sum_kernel, triples), grid=(STEPS,), in_...  9.67 us
    all_to_all x1, starting transfers between devices, local(): lax.all_to_all(jnp.broadcast_to(norm, (everyone, 1, TIME)), ('group', 'tm...  5.15 us
    ppermute x2, starting transfers between devices, from_others(): high = lax.ppermute(ahead[DAYS // 2:], 'group', down)  4.22 us
  transfers between devices with their start and end apart: 11, of which 5 were waited for; matrix products, arithmetic and copies ran while one was open for 3% of the time, Pallas kernels for 21%

profile of v2, /device:TPU:1, one launch (start us, length us, event | category | flops | bytes accessed | tf_op | source)
XLA Modules:
  0.0 199.9 jit_solution(9825729822035989578)
XLA Ops:
  0.6 6.2 %pack0.1 = bf16[32,4,192,128]{3,2,1,0:T(8,128)(2,1)} custom-call(bf16[4,1440,720]{2,1,0:T(8,128)(2,1)} %bitcast.17), custom_call_target="tpu_custom_call" | custom-call | flops 10000000 | bytes 12000000 | tf_op jit(solution)/shard_map/pack0/pallas_call | solution.py:99
  6.8 9.5 %all-to-all-start.1 = ((bf16[32,4,192,128]{3,2,1,0:T(8,128)(2,1)}), bf16[32,4,192,128]{3,2,1,0:T(8,128)(2,1)}, u32[]{:S(2)}, u32[]{:S(2)}) async-start(bf16[32,4,192,128]{3,2,1,0:T(8,128)(2,1)} %pack0.1), calls=%async_computation.1 | async-start | bytes 12582912 | tf_op jit(solution)/shard_map/all_to_all | solution.py:354
  16.3 5.1 %pack33.1 = bf16[32,4,72,128]{3,2,1,0:T(8,128)(2,1)} custom-call(bf16[4,1440,720]{2,1,0:T(8,128)(2,1)} %bitcast.18), custom_call_target="tpu_custom_call" | custom-call | flops 10000000 | bytes 12000000 | tf_op jit(solution)/shard_map/pack33/pallas_call | solution.py:99
  21.4 0.0 copy-start.9
  21.5 0.0 copy-start.7
  21.5 72.1 %all-to-all-done.1 = bf16[32,4,192,128]{3,2,1,0:T(8,128)(2,1)} async-done(((bf16[32,4,192,128]{3,2,1,0:T(8,128)(2,1)}), bf16[32,4,192,128]{3,2,1,0:T(8,128)(2,1)}, u32[]{:S(2)}, u32[]{:S(2)}) %all-to-all-start.1) | async-done | bytes 6291488 | tf_op jit(solution)/shard_map/all_to_all | solution.py:354
  93.6 14.7 %all-to-all-start = ((bf16[32,4,72,128]{3,2,1,0:T(8,128)(2,1)}), bf16[32,4,72,128]{3,2,1,0:T(8,128)(2,1)S(1)}, u32[]{:S(2)}, u32[]{:S(2)}) async-start(bf16[32,4,72,128]{3,2,1,0:T(8,128)(2,1)} %pack33.1), calls=%async_computation | async-start | bytes 4718592 | tf_op jit(solution)/shard_map/all_to_all | solution.py:354
  108.3 0.1 fusion.3
  108.4 0.1 convert_reduce_fusion
  108.5 0.5 maximum_divide_fusion.inverse
  109.1 5.8 %sums11.1 = (f32[3088,128]{1,0:T(8,128)}, bf16[16,192,128]{2,1,0:T(8,128)(2,1)}) custom-call(s32[128]{0:T(128)} %refs_0_.3, f32[16]{0:T(128)} %maximum_divide_fusion.inverse, bf16[128,192,128]{2,1,0:T(8,128)(2,1)} %bitcast.2.x.refs_1_), custom_call_target="tpu_custom_call" | custom-call | flops 110000000 | bytes 7700000 | tf_op jit(solution)/shard_map/sums11/pallas_call | solution.py:185
  114.9 1.3 collective-permute-start.4
  116.2 1.5 collective-permute-start.5
  117.7 0.1 fusion.1
  117.8 21.6 %all-to-all-done = bf16[32,4,72,128]{3,2,1,0:T(8,128)(2,1)S(1)} async-done(((bf16[32,4,72,128]{3,2,1,0:T(8,128)(2,1)}), bf16[32,4,72,128]{3,2,1,0:T(8,128)(2,1)S(1)}, u32[]{:S(2)}, u32[]{:S(2)}) %all-to-all-start) | async-done | bytes 2359328 | tf_op jit(solution)/shard_map/all_to_all | solution.py:354
  139.4 1.4 copy-done
  140.8 3.8 %sums4.1 = (f32[1168,128]{1,0:T(8,128)}, bf16[16,72,128]{2,1,0:T(8,128)(2,1)}) custom-call(s32[128]{0:T(128)} %refs_0_.3, f32[16]{0:T(128)} %maximum_divide_fusion.inverse, bf16[128,72,128]{2,1,0:T(8,128)(2,1)} %bitcast.19), custom_call_target="tpu_custom_call" | custom-call | flops 40000000 | bytes 2800000 | tf_op jit(solution)/shard_map/sums4/pallas_call | solution.py:185
  144.7 1.3 collective-permute-start
  146.0 1.4 collective-permute-start.1
  147.4 0.1 multiply_reduce_fusion
  147.5 0.7 broadcast_in_dim.12.refs_3_
  148.2 0.5 broadcast_in_dim.13.refs_5_
  148.7 12.3 %moments0.1 = (bf16[45,16,720]{2,1,0:T(8,128)(2,1)}, bf16[45,16,720]{2,1,0:T(8,128)(2,1)}, bf16[45,16,720]{2,1,0:T(8,128)(2,1)}, f32[1,128]{1,0:T(1,128)}) custom-call(s32[128]{0:T(128)} %refs_0_.3, bf16[128,192,128]{2,1,0:T(8,128)(2,1)} %bitcast.2.x.refs_1_, f32[3088,128]{1,0:T(8,128)} %get-tuple-element.18.refs_2_, f32[16,128]{1,0:T(8,128)} %broadcast_in_dim.12.refs_3_, ...), custom_call_target="tpu_custom_call" | custom-call | flops 440000000 | bytes 11000000 | tf_op jit(solution)/shard_map/moments0/pallas_call | solution.py:258
  161.0 6.8 %moments33.1 = (bf16[45,16,720]{2,1,0:T(8,128)(2,1)}, bf16[45,16,720]{2,1,0:T(8,128)(2,1)}, bf16[45,16,720]{2,1,0:T(8,128)(2,1)}, f32[1,128]{1,0:T(1,128)}) custom-call(s32[128]{0:T(128)} %refs_0_.3, bf16[128,72,128]{2,1,0:T(8,128)(2,1)} %bitcast.20, ...), custom_call_target="tpu_custom_call", output_to_operand_aliasing={{0}: (6, {}), {1}: (7, {}), {2}: (8, {})} | custom-call | flops 160000000 | bytes 4000000 | tf_op jit(solution)/shard_map/moments33/pallas_call | solution.py:258
  167.8 1.3 broadcast_in_dim.17
  169.1 5.2 %all-to-all-start.2 = ((f32[128,1,128]{2,1,0:T(1,128)}), f32[128,1,128]{2,1,0:T(1,128)S(1)}, u32[]{:S(2)}, u32[]{:S(2)}) async-start(f32[128,1,128]{2,1,0:T(1,128)} %broadcast_in_dim.17), calls=%async_computation.2 | async-start | bytes 131072 | tf_op jit(solution)/shard_map/all_to_all | solution.py:367
  174.3 0.0 collective-permute-done.4.refs_2_
  174.3 1.4 collective-permute-start.6
  175.8 0.0 collective-permute-done.5.refs_3_
  175.8 1.0 slice.19
  176.8 1.5 collective-permute-start.7
  178.3 0.7 broadcast_divide_fusion.refs_0_
  179.0 0.0 collective-permute-done.refs_2_
  179.0 0.1 collective-permute-start.2
  179.1 0.0 collective-permute-done.1.refs_3_
  179.1 2.7 %collective-permute-start.3 = (bf16[8,72,128]{2,1,0:T(8,128)(2,1)S(1)}, bf16[8,72,128]{2,1,0:T(8,128)(2,1)}, u32[]{:S(2)}, u32[]{:S(2)}) collective-permute-start(bf16[8,72,128]{2,1,0:T(8,128)(2,1)S(1)} %slice.17), channel_id=1, source_target_pairs={{0,96},{32,0},{64,32},{96,64},{1,97},{33,1},{65,33},{97,65},{2,98}... | collective-permute-start | bytes 442376 | tf_op jit(solution)/shard_map/ppermute | solution.py:329
  181.8 1.8 all-to-all-done.2
  183.7 0.6 multiply_sqrt_fusion
  184.3 1.8 collective-permute-done.6.refs_4_
  186.1 0.9 collective-permute-done.7.refs_5_
  187.0 0.7 copy-done.5
  187.7 7.6 %families0.1.refs_6_ = bf16[3,45,16,720]{3,2,1,0:T(8,128)(2,1)} custom-call(f32[3,4]{1,0:T(4,128)} %broadcast_divide_fusion.refs_0_, bf16[16,192,128]{2,1,0:T(8,128)(2,1)} %get-tuple-element.27.refs_1_, bf16[16,192,128]{2,1,0:T(8,128)(2,1)} %copy-done.1, bf16[16,192,128]{2,1,0:T(8,128)(2,1)} %collective-permute-done.5.refs_3_, ...), custom_call_target="tpu_custom_call" | custom-call | flops 110000000 | bytes 5500000 | tf_op jit(solution)/shard_map/families0/pallas_call | solution.py:307
  195.4 0.0 copy-done.2
  195.4 0.0 copy-done.3
  195.4 0.0 collective-permute-done.2.refs_4_
  195.4 0.0 collective-permute-done.3.refs_5_
  195.4 0.7 copy-done.6
  196.1 3.8 %families33.1 = bf16[3,45,16,720]{3,2,1,0:T(8,128)(2,1)} custom-call(f32[3,4]{1,0:T(4,128)} %broadcast_divide_fusion.refs_0_, bf16[16,72,128]{2,1,0:T(8,128)(2,1)} %get-tuple-element.26.refs_1_, bf16[16,72,128]{2,1,0:T(8,128)(2,1)} %copy-done.2, bf16[16,72,128]{2,1,0:T(8,128)(2,1)} %copy-done.3, ...), custom_call_target="tpu_custom_call", output_to_operand_aliasing={{}: (6, {})} | custom-call | flops 40000000 | bytes 2000000 | tf_op jit(solution)/shard_map/families33/pallas_call | solution.py:307
  (22 shorter events, 0.1 us)
Async XLA Ops:
  6.8 86.8 %all-to-all-start.1 = ((bf16[32,4,192,128]{3,2,1,0:T(8,128)(2,1)}), bf16[32,4,192,128]{3,2,1,0:T(8,128)(2,1)}, u32[]{:S(2)}, u32[]{:S(2)}) async-start(bf16[32,4,192,128]{3,2,1,0:T(8,128)(2,1)} %pack0.1), calls=%async_computation.1 | async-start | bytes 12582912 | tf_op jit(solution)/shard_map/all_to_all | solution.py:354
  21.4 86.8 %copy-start.9 = (s32[4]{0:T(128)S(1)}, s32[4]{0:T(128)}, u32[]{:S(2)}) copy-start(s32[4]{0:T(128)} %param.8) | copy-start | bytes 52
  21.5 86.9 %copy-start.7 = (s32[128]{0:T(128)S(1)}, s32[128]{0:T(128)}, u32[]{:S(2)}) copy-start(s32[128]{0:T(128)} %refs_0_.3) | copy-start | bytes 1540
  93.6 45.8 %all-to-all-start = ((bf16[32,4,72,128]{3,2,1,0:T(8,128)(2,1)}), bf16[32,4,72,128]{3,2,1,0:T(8,128)(2,1)S(1)}, u32[]{:S(2)}, u32[]{:S(2)}) async-start(bf16[32,4,72,128]{3,2,1,0:T(8,128)(2,1)} %pack33.1), calls=%async_computation | async-start | bytes 4718592 | tf_op jit(solution)/shard_map/all_to_all | solution.py:354
  109.0 8.6 %copy-start.10 = (s32[4]{0:T(128)S(1)}, s32[4]{0:T(128)}, u32[]{:S(2)}) copy-start(s32[4]{0:T(128)} %constant.36.clone) | copy-start | bytes 52
  114.9 32.6 %copy-start.8 = (f32[16]{0:T(128)S(1)}, f32[16]{0:T(128)}, u32[]{:S(2)}) copy-start(f32[16]{0:T(128)} %maximum_divide_fusion.inverse) | copy-start | bytes 196
  114.9 59.4 %collective-permute-start.4 = (bf16[16,192,128]{2,1,0:T(8,128)(2,1)}, bf16[16,192,128]{2,1,0:T(8,128)(2,1)S(1)}, u32[]{:S(2)}, u32[]{:S(2)}) collective-permute-start(bf16[16,192,128]{2,1,0:T(8,128)(2,1)} %get-tuple-element.27.refs_1_), channel_id=1, source_target_pairs={{0,32},{32,64},{64,96},{96,0},{1,33},{33,65},{65,97},{97,1},{2,34}... | collective-permute-start | bytes 2359304 | tf_op jit(solution)/shard_map/ppermute | solution.py:326
  116.2 59.6 %collective-permute-start.5 = (bf16[16,192,128]{2,1,0:T(8,128)(2,1)}, bf16[16,192,128]{2,1,0:T(8,128)(2,1)}, u32[]{:S(2)}, u32[]{:S(2)}) collective-permute-start(bf16[16,192,128]{2,1,0:T(8,128)(2,1)} %get-tuple-element.27.refs_1_), channel_id=1, source_target_pairs={{0,96},{32,0},{64,32},{96,64},{1,97},{33,1},{65,33},{97,65},{2,98}... | collective-permute-start | bytes 2359304 | tf_op jit(solution)/shard_map/ppermute | solution.py:327
  139.4 1.4 copy-start
  144.7 34.3 %collective-permute-start = (bf16[16,72,128]{2,1,0:T(8,128)(2,1)}, bf16[16,72,128]{2,1,0:T(8,128)(2,1)S(1)}, u32[]{:S(2)}, u32[]{:S(2)}) collective-permute-start(bf16[16,72,128]{2,1,0:T(8,128)(2,1)} %get-tuple-element.26.refs_1_), channel_id=1, source_target_pairs={{0,32},{32,64},{64,96},{96,0},{1,33},{33,65},{65,97},{97,1},{2,34}... | collective-permute-start | bytes 884744 | tf_op jit(solution)/shard_map/ppermute | solution.py:326
  146.0 33.1 %collective-permute-start.1 = (bf16[16,72,128]{2,1,0:T(8,128)(2,1)}, bf16[16,72,128]{2,1,0:T(8,128)(2,1)S(1)}, u32[]{:S(2)}, u32[]{:S(2)}) collective-permute-start(bf16[16,72,128]{2,1,0:T(8,128)(2,1)} %get-tuple-element.26.refs_1_), channel_id=1, source_target_pairs={{0,96},{32,0},{64,32},{96,64},{1,97},{33,1},{65,33},{97,65},{2,98}... | collective-permute-start | bytes 884744 | tf_op jit(solution)/shard_map/ppermute | solution.py:327
  169.1 14.5 %all-to-all-start.2 = ((f32[128,1,128]{2,1,0:T(1,128)}), f32[128,1,128]{2,1,0:T(1,128)S(1)}, u32[]{:S(2)}, u32[]{:S(2)}) async-start(f32[128,1,128]{2,1,0:T(1,128)} %broadcast_in_dim.17), calls=%async_computation.2 | async-start | bytes 131072 | tf_op jit(solution)/shard_map/all_to_all | solution.py:367
  174.3 12.7 %copy-start.1 = (bf16[16,192,128]{2,1,0:T(8,128)(2,1)}, bf16[16,192,128]{2,1,0:T(8,128)(2,1)S(1)}, u32[]{:S(2)}) copy-start(bf16[16,192,128]{2,1,0:T(8,128)(2,1)S(1)} %collective-permute-done.4.refs_2_) | copy-start | bytes 2359300
  174.3 11.7 %collective-permute-start.6 = (bf16[8,192,128]{2,1,0:T(8,128)(2,1)S(1)}, bf16[8,192,128]{2,1,0:T(8,128)(2,1)S(1)}, u32[]{:S(2)}, u32[]{:S(2)}) collective-permute-start(bf16[8,192,128]{2,1,0:T(8,128)(2,1)S(1)} %slice.18), channel_id=1, source_target_pairs={{0,32},{32,64},{64,96},{96,0},{1,33},{33,65},{65,97},{97,1},{2,34}... | collective-permute-start | bytes 1179656 | tf_op jit(solution)/shard_map/ppermute | solution.py:328
  176.8 10.2 %collective-permute-start.7 = (bf16[8,192,128]{2,1,0:T(8,128)(2,1)S(1)}, bf16[8,192,128]{2,1,0:T(8,128)(2,1)S(1)}, u32[]{:S(2)}, u32[]{:S(2)}) collective-permute-start(bf16[8,192,128]{2,1,0:T(8,128)(2,1)S(1)} %slice.19), channel_id=1, source_target_pairs={{0,96},{32,0},{64,32},{96,64},{1,97},{33,1},{65,33},{97,65},{2,98}... | collective-permute-start | bytes 1179656 | tf_op jit(solution)/shard_map/ppermute | solution.py:329
  179.0 16.4 %copy-start.2 = (bf16[16,72,128]{2,1,0:T(8,128)(2,1)}, bf16[16,72,128]{2,1,0:T(8,128)(2,1)S(1)}, u32[]{:S(2)}) copy-start(bf16[16,72,128]{2,1,0:T(8,128)(2,1)S(1)} %collective-permute-done.refs_2_) | copy-start | bytes 884740
  179.0 16.4 %collective-permute-start.2 = (bf16[8,72,128]{2,1,0:T(8,128)(2,1)S(1)}, bf16[8,72,128]{2,1,0:T(8,128)(2,1)S(1)}, u32[]{:S(2)}, u32[]{:S(2)}) collective-permute-start(bf16[8,72,128]{2,1,0:T(8,128)(2,1)S(1)} %slice.16), channel_id=1, source_target_pairs={{0,32},{32,64},{64,96},{96,0},{1,33},{33,65},{65,97},{97,1},{2,34}... | collective-permute-start | bytes 442376 | tf_op jit(solution)/shard_map/ppermute | solution.py:328
  179.1 16.3 %copy-start.3 = (bf16[16,72,128]{2,1,0:T(8,128)(2,1)}, bf16[16,72,128]{2,1,0:T(8,128)(2,1)S(1)}, u32[]{:S(2)}) copy-start(bf16[16,72,128]{2,1,0:T(8,128)(2,1)S(1)} %collective-permute-done.1.refs_3_) | copy-start | bytes 884740
  179.1 16.3 %collective-permute-start.3 = (bf16[8,72,128]{2,1,0:T(8,128)(2,1)S(1)}, bf16[8,72,128]{2,1,0:T(8,128)(2,1)}, u32[]{:S(2)}, u32[]{:S(2)}) collective-permute-start(bf16[8,72,128]{2,1,0:T(8,128)(2,1)S(1)} %slice.17), channel_id=1, source_target_pairs={{0,96},{32,0},{64,32},{96,64},{1,97},{33,1},{65,33},{97,65},{2,98}... | collective-permute-start | bytes 442376 | tf_op jit(solution)/shard_map/ppermute | solution.py:329
  186.1 0.9 copy-start.4
  187.0 0.7 copy-start.5
  195.4 0.7 copy-start.6

commit v3 on v1

v3 whole, which is shorter than its diff:
```python
import functools
import math

import jax
import jax.numpy as jnp
import numpy as np
from jax import lax
from jax.experimental import pallas as pl
from jax.experimental.pallas import tpu as pltpu
from jax.sharding import PartitionSpec as P


LON = 1440
LAT = 720
DAYS = 16
FAM = 3
MODELS = 4
TIME = 128
LANES = 128
FULL = LAT // LANES
TAIL = LAT - FULL * LANES
HALF = TAIL // 2
PEERS = 32
BAND = LON // PEERS
BLOCK = 8 * BAND
CHUNKS = (11, 4)
STARTS = tuple(3 * sum(CHUNKS[:c]) for c in range(len(CHUNKS)))

SMEM = pl.BlockSpec(memory_space=pltpu.SMEM)
VMEM = pl.BlockSpec(memory_space=pltpu.VMEM)
ANY = pl.BlockSpec(memory_space=pl.ANY)
STEPS = 8
SPAN = TIME // STEPS

F32 = jnp.float32
BF16 = jnp.bfloat16


def rows_of(triples):
    return -(-17 * triples // 8) * 8


def packed_weight(triples):
    lat = np.arange(LAT, dtype=np.float64)
    weight = np.cos((-90.0 + (lat + 0.5) * 180.0 / LAT) * (math.pi / 180.0))
    count = 3 * triples
    rows = np.zeros((rows_of(triples), LANES))
    for j in range(FULL):
        rows[j * count : (j + 1) * count] = weight[j * LANES : (j + 1) * LANES]
    tail = weight[FULL * LANES :]
    for half in range(2):
        part = rows[FULL * count + half * triples : FULL * count + (half + 1) * triples]
        part[:, :TAIL] = tail
        part[:, TAIL : TAIL + HALF] = tail[half * HALF : (half + 1) * HALF]
    return rows.astype(np.float32), float(weight.sum() * LON)


def pack_rows(first, triples, wide, rows, ready):
    count = 3 * triples
    lane = lax.broadcasted_iota(jnp.int32, (triples, LANES), 1)
    for r in range(8):
        s = BAND * r + first
        for j in range(FULL):
            rows[j * count : (j + 1) * count, :] = wide[j, s : s + count, :]
        third = wide[FULL, s + 2 * triples : s + 3 * triples, :]
        for half in range(2):
            own = wide[FULL, s + half * triples : s + (half + 1) * triples, :]
            moved = pltpu.roll(third, TAIL - half * HALF, 1)
            rows[FULL * count + half * triples : FULL * count + (half + 1) * triples, :] = jnp.where(
                lane < TAIL, own, jnp.where(lane < TAIL + HALF, moved, 0.0)
            )
        ready[r] = rows[...].astype(BF16)


def pack_kernel(steps, x, *refs):
    n = len(CHUNKS)
    outs, held, ready, wide = refs[:n], refs[n], refs[n + 1 : 2 * n + 1], refs[2 * n + 1]
    rows, got, put = refs[2 * n + 2 : 3 * n + 2], refs[3 * n + 2], refs[3 * n + 3]
    pieces = LON // BLOCK * steps

    def enter(i):
        q, t = i // steps, i % steps
        return pltpu.make_async_copy(x.at[t, pl.ds(pl.multiple_of(q * BLOCK, 8), BLOCK)], held.at[i], got.at[i])

    def leave(c, i):
        q, t = i // steps, i % steps
        return pltpu.make_async_copy(ready[c].at[i], outs[c].at[pl.ds(q * 8, 8), t], put.at[c, i])

    for i in range(pieces):
        enter(i).start()
    for c, triples in enumerate(CHUNKS):
        total = rows_of(triples)
        rows[c][total - 8 :, :] = jnp.zeros((8, LANES), F32)

    def piece(i, carry):
        enter(i).wait()
        for j in range(FULL):
            wide[j] = held[i, :, j * LANES : (j + 1) * LANES].astype(F32)
        wide[FULL, :, :TAIL] = held[i, :, FULL * LANES :].astype(F32)
        for c, triples in enumerate(CHUNKS):
            pack_rows(STARTS[c], triples, wide, rows[c], ready[c].at[i])
            leave(c, i).start()
        return carry

    lax.fori_loop(0, pieces, piece, 0)
    for c in range(n):
        for i in range(pieces):
            leave(c, i).wait()


def pack(x):
    steps = x.shape[0]
    totals = [rows_of(n) for n in CHUNKS]
    pieces = LON // BLOCK * steps
    return pl.pallas_call(
        functools.partial(pack_kernel, steps),
        in_specs=[ANY],
        out_specs=[ANY] * len(CHUNKS),
        out_shape=[jax.ShapeDtypeStruct((PEERS, steps, total, LANES), BF16) for total in totals],
        scratch_shapes=[pltpu.VMEM((pieces, BLOCK, LAT), BF16)]
        + [pltpu.VMEM((pieces, 8, total, LANES), BF16) for total in totals]
        + [pltpu.VMEM((FULL + 1, BLOCK, LANES), F32)]
        + [pltpu.VMEM((total, LANES), F32) for total in totals]
        + [pltpu.SemaphoreType.DMA((pieces,)), pltpu.SemaphoreType.DMA((len(CHUNKS), pieces))],
        cost_estimate=pl.CostEstimate(flops=10_000_000, bytes_accessed=17_000_000, transcendentals=0),
        name="pack",
    )(x)


def unpack(table, scale, out, triples):
    stride = rows_of(triples) + 1
    count = 3 * triples
    lane = lax.broadcasted_iota(jnp.int32, (DAYS, LANES), 1)

    def row(index):
        halves = [table[pl.ds(8 * h * stride + index, 8, stride=stride), :] for h in range(DAYS // 8)]
        value = jnp.concatenate(halves, axis=0)
        return value if scale is None else value * scale

    def whole(lon, carry):
        for j in range(FULL):
            out[lon, :, j * LANES : (j + 1) * LANES] = row(j * count + lon).astype(BF16)
        return carry

    def tail(lon, carry):
        out[lon, :, FULL * LANES :] = row(FULL * count + lon)[:, :TAIL].astype(BF16)
        return carry

    def last(k, carry):
        low = pltpu.roll(row(FULL * count + k), LANES - TAIL, 1)
        high = pltpu.roll(row(FULL * count + triples + k), LANES - TAIL + HALF, 1)
        joined = jnp.where(lane < HALF, low, high)
        out[2 * triples + k, :, FULL * LANES :] = joined[:, :TAIL].astype(BF16)
        return carry

    lax.fori_loop(0, count, whole, 0)
    lax.fori_loop(0, 2 * triples, tail, 0)
    lax.fori_loop(0, triples, last, 0)


def moment_kernel(first, triples, chained, *refs):
    bins, inverse, x, scale, weight, before = refs[:6]
    refs = refs[6 + (3 if chained else 0) :]
    outs, refs = refs[:3], refs[3:]
    packed, after, held, mean, second, third, norm, wide, got, put = refs
    total = rows_of(triples)
    stride = total + 1
    count = 3 * triples

    def enter(i):
        span = pl.ds(i * SPAN, SPAN)
        return pltpu.make_async_copy(x.at[span], held.at[span], got.at[i])

    def leave(i):
        return pltpu.make_async_copy(wide.at[i], outs[i].at[pl.ds(first, count)], put.at[i])

    for i in range(STEPS):
        enter(i).start()
    for ref in (mean, second, third):
        for d in range(DAYS):
            ref[d * stride : (d + 1) * stride, :] = jnp.zeros((stride, LANES), F32)

    def add(t, carry):
        at = bins[t] * stride
        for k in range(total // 8):
            rows = pl.ds(at + 8 * k, 8)
            mean[rows, :] = mean[rows, :] + held[t, 8 * k : 8 * k + 8].astype(F32)
        return carry

    def adds(i, carry):
        enter(i).wait()
        return lax.fori_loop(0, SPAN, lambda t, c: add(i * SPAN + t, c), carry, unroll=4)

    lax.fori_loop(0, STEPS, adds, 0)

    for d in range(DAYS):
        rows = slice(d * stride, d * stride + total)
        value = mean[rows, :] * inverse[d]
        mean[rows, :] = value
        packed[d] = value.astype(BF16)
    unpack(mean, None, wide.at[0], triples)
    leave(0).start()

    def moments(t, carry):
        at = bins[t] * stride
        sums = None
        for k in range(total // 8):
            rows = pl.ds(at + 8 * k, 8)
            tile = slice(8 * k, 8 * k + 8)
            a = held[t, tile].astype(F32) - mean[rows, :]
            q = a * a
            second[rows, :] = second[rows, :] + q
            third[rows, :] = third[rows, :] + q * a
            w = q * weight[tile, :]
            sums = w if sums is None else sums + w
        norm[t] = sums
        return carry

    lax.fori_loop(0, TIME, moments, 0, unroll=2)

    by_time = jnp.sum(norm[...], axis=1)
    after[...] = before[...] + jnp.sum(by_time.T, axis=0, keepdims=True)
    unpack(second, scale[...], wide.at[1], triples)
    leave(1).start()
    unpack(third, scale[...], wide.at[2], triples)
    leave(2).start()
    for i in range(3):
        leave(i).wait()


def moments(bins, inverse, x, scale, weight, before, outs, first, triples):
    total = rows_of(triples)
    count = 3 * triples
    chained = outs is not None
    field = jax.ShapeDtypeStruct((BAND, DAYS, LAT), BF16)
    table = pltpu.VMEM((DAYS * (total + 1), LANES), F32)
    result = pl.pallas_call(
        functools.partial(moment_kernel, first, triples, chained),
        in_specs=[SMEM, SMEM, ANY, VMEM, VMEM, VMEM] + [ANY] * (3 if chained else 0),
        out_specs=[ANY] * 3 + [VMEM] * 2,
        out_shape=[
            field,
            field,
            field,
            jax.ShapeDtypeStruct((DAYS, total, LANES), BF16),
            jax.ShapeDtypeStruct((1, TIME), F32),
        ],
        input_output_aliases={6: 0, 7: 1, 8: 2} if chained else {},
        scratch_shapes=[
            pltpu.VMEM((TIME, total, LANES), BF16),
            table,
            table,
            table,
            pltpu.VMEM((TIME, 8, LANES), F32),
            pltpu.VMEM((3, count, DAYS, LAT), BF16),
            pltpu.SemaphoreType.DMA((STEPS,)),
            pltpu.SemaphoreType.DMA((3,)),
        ],
        cost_estimate=pl.CostEstimate(flops=40_000_000 * triples, bytes_accessed=1_000_000 * triples, transcendentals=0),
    )(bins, inverse, x, scale, weight, before, *(outs or ()))
    return result[:3], result[3], result[4]


def family_kernel(first, triples, chained, *refs):
    share, *means = refs[: MODELS + 1]
    out, table, wide, sem = refs[MODELS + 1 + (1 if chained else 0) :]
    total = rows_of(triples)
    stride = total + 1
    count = 3 * triples
    for d in range(DAYS):
        values = [m[d].astype(F32) for m in means]
        for f in range(FAM):
            value = values[0] * share[f, 0]
            for k in range(1, MODELS):
                value = value + values[k] * share[f, k]
            table[f, d * stride : d * stride + total, :] = value
    copies = []
    for f in range(FAM):
        unpack(table.at[f], None, wide.at[f], triples)
        copies.append(pltpu.make_async_copy(wide.at[f], out.at[f, pl.ds(first, count)], sem.at[f]))
        copies[-1].start()
    for copy in copies:
        copy.wait()


def families(share, means, out, first, triples):
    total = rows_of(triples)
    count = 3 * triples
    chained = out is not None
    return pl.pallas_call(
        functools.partial(family_kernel, first, triples, chained),
        in_specs=[SMEM] + [VMEM] * MODELS + [ANY] * (1 if chained else 0),
        out_specs=ANY,
        out_shape=jax.ShapeDtypeStruct((FAM, BAND, DAYS, LAT), BF16),
        input_output_aliases={MODELS + 1: 0} if chained else {},
        scratch_shapes=[
            pltpu.VMEM((FAM, DAYS * (total + 1), LANES), F32),
            pltpu.VMEM((FAM, count, DAYS, LAT), BF16),
            pltpu.SemaphoreType.DMA((FAM,)),
        ],
        cost_estimate=pl.CostEstimate(flops=10_000_000 * triples, bytes_accessed=500_000 * triples, transcendentals=0),
    )(share, *means, *(() if out is None else (out,)))


def from_others(mean):
    return [lax.ppermute(mean, "group", [(i, (i + k) % MODELS) for i in range(MODELS)]) for k in range(1, MODELS)]


def exchange(array):
    return lax.all_to_all(array, "tm", split_axis=0, concat_axis=0, tiled=True)


def local(precip, day_bins, family_of):
    sent = pack(precip[0])
    got0, later, day_bins, family_of = lax.optimization_barrier((exchange(sent[0]), sent[1], day_bins, family_of))
    got1 = exchange(later)

    days = jnp.arange(DAYS, dtype=jnp.int32)
    counts = jnp.sum((day_bins[None, :] == days[:, None]).astype(F32), axis=1)
    inverse = 1.0 / jnp.maximum(counts, 1.0)
    scale = jnp.broadcast_to(inverse[:, None], (DAYS, LANES))

    group = lax.axis_index("group")
    turned = (group + MODELS - jnp.arange(MODELS, dtype=jnp.int32)) % MODELS
    models = jnp.arange(MODELS, dtype=jnp.int32)
    hot = (family_of[None, :] == jnp.arange(FAM, dtype=jnp.int32)[:, None]).astype(F32)
    members = jnp.maximum(jnp.sum(hot, axis=1), 1.0)
    at = (turned[:, None] == models[None, :]).astype(F32)
    share = jnp.sum(hot[:, None, :] * at[None], axis=2) / members[:, None]

    def chunk(c, got, norm, outs):
        weight, _ = packed_weight(CHUNKS[c])
        x = got.reshape(TIME, rows_of(CHUNKS[c]), LANES)
        return moments(day_bins, inverse, x, scale, jnp.asarray(weight), norm, outs, STARTS[c], CHUNKS[c])

    outs, mean0, norm = chunk(0, got0, jnp.zeros((1, TIME), F32), None)
    means0 = [mean0, *from_others(mean0)]
    got1, outs = lax.optimization_barrier((got1, outs))
    outs, mean1, norm = chunk(1, got1, norm, outs)
    means1 = [mean1, *from_others(mean1)]

    everyone = MODELS * PEERS
    parts = lax.all_to_all(
        jnp.broadcast_to(norm, (everyone, 1, TIME)), ("group", "tm"), split_axis=0, concat_axis=0, tiled=True
    )
    fam = families(share, means0, None, STARTS[0], CHUNKS[0])
    fam = families(share, means1, fam, STARTS[1], CHUNKS[1])

    _, total_weight = packed_weight(CHUNKS[0])
    anomaly_norm = jnp.sqrt(jnp.sum(parts.reshape(MODELS, PEERS, TIME), axis=1) / total_weight)
    fields = [o[None].transpose(0, 2, 1, 3) for o in outs]
    return (*fields, fam.transpose(0, 2, 1, 3), anomaly_norm)


def solution(mesh):
    in_specs = (P("group", "tm", None, None), P(), P())
    out_specs = (
        P("group", None, "tm", None),
        P("group", None, "tm", None),
        P("group", None, "tm", None),
        P(None, None, "tm", None),
        P(),
    )
    return jax.shard_map(local, mesh=mesh, in_specs=in_specs, out_specs=out_specs, check_vma=False)
```

time: 277 us -> 179 us (0.65)
  waiting for transfers between devices: 68.8 us -> 28.9 us
  Pallas kernels: 77.1 us -> 40.4 us
  starting transfers between devices: 33.2 us -> 19.2 us
  blocking collectives: 87 us -> 82.6 us
    psum x1 -> x0, blocking collectives: 87 us -> none  [local(): anomaly_norm = jnp.sqrt(lax.psum(mine, ('group', 'tm')) / total_weight)]
    all_to_all x0 -> x1, blocking collectives: none -> 82.6 us  [exchange(): return lax.all_to_all(array, 'tm', split_axis=0, concat_axis=0, tiled=True)]
    all_to_all x3 -> x2, waiting for transfers between devices: 68.8 us -> 10.2 us  [the longest x1 10.2 us: exchange(): return lax.all_to_all(array, 'tm', split_axis=0, concat_axis=0, tiled=True)]
    pallas_call x3 -> x1, Pallas kernels: 34.6 us -> 7.15 us  [pack(): pl.pallas_call(functools.partial(pack_kernel, steps), in_specs=[ANY], out...]
    ppermute x9 -> x6, waiting for transfers between devices: 0.02 us -> 18.7 us  [from_others(): lax.ppermute(mean, 'group', [(i, (i + k) % MODELS) for i in range(MODELS)])]
    all_to_all x3 -> x2, starting transfers between devices: 22 us -> 9.92 us  [the longest x1 5.86 us: local(): lax.all_to_all(jnp.broadcast_to(norm, (everyone, 1, TIME)), ('group', 'tm...]
    pallas_call x3 -> x2, Pallas kernels: 28 us -> 21.8 us  [moments(): pl.pallas_call(functools.partial(moment_kernel, first, triples, chained),...]
    pallas_call x3 -> x2, Pallas kernels: 14.5 us -> 11.4 us  [families(): pl.pallas_call(functools.partial(family_kernel, first, triples, chained),...]
  transfers between devices with their start and end apart: 12 -> 8, of which waited for: 2 -> 4; matrix products, arithmetic and copies ran while one was open for 1% -> 2% of each run, Pallas kernels for 23% -> 16%
where the time goes in v3:
time: 179 us
  blocking collectives  82.6 us (46%)
  Pallas kernels  40.4 us (23%)
  waiting for transfers between devices  28.9 us (16%)
  starting transfers between devices  19.2 us (11%)
  local copies, waits for them, and re-layouts  5.34 us (3%)
    all_to_all x1, blocking collectives, exchange(): return lax.all_to_all(array, 'tm', split_axis=0, concat_axis=0, tiled=True)  82.6 us
    pallas_call x2, Pallas kernels, moments(): pl.pallas_call(functools.partial(moment_kernel, first, triples, chained),...  21.8 us
    ppermute x6, waiting for transfers between devices, from_others(): lax.ppermute(mean, 'group', [(i, (i + k) % MODELS) for i in range(MODELS)])  18.7 us
    pallas_call x2, Pallas kernels, families(): pl.pallas_call(functools.partial(family_kernel, first, triples, chained),...  11.4 us
    all_to_all x1, waiting for transfers between devices, exchange(): return lax.all_to_all(array, 'tm', split_axis=0, concat_axis=0, tiled=True)  10.2 us
    ppermute x6, starting transfers between devices, from_others(): lax.ppermute(mean, 'group', [(i, (i + k) % MODELS) for i in range(MODELS)])  9.24 us
    pallas_call x1, Pallas kernels, pack(): pl.pallas_call(functools.partial(pack_kernel, steps), in_specs=[ANY], out...  7.15 us
    all_to_all x1, starting transfers between devices, local(): lax.all_to_all(jnp.broadcast_to(norm, (everyone, 1, TIME)), ('group', 'tm...  5.86 us
  transfers between devices with their start and end apart: 8, of which 4 were waited for; matrix products, arithmetic and copies ran while one was open for 2% of the time, Pallas kernels for 16%

profile of v3, /device:TPU:1, one launch (start us, length us, event | category | flops | bytes accessed | tf_op | source)
XLA Modules:
  0.0 178.9 jit_solution(11781131960934066350)
XLA Ops:
  0.6 7.1 %pack.1 = (bf16[32,4,192,128]{3,2,1,0:T(8,128)(2,1)}, bf16[32,4,72,128]{3,2,1,0:T(8,128)(2,1)}) custom-call(bf16[4,1440,720]{2,1,0:T(8,128)(2,1)} %bitcast.20), custom_call_target="tpu_custom_call" | custom-call | flops 10000000 | bytes 17000000 | tf_op jit(solution)/shard_map/pack/pallas_call | solution.py:115
  7.8 82.6 %all_to_all.15 = bf16[32,4,192,128]{3,2,1,0:T(8,128)(2,1)} all-to-all(bf16[32,4,192,128]{3,2,1,0:T(8,128)(2,1)} %get-tuple-element.25), channel_id=1, replica_groups=mesh['group'=4,'tm'=32] {'tm'}, dimensions={0} | all-to-all | bytes 12582912 | tf_op jit(solution)/shard_map/all_to_all | solution.py:310
  90.4 4.1 %all-to-all-start.1 = ((bf16[32,4,72,128]{3,2,1,0:T(8,128)(2,1)}), bf16[32,4,72,128]{3,2,1,0:T(8,128)(2,1)S(1)}, u32[]{:S(2)}, u32[]{:S(2)}) async-start(bf16[32,4,72,128]{3,2,1,0:T(8,128)(2,1)} %get-tuple-element.28), calls=%async_computation.1 | async-start | bytes 4718592 | tf_op jit(solution)/shard_map/all_to_all | solution.py:310
  94.5 0.1 fusion.1
  94.6 0.0 copy-done.7
  94.6 0.1 convert_reduce_fusion
  94.7 0.0 copy-start.6
  94.7 0.7 broadcast_in_dim.12.refs_3_
  95.4 0.6 broadcast_in_dim.13.refs_5_
  96.0 0.0 copy-done.6
  96.0 0.0 copy-start.8
  96.0 14.2 %shard_map.92 = (bf16[45,16,720]{2,1,0:T(8,128)(2,1)}, bf16[45,16,720]{2,1,0:T(8,128)(2,1)}, bf16[45,16,720]{2,1,0:T(8,128)(2,1)}, bf16[16,192,128]{2,1,0:T(8,128)(2,1)}, f32[1,128]{1,0:T(1,128)}) custom-call(s32[128]{0:T(128)} %refs_0_.1, f32[16]{0:T(128)} %copy-done.6, bf16[128,192,128]{2,1,0:T(8,128)(2,1)} %bitcast.17, ...), custom_call_target="tpu_custom_call" | custom-call | flops 440000000 | bytes 11000000 | tf_op jit(solution)/shard_map/pallas_call | solution.py:237
  110.2 1.4 collective-permute-start.3
  111.6 2.6 %collective-permute-start.4 = (bf16[16,192,128]{2,1,0:T(8,128)(2,1)}, bf16[16,192,128]{2,1,0:T(8,128)(2,1)}, u32[]{:S(2)}, u32[]{:S(2)}) collective-permute-start(bf16[16,192,128]{2,1,0:T(8,128)(2,1)} %get-tuple-element.43.refs_1_), channel_id=1, source_target_pairs={{0,64},{32,96},{64,0},{96,32},{1,65},{33,97},{65,1},{97,33},{2,66}... | collective-permute-start | bytes 2359304 | tf_op jit(solution)/shard_map/ppermute | solution.py:306
  114.2 1.1 collective-permute-start.5
  115.3 0.0 copy-done.8
  115.3 0.1 fusion.3
  115.4 0.1 multiply_reduce_fusion
  115.5 10.2 %all-to-all-done.1 = bf16[32,4,72,128]{3,2,1,0:T(8,128)(2,1)S(1)} async-done(((bf16[32,4,72,128]{3,2,1,0:T(8,128)(2,1)}), bf16[32,4,72,128]{3,2,1,0:T(8,128)(2,1)S(1)}, u32[]{:S(2)}, u32[]{:S(2)}) %all-to-all-start.1) | async-done | bytes 2359328 | tf_op jit(solution)/shard_map/all_to_all | solution.py:310
  125.6 0.0 copy-start
  125.6 1.4 copy-done
  127.1 7.6 %shard_map.93 = (bf16[45,16,720]{2,1,0:T(8,128)(2,1)}, bf16[45,16,720]{2,1,0:T(8,128)(2,1)}, bf16[45,16,720]{2,1,0:T(8,128)(2,1)}, bf16[16,72,128]{2,1,0:T(8,128)(2,1)}, f32[1,128]{1,0:T(1,128)}) custom-call(s32[128]{0:T(128)} %refs_0_.1, f32[16]{0:T(128)} %copy-done.6, ...), custom_call_target="tpu_custom_call", output_to_operand_aliasing={{0}: (6, {}), {1}: (7, {}), {2}: (8, {})} | custom-call | flops 160000000 | bytes 4000000 | tf_op jit(solution)/shard_map/pallas_call | solution.py:237
  134.6 1.2 broadcast_in_dim.17
  135.9 5.9 %all-to-all-start.2 = ((f32[128,1,128]{2,1,0:T(1,128)}), f32[128,1,128]{2,1,0:T(1,128)S(1)}, u32[]{:S(2)}, u32[]{:S(2)}) async-start(f32[128,1,128]{2,1,0:T(1,128)} %broadcast_in_dim.17), calls=%async_computation.2 | async-start | bytes 131072 | tf_op jit(solution)/shard_map/all_to_all | solution.py:343
  141.7 0.7 broadcast_divide_fusion.refs_0_
  142.4 0.0 copy-start.2
  142.4 0.0 collective-permute-done.3.refs_2_
  142.4 0.0 copy-start.1
  142.4 6.8 %collective-permute-done.4.refs_3_ = bf16[16,192,128]{2,1,0:T(8,128)(2,1)} collective-permute-done((bf16[16,192,128]{2,1,0:T(8,128)(2,1)}, bf16[16,192,128]{2,1,0:T(8,128)(2,1)}, u32[]{:S(2)}, u32[]{:S(2)}) %collective-permute-start.4) | collective-permute-done | bytes 786464 | tf_op jit(solution)/shard_map/ppermute | solution.py:306
  149.3 0.0 collective-permute-done.5.refs_4_
  149.3 0.0 copy-done.1
  149.3 7.7 %shard_map.94.refs_5_ = bf16[3,45,16,720]{3,2,1,0:T(8,128)(2,1)} custom-call(f32[3,4]{1,0:T(4,128)} %broadcast_divide_fusion.refs_0_, bf16[16,192,128]{2,1,0:T(8,128)(2,1)} %get-tuple-element.43.refs_1_, bf16[16,192,128]{2,1,0:T(8,128)(2,1)} %copy-done.1, bf16[16,192,128]{2,1,0:T(8,128)(2,1)} %collective-permute-done.4.refs_3_, ...), custom_call_target="tpu_custom_call" | custom-call | flops 110000000 | bytes 5500000 | tf_op jit(solution)/shard_map/pallas_call | solution.py:290
  157.0 0.0 copy-done.2
  157.0 0.9 collective-permute-start
  157.9 2.9 %collective-permute-start.1 = (bf16[16,72,128]{2,1,0:T(8,128)(2,1)S(1)}, bf16[16,72,128]{2,1,0:T(8,128)(2,1)S(1)}, u32[]{:S(2)}, u32[]{:S(2)}) collective-permute-start(bf16[16,72,128]{2,1,0:T(8,128)(2,1)S(1)} %copy-done.2), channel_id=1, source_target_pairs={{0,64},{32,96},{64,0},{96,32},{1,65},{33,97},{65,1},{97,33},{2,66}... | collective-permute-start | bytes 884744 | tf_op jit(solution)/shard_map/ppermute | solution.py:306
  160.8 0.4 collective-permute-start.2
  161.1 0.0 all-to-all-done.2
  161.2 0.6 multiply_sqrt_fusion
  161.8 3.8 %collective-permute-done.refs_2_ = bf16[16,72,128]{2,1,0:T(8,128)(2,1)S(1)} collective-permute-done((bf16[16,72,128]{2,1,0:T(8,128)(2,1)S(1)}, bf16[16,72,128]{2,1,0:T(8,128)(2,1)S(1)}, u32[]{:S(2)}, u32[]{:S(2)}) %collective-permute-start) | collective-permute-done | bytes 294944 | tf_op jit(solution)/shard_map/ppermute | solution.py:306
  165.6 0.0 copy-start.3
  165.6 8.1 %collective-permute-done.1.refs_3_ = bf16[16,72,128]{2,1,0:T(8,128)(2,1)S(1)} collective-permute-done((bf16[16,72,128]{2,1,0:T(8,128)(2,1)S(1)}, bf16[16,72,128]{2,1,0:T(8,128)(2,1)S(1)}, u32[]{:S(2)}, u32[]{:S(2)}) %collective-permute-start.1) | collective-permute-done | bytes 294944 | tf_op jit(solution)/shard_map/ppermute | solution.py:306
  173.6 0.0 copy-start.4
  173.6 0.0 collective-permute-done.2.refs_4_
  173.6 0.0 copy-done.3
  173.6 0.7 copy-done.4
  174.4 0.0 copy-start.5
  174.4 0.7 copy-done.5
  175.1 3.8 %shard_map.95 = bf16[3,45,16,720]{3,2,1,0:T(8,128)(2,1)} custom-call(f32[3,4]{1,0:T(4,128)} %broadcast_divide_fusion.refs_0_, bf16[16,72,128]{2,1,0:T(8,128)(2,1)} %get-tuple-element.42.refs_1_, bf16[16,72,128]{2,1,0:T(8,128)(2,1)} %copy-done.3, bf16[16,72,128]{2,1,0:T(8,128)(2,1)} %copy-done.4, ...), custom_call_target="tpu_custom_call", output_to_operand_aliasing={{}: (5, {})} | custom-call | flops 40000000 | bytes 2000000 | tf_op jit(solution)/shard_map/pallas_call | solution.py:290
  (6 shorter events, 0.0 us)
Async XLA Ops:
  90.4 4.2 %copy-start.7 = (s32[128]{0:T(128)S(1)}, s32[128]{0:T(128)}, u32[]{:S(2)}) copy-start(s32[128]{0:T(128)} %refs_0_.1) | copy-start | bytes 1540
  90.4 35.2 %all-to-all-start.1 = ((bf16[32,4,72,128]{3,2,1,0:T(8,128)(2,1)}), bf16[32,4,72,128]{3,2,1,0:T(8,128)(2,1)S(1)}, u32[]{:S(2)}, u32[]{:S(2)}) async-start(bf16[32,4,72,128]{3,2,1,0:T(8,128)(2,1)} %get-tuple-element.28), calls=%async_computation.1 | async-start | bytes 4718592 | tf_op jit(solution)/shard_map/all_to_all | solution.py:310
  94.7 1.3 copy-start.6
  96.0 19.3 %copy-start.8 = (s32[4]{0:T(128)S(1)}, s32[4]{0:T(128)}, u32[]{:S(2)}) copy-start(s32[4]{0:T(128)} %param.7) | copy-start | bytes 52
  110.2 32.2 %collective-permute-start.3 = (bf16[16,192,128]{2,1,0:T(8,128)(2,1)}, bf16[16,192,128]{2,1,0:T(8,128)(2,1)S(1)}, u32[]{:S(2)}, u32[]{:S(2)}) collective-permute-start(bf16[16,192,128]{2,1,0:T(8,128)(2,1)} %get-tuple-element.43.refs_1_), channel_id=1, source_target_pairs={{0,32},{32,64},{64,96},{96,0},{1,33},{33,65},{65,97},{97,1},{2,34}... | collective-permute-start | bytes 2359304 | tf_op jit(solution)/shard_map/ppermute | solution.py:306
  111.6 37.7 %collective-permute-start.4 = (bf16[16,192,128]{2,1,0:T(8,128)(2,1)}, bf16[16,192,128]{2,1,0:T(8,128)(2,1)}, u32[]{:S(2)}, u32[]{:S(2)}) collective-permute-start(bf16[16,192,128]{2,1,0:T(8,128)(2,1)} %get-tuple-element.43.refs_1_), channel_id=1, source_target_pairs={{0,64},{32,96},{64,0},{96,32},{1,65},{33,97},{65,1},{97,33},{2,66}... | collective-permute-start | bytes 2359304 | tf_op jit(solution)/shard_map/ppermute | solution.py:306
  114.2 35.1 %collective-permute-start.5 = (bf16[16,192,128]{2,1,0:T(8,128)(2,1)}, bf16[16,192,128]{2,1,0:T(8,128)(2,1)}, u32[]{:S(2)}, u32[]{:S(2)}) collective-permute-start(bf16[16,192,128]{2,1,0:T(8,128)(2,1)} %get-tuple-element.43.refs_1_), channel_id=1, source_target_pairs={{0,96},{32,0},{64,32},{96,64},{1,97},{33,1},{65,33},{97,65},{2,98}... | collective-permute-start | bytes 2359304 | tf_op jit(solution)/shard_map/ppermute | solution.py:306
  125.6 1.4 copy-start
  135.9 25.3 %all-to-all-start.2 = ((f32[128,1,128]{2,1,0:T(1,128)}), f32[128,1,128]{2,1,0:T(1,128)S(1)}, u32[]{:S(2)}, u32[]{:S(2)}) async-start(f32[128,1,128]{2,1,0:T(1,128)} %broadcast_in_dim.17), calls=%async_computation.2 | async-start | bytes 131072 | tf_op jit(solution)/shard_map/all_to_all | solution.py:343
  142.4 14.5 %copy-start.2 = (bf16[16,72,128]{2,1,0:T(8,128)(2,1)S(1)}, bf16[16,72,128]{2,1,0:T(8,128)(2,1)}, u32[]{:S(2)}) copy-start(bf16[16,72,128]{2,1,0:T(8,128)(2,1)} %get-tuple-element.42.refs_1_) | copy-start | bytes 884740
  142.4 6.9 %copy-start.1 = (bf16[16,192,128]{2,1,0:T(8,128)(2,1)}, bf16[16,192,128]{2,1,0:T(8,128)(2,1)S(1)}, u32[]{:S(2)}) copy-start(bf16[16,192,128]{2,1,0:T(8,128)(2,1)S(1)} %collective-permute-done.3.refs_2_) | copy-start | bytes 2359300
  157.0 8.6 %collective-permute-start = (bf16[16,72,128]{2,1,0:T(8,128)(2,1)S(1)}, bf16[16,72,128]{2,1,0:T(8,128)(2,1)S(1)}, u32[]{:S(2)}, u32[]{:S(2)}) collective-permute-start(bf16[16,72,128]{2,1,0:T(8,128)(2,1)S(1)} %copy-done.2), channel_id=1, source_target_pairs={{0,32},{32,64},{64,96},{96,0},{1,33},{33,65},{65,97},{97,1},{2,34}... | collective-permute-start | bytes 884744 | tf_op jit(solution)/shard_map/ppermute | solution.py:306
  157.9 15.7 %collective-permute-start.1 = (bf16[16,72,128]{2,1,0:T(8,128)(2,1)S(1)}, bf16[16,72,128]{2,1,0:T(8,128)(2,1)S(1)}, u32[]{:S(2)}, u32[]{:S(2)}) collective-permute-start(bf16[16,72,128]{2,1,0:T(8,128)(2,1)S(1)} %copy-done.2), channel_id=1, source_target_pairs={{0,64},{32,96},{64,0},{96,32},{1,65},{33,97},{65,1},{97,33},{2,66}... | collective-permute-start | bytes 884744 | tf_op jit(solution)/shard_map/ppermute | solution.py:306
  160.8 12.9 %collective-permute-start.2 = (bf16[16,72,128]{2,1,0:T(8,128)(2,1)S(1)}, bf16[16,72,128]{2,1,0:T(8,128)(2,1)S(1)}, u32[]{:S(2)}, u32[]{:S(2)}) collective-permute-start(bf16[16,72,128]{2,1,0:T(8,128)(2,1)S(1)} %copy-done.2), channel_id=1, source_target_pairs={{0,96},{32,0},{64,32},{96,64},{1,97},{33,1},{65,33},{97,65},{2,98}... | collective-permute-start | bytes 884744 | tf_op jit(solution)/shard_map/ppermute | solution.py:306
  165.6 8.1 %copy-start.3 = (bf16[16,72,128]{2,1,0:T(8,128)(2,1)}, bf16[16,72,128]{2,1,0:T(8,128)(2,1)S(1)}, u32[]{:S(2)}) copy-start(bf16[16,72,128]{2,1,0:T(8,128)(2,1)S(1)} %collective-permute-done.refs_2_) | copy-start | bytes 884740
  173.6 0.7 copy-start.4
  174.4 0.7 copy-start.5

commit v4 on v3

--- a/solution.py
+++ b/solution.py
@@ -30,6 +30,7 @@
 VMEM = pl.BlockSpec(memory_space=pltpu.VMEM)
 ANY = pl.BlockSpec(memory_space=pl.ANY)
 STEPS = 8
+SPARE = 94_000
 SPAN = TIME // STEPS
 
 F32 = jnp.float32
@@ -153,32 +154,18 @@
         out[2 * triples + k, :, FULL * LANES :] = joined[:, :TAIL].astype(BF16)
         return carry
 
-    lax.fori_loop(0, count, whole, 0)
-    lax.fori_loop(0, 2 * triples, tail, 0)
+    lax.fori_loop(0, count, whole, 0, unroll=3)
+    lax.fori_loop(0, 2 * triples, tail, 0, unroll=2)
     lax.fori_loop(0, triples, last, 0)
 
 
-def moment_kernel(first, triples, chained, *refs):
-    bins, inverse, x, scale, weight, before = refs[:6]
-    refs = refs[6 + (3 if chained else 0) :]
-    outs, refs = refs[:3], refs[3:]
-    packed, after, held, mean, second, third, norm, wide, got, put = refs
-    total = rows_of(triples)
+def zero(table, stride):
+    for d in range(DAYS):
+        table[d * stride : (d + 1) * stride, :] = jnp.zeros((stride, LANES), F32)
+
+
+def add_up(bins, x, held, got, mean, total):
     stride = total + 1
-    count = 3 * triples
-
-    def enter(i):
-        span = pl.ds(i * SPAN, SPAN)
-        return pltpu.make_async_copy(x.at[span], held.at[span], got.at[i])
-
-    def leave(i):
-        return pltpu.make_async_copy(wide.at[i], outs[i].at[pl.ds(first, count)], put.at[i])
-
-    for i in range(STEPS):
-        enter(i).start()
-    for ref in (mean, second, third):
-        for d in range(DAYS):
-            ref[d * stride : (d + 1) * stride, :] = jnp.zeros((stride, LANES), F32)
 
     def add(t, carry):
         at = bins[t] * stride
@@ -188,20 +175,31 @@
         return carry
 
     def adds(i, carry):
-        enter(i).wait()
+        enter(x, held, got, i).wait()
         return lax.fori_loop(0, SPAN, lambda t, c: add(i * SPAN + t, c), carry, unroll=4)
 
     lax.fori_loop(0, STEPS, adds, 0)
 
+
+def enter(x, held, got, i):
+    span = pl.ds(i * SPAN, SPAN)
+    return pltpu.make_async_copy(x.at[span], held.at[span], got.at[i])
+
+
+def divide(inverse, mean, packed, total):
+    stride = total + 1
     for d in range(DAYS):
         rows = slice(d * stride, d * stride + total)
         value = mean[rows, :] * inverse[d]
         mean[rows, :] = value
-        packed[d] = value.astype(BF16)
-    unpack(mean, None, wide.at[0], triples)
-    leave(0).start()
-
-    def moments(t, carry):
+        each = DAYS // len(packed)
+        packed[d // each][d % each] = value.astype(BF16)
+
+
+def powers(bins, held, mean, second, third, weight, norm, total, ready=None):
+    stride = total + 1
+
+    def one(t, carry):
         at = bins[t] * stride
         sums = None
         for k in range(total // 8):
@@ -216,59 +214,162 @@
         norm[t] = sums
         return carry
 
-    lax.fori_loop(0, TIME, moments, 0, unroll=2)
-
-    by_time = jnp.sum(norm[...], axis=1)
-    after[...] = before[...] + jnp.sum(by_time.T, axis=0, keepdims=True)
-    unpack(second, scale[...], wide.at[1], triples)
-    leave(1).start()
-    unpack(third, scale[...], wide.at[2], triples)
-    leave(2).start()
+    def some(i, carry):
+        if ready is not None:
+            ready(i)
+        return lax.fori_loop(0, SPAN, lambda t, c: one(i * SPAN + t, c), carry, unroll=2 if total > 100 else 4)
+
+    lax.fori_loop(0, STEPS, some, 0)
+
+
+def total_norm(norm):
+    return jnp.sum(jnp.sum(norm[...], axis=1).T, axis=0, keepdims=True)
+
+
+def leave(wide, outs, put, first, count, i):
+    return pltpu.make_async_copy(wide.at[i], outs[i].at[pl.ds(first, count)], put.at[i])
+
+
+def sum_kernel(total, bins, inverse, x, mean, low, high, held, got):
+    for i in range(STEPS):
+        enter(x, held, got, i).start()
+    zero(mean, total + 1)
+    add_up(bins, x, held, got, mean, total)
+    divide(inverse, mean, (low, high), total)
+
+
+def table_shape(total):
+    return (DAYS * (total + 1), LANES)
+
+
+def half_shape(total):
+    return jax.ShapeDtypeStruct((DAYS // 2, total, LANES), BF16)
+
+
+def sums(bins, inverse, x, triples):
+    total = rows_of(triples)
+    return pl.pallas_call(
+        functools.partial(sum_kernel, total),
+        in_specs=[SMEM, SMEM, ANY],
+        out_specs=[VMEM] * 3,
+        out_shape=[jax.ShapeDtypeStruct(table_shape(total), F32), half_shape(total), half_shape(total)],
+        scratch_shapes=[pltpu.VMEM((TIME, total, LANES), BF16), pltpu.SemaphoreType.DMA((STEPS,))],
+        cost_estimate=pl.CostEstimate(flops=10_000_000 * triples, bytes_accessed=700_000 * triples, transcendentals=0),
+        name="sums",
+    )(bins, inverse, x)
+
+
+def power_kernel(first, triples, bins, x, mean, scale, weight, *refs):
+    outs, (after, held, second, third, norm, wide, got, put, _) = refs[:3], refs[3:]
+    total = rows_of(triples)
+    count = 3 * triples
+    for i in range(STEPS):
+        enter(x, held, got, i).start()
+    zero(second, total + 1)
+    zero(third, total + 1)
+    unpack(mean, None, wide.at[0], triples)
+    leave(wide, outs, put, first, count, 0).start()
+    powers(
+        bins, held, mean, second, third, weight, norm, total, lambda i: enter(x, held, got, i).wait()
+    )
+    after[...] = total_norm(norm)
+    for i, table in ((1, second), (2, third)):
+        unpack(table, scale[...], wide.at[i], triples)
+        leave(wide, outs, put, first, count, i).start()
     for i in range(3):
-        leave(i).wait()
-
-
-def moments(bins, inverse, x, scale, weight, before, outs, first, triples):
-    total = rows_of(triples)
-    count = 3 * triples
-    chained = outs is not None
-    field = jax.ShapeDtypeStruct((BAND, DAYS, LAT), BF16)
-    table = pltpu.VMEM((DAYS * (total + 1), LANES), F32)
+        leave(wide, outs, put, first, count, i).wait()
+
+
+FIELD = jax.ShapeDtypeStruct((BAND, DAYS, LAT), BF16)
+
+
+def higher(bins, x, mean, scale, weight, first, triples):
+    total = rows_of(triples)
     result = pl.pallas_call(
-        functools.partial(moment_kernel, first, triples, chained),
-        in_specs=[SMEM, SMEM, ANY, VMEM, VMEM, VMEM] + [ANY] * (3 if chained else 0),
-        out_specs=[ANY] * 3 + [VMEM] * 2,
-        out_shape=[
-            field,
-            field,
-            field,
-            jax.ShapeDtypeStruct((DAYS, total, LANES), BF16),
-            jax.ShapeDtypeStruct((1, TIME), F32),
-        ],
-        input_output_aliases={6: 0, 7: 1, 8: 2} if chained else {},
+        functools.partial(power_kernel, first, triples),
+        in_specs=[SMEM, ANY] + [VMEM] * 3,
+        out_specs=[ANY] * 3 + [VMEM],
+        out_shape=[FIELD] * 3 + [jax.ShapeDtypeStruct((1, TIME), F32)],
         scratch_shapes=[
             pltpu.VMEM((TIME, total, LANES), BF16),
-            table,
-            table,
-            table,
+            pltpu.VMEM(table_shape(total), F32),
+            pltpu.VMEM(table_shape(total), F32),
             pltpu.VMEM((TIME, 8, LANES), F32),
-            pltpu.VMEM((3, count, DAYS, LAT), BF16),
+            pltpu.VMEM((3, 3 * triples, DAYS, LAT), BF16),
             pltpu.SemaphoreType.DMA((STEPS,)),
             pltpu.SemaphoreType.DMA((3,)),
+            pltpu.VMEM((SPARE, LANES), F32),
         ],
         cost_estimate=pl.CostEstimate(flops=40_000_000 * triples, bytes_accessed=1_000_000 * triples, transcendentals=0),
-    )(bins, inverse, x, scale, weight, before, *(outs or ()))
+        name="higher",
+    )(bins, x, mean, scale, weight)
+    return result[:3], result[3]
+
+
+def both_kernel(total, bins, inverse, x, weight, before, mean, second, third, packed, after, held, norm, got):
+    for i in range(STEPS):
+        enter(x, held, got, i).start()
+    for table in (mean, second, third):
+        zero(table, total + 1)
+    add_up(bins, x, held, got, mean, total)
+    divide(inverse, mean, (packed,), total)
+    powers(bins, held, mean, second, third, weight, norm, total)
+    row = before[...] + total_norm(norm)
+    after[:, 0, :] = jnp.broadcast_to(row, (MODELS * PEERS, TIME))
+
+
+def both(bins, inverse, x, weight, before, triples):
+    total = rows_of(triples)
+    table = jax.ShapeDtypeStruct(table_shape(total), F32)
+    result = pl.pallas_call(
+        functools.partial(both_kernel, total),
+        in_specs=[SMEM, SMEM, ANY, VMEM, VMEM],
+        out_specs=[VMEM] * 5,
+        out_shape=[table] * 3
+        + [jax.ShapeDtypeStruct((DAYS, total, LANES), BF16)]
+        + [jax.ShapeDtypeStruct((MODELS * PEERS, 1, TIME), F32)],
+        scratch_shapes=[
+            pltpu.VMEM((TIME, total, LANES), BF16),
+            pltpu.VMEM((TIME, 8, LANES), F32),
+            pltpu.SemaphoreType.DMA((STEPS,)),
+        ],
+        cost_estimate=pl.CostEstimate(flops=50_000_000 * triples, bytes_accessed=1_000_000 * triples, transcendentals=0),
+        name="both",
+    )(bins, inverse, x, weight, before)
     return result[:3], result[3], result[4]
 
 
-def family_kernel(first, triples, chained, *refs):
-    share, *means = refs[: MODELS + 1]
-    out, table, wide, sem = refs[MODELS + 1 + (1 if chained else 0) :]
+def unpack_kernel(first, triples, scale, *refs):
+    tables, outs, wide, put = refs[:3], refs[6:9], refs[9], refs[10]
+    for i in range(3):
+        unpack(tables[i], None if i == 0 else scale[...], wide.at[i], triples)
+        leave(wide, outs, put, first, 3 * triples, i).start()
+    for i in range(3):
+        leave(wide, outs, put, first, 3 * triples, i).wait()
+
+
+def unpacked(scale, tables, outs, first, triples):
+    return pl.pallas_call(
+        functools.partial(unpack_kernel, first, triples),
+        in_specs=[VMEM] * 4 + [ANY] * 3,
+        out_specs=[ANY] * 3,
+        out_shape=[FIELD] * 3,
+        input_output_aliases={4: 0, 5: 1, 6: 2},
+        scratch_shapes=[pltpu.VMEM((3, 3 * triples, DAYS, LAT), BF16), pltpu.SemaphoreType.DMA((3,))],
+        cost_estimate=pl.CostEstimate(flops=3_000_000 * triples, bytes_accessed=700_000 * triples, transcendentals=0),
+        name="unpacked",
+    )(scale, *tables, *outs)
+
+
+def family_kernel(first, triples, chained, pieces, share, *refs):
+    means, refs = refs[: pieces * MODELS], refs[pieces * MODELS + (1 if chained else 0) :]
+    each = DAYS // pieces
+    out, table, wide, sem = refs
     total = rows_of(triples)
     stride = total + 1
     count = 3 * triples
     for d in range(DAYS):
-        values = [m[d].astype(F32) for m in means]
+        values = [means[pieces * k + d // each][d % each].astype(F32) for k in range(MODELS)]
         for f in range(FAM):
             value = values[0] * share[f, 0]
             for k in range(1, MODELS):
@@ -285,25 +386,34 @@
 
 def families(share, means, out, first, triples):
     total = rows_of(triples)
-    count = 3 * triples
     chained = out is not None
     return pl.pallas_call(
-        functools.partial(family_kernel, first, triples, chained),
-        in_specs=[SMEM] + [VMEM] * MODELS + [ANY] * (1 if chained else 0),
+        functools.partial(family_kernel, first, triples, chained, len(means) // MODELS),
+        in_specs=[SMEM] + [VMEM] * len(means) + [ANY] * (1 if chained else 0),
         out_specs=ANY,
         out_shape=jax.ShapeDtypeStruct((FAM, BAND, DAYS, LAT), BF16),
-        input_output_aliases={MODELS + 1: 0} if chained else {},
+        input_output_aliases={1 + len(means): 0} if chained else {},
         scratch_shapes=[
-            pltpu.VMEM((FAM, DAYS * (total + 1), LANES), F32),
-            pltpu.VMEM((FAM, count, DAYS, LAT), BF16),
+            pltpu.VMEM((FAM, *table_shape(total)), F32),
+            pltpu.VMEM((FAM, 3 * triples, DAYS, LAT), BF16),
             pltpu.SemaphoreType.DMA((FAM,)),
         ],
         cost_estimate=pl.CostEstimate(flops=10_000_000 * triples, bytes_accessed=500_000 * triples, transcendentals=0),
     )(share, *means, *(() if out is None else (out,)))
 
 
-def from_others(mean):
-    return [lax.ppermute(mean, "group", [(i, (i + k) % MODELS) for i in range(MODELS)]) for k in range(1, MODELS)]
+def moved(array, by):
+    return lax.ppermute(array, "group", [(i, (i + by) % MODELS) for i in range(MODELS)])
+
+
+def forwarded(low, high):
+    behind_low = moved(low, 1)
+    ahead_high = moved(high, -1)
+    behind_high = moved(high, 1)
+    ahead_low = moved(low, -1)
+    across_low = moved(behind_low, 1)
+    across_high = moved(ahead_high, -1)
+    return [low, high, behind_low, behind_high, ahead_low, ahead_high, across_low, across_high]
 
 
 def exchange(array):
@@ -321,32 +431,28 @@
     scale = jnp.broadcast_to(inverse[:, None], (DAYS, LANES))
 
     group = lax.axis_index("group")
-    turned = (group + MODELS - jnp.arange(MODELS, dtype=jnp.int32)) % MODELS
+    turned = (group + jnp.array([0, MODELS - 1, 1, 2], dtype=jnp.int32)) % MODELS
     models = jnp.arange(MODELS, dtype=jnp.int32)
     hot = (family_of[None, :] == jnp.arange(FAM, dtype=jnp.int32)[:, None]).astype(F32)
     members = jnp.maximum(jnp.sum(hot, axis=1), 1.0)
     at = (turned[:, None] == models[None, :]).astype(F32)
     share = jnp.sum(hot[:, None, :] * at[None], axis=2) / members[:, None]
 
-    def chunk(c, got, norm, outs):
-        weight, _ = packed_weight(CHUNKS[c])
-        x = got.reshape(TIME, rows_of(CHUNKS[c]), LANES)
-        return moments(day_bins, inverse, x, scale, jnp.asarray(weight), norm, outs, STARTS[c], CHUNKS[c])
-
-    outs, mean0, norm = chunk(0, got0, jnp.zeros((1, TIME), F32), None)
-    means0 = [mean0, *from_others(mean0)]
-    got1, outs = lax.optimization_barrier((got1, outs))
-    outs, mean1, norm = chunk(1, got1, norm, outs)
-    means1 = [mean1, *from_others(mean1)]
-
-    everyone = MODELS * PEERS
-    parts = lax.all_to_all(
-        jnp.broadcast_to(norm, (everyone, 1, TIME)), ("group", "tm"), split_axis=0, concat_axis=0, tiled=True
-    )
+    weight0, total_weight = packed_weight(CHUNKS[0])
+    weight1, _ = packed_weight(CHUNKS[1])
+    x0 = got0.reshape(TIME, rows_of(CHUNKS[0]), LANES)
+    table0, low0, high0 = sums(day_bins, inverse, x0, CHUNKS[0])
+    means0 = forwarded(low0, high0)
+    outs, norm0 = higher(day_bins, x0, table0, scale, jnp.asarray(weight0), STARTS[0], CHUNKS[0])
+    got1, norm0 = lax.optimization_barrier((got1, norm0))
+    x1 = got1.reshape(TIME, rows_of(CHUNKS[1]), LANES)
+    tables1, mean1, norm = both(day_bins, inverse, x1, jnp.asarray(weight1), norm0, CHUNKS[1])
+    means1 = [mean1, *(moved(mean1, by) for by in (1, -1, 2))]
+    parts = lax.all_to_all(norm, ("group", "tm"), split_axis=0, concat_axis=0, tiled=True)
+    outs = unpacked(scale, tables1, outs, STARTS[1], CHUNKS[1])
     fam = families(share, means0, None, STARTS[0], CHUNKS[0])
     fam = families(share, means1, fam, STARTS[1], CHUNKS[1])
 
-    _, total_weight = packed_weight(CHUNKS[0])
     anomaly_norm = jnp.sqrt(jnp.sum(parts.reshape(MODELS, PEERS, TIME), axis=1) / total_weight)
     fields = [o[None].transpose(0, 2, 1, 3) for o in outs]
     return (*fields, fam.transpose(0, 2, 1, 3), anomaly_norm)

time: 179 us -> 181 us (1.011)
  waiting for transfers between devices: 28.9 us -> 22.6 us
  starting transfers between devices: 19.2 us -> 24.9 us
  Pallas kernels: 40.4 us -> 43.3 us
    all_to_all x1, waiting for transfers between devices: 10.2 us -> 0.01 us  [exchange(): return lax.all_to_all(array, 'tm', split_axis=0, concat_axis=0, tiled=True)]
    ppermute x6 -> x9, waiting for transfers between devices: 18.7 us -> 22.6 us  [moved(): lax.ppermute(array, 'group', [(i, (i + by) % MODELS) for i in range(MODEL...]
    ppermute x6 -> x9, starting transfers between devices: 9.24 us -> 12.8 us  [moved(): lax.ppermute(array, 'group', [(i, (i + by) % MODELS) for i in range(MODEL...]
    pallas_call x4 -> x6, Pallas kernels: 33.3 us -> 36.2 us  [the longest x1 11.3 us: higher(): pl.pallas_call(functools.partial(power_kernel, first, triples), in_specs=...]
    all_to_all x1, starting transfers between devices: 5.86 us -> 8.04 us  [local(): lax.all_to_all(norm, ('group', 'tm'), split_axis=0, concat_axis=0, tiled=...]
    broadcast_in_dim x2 -> x0, local copies, waits for them, and re-layouts: 1.82 us -> none  [the longest x1 1.24 us: local(): jnp.broadcast_to(norm, (everyone, 1, TIME))]
  transfers between devices with their start and end apart: 8 -> 11, of which waited for: 4 -> 5; matrix products, arithmetic and copies ran while one was open for 2% -> 2% of each run, Pallas kernels for 16% -> 18%
where the time goes in v4:
time: 181 us
  blocking collectives  82.6 us (46%)
  Pallas kernels  43.3 us (24%)
  starting transfers between devices  24.9 us (14%)
  waiting for transfers between devices  22.6 us (12%)
  local copies, waits for them, and re-layouts  3.68 us (2%)
  other arithmetic  2.68 us (1%)
    all_to_all x1, blocking collectives, exchange(): return lax.all_to_all(array, 'tm', split_axis=0, concat_axis=0, tiled=True)  82.6 us
    ppermute x9, waiting for transfers between devices, moved(): lax.ppermute(array, 'group', [(i, (i + by) % MODELS) for i in range(MODEL...  22.6 us
    ppermute x9, starting transfers between devices, moved(): lax.ppermute(array, 'group', [(i, (i + by) % MODELS) for i in range(MODEL...  12.8 us
    pallas_call x1, Pallas kernels, higher(): pl.pallas_call(functools.partial(power_kernel, first, triples), in_specs=...  11.3 us
    pallas_call x2, Pallas kernels, families(): pl.pallas_call(functools.partial(family_kernel, first, triples, chained,...  10.8 us
    all_to_all x1, starting transfers between devices, local(): lax.all_to_all(norm, ('group', 'tm'), split_axis=0, concat_axis=0, tiled=...  8.04 us
    pallas_call x1, Pallas kernels, pack(): pl.pallas_call(functools.partial(pack_kernel, steps), in_specs=[ANY], out...  7.12 us
    pallas_call x1, Pallas kernels, both(): pl.pallas_call(functools.partial(both_kernel, total), in_specs=[SMEM, SME...  5.51 us
  transfers between devices with their start and end apart: 11, of which 5 were waited for; matrix products, arithmetic and copies ran while one was open for 2% of the time, Pallas kernels for 18%

profile of v4, /device:TPU:1, one launch (start us, length us, event | category | flops | bytes accessed | tf_op | source)
XLA Modules:
  0.0 180.7 jit_solution(5269195085108910330)
XLA Ops:
  0.6 7.1 %pack.1 = (bf16[32,4,192,128]{3,2,1,0:T(8,128)(2,1)}, bf16[32,4,72,128]{3,2,1,0:T(8,128)(2,1)}) custom-call(bf16[4,1440,720]{2,1,0:T(8,128)(2,1)} %bitcast.20), custom_call_target="tpu_custom_call" | custom-call | flops 10000000 | bytes 17000000 | tf_op jit(solution)/shard_map/pack/pallas_call | solution.py:116
  7.8 82.6 %all_to_all.15 = bf16[32,4,192,128]{3,2,1,0:T(8,128)(2,1)} all-to-all(bf16[32,4,192,128]{3,2,1,0:T(8,128)(2,1)} %get-tuple-element.28), channel_id=1, replica_groups=mesh['group'=4,'tm'=32] {'tm'}, dimensions={0} | all-to-all | bytes 12582912 | tf_op jit(solution)/shard_map/all_to_all | solution.py:420
  90.4 4.1 %all-to-all-start.1 = ((bf16[32,4,72,128]{3,2,1,0:T(8,128)(2,1)}), bf16[32,4,72,128]{3,2,1,0:T(8,128)(2,1)S(1)}, u32[]{:S(2)}, u32[]{:S(2)}) async-start(bf16[32,4,72,128]{3,2,1,0:T(8,128)(2,1)} %get-tuple-element.31), calls=%async_computation.1 | async-start | bytes 4718592 | tf_op jit(solution)/shard_map/all_to_all | solution.py:420
  94.5 0.0 copy-done.12
  94.5 0.1 fusion.1
  94.6 0.0 copy-done.8
  94.6 0.1 convert_reduce_fusion
  94.7 0.5 maximum_divide_fusion.inverse
  95.2 5.3 %sums.1 = (f32[3088,128]{1,0:T(8,128)}, bf16[8,192,128]{2,1,0:T(8,128)(2,1)}, bf16[8,192,128]{2,1,0:T(8,128)(2,1)}) custom-call(s32[128]{0:T(128)} %bins.2, f32[16]{0:T(128)} %maximum_divide_fusion.inverse, bf16[128,192,128]{2,1,0:T(8,128)(2,1)} %bitcast.16), custom_call_target="tpu_custom_call" | custom-call | flops 110000000 | bytes 7700000 | tf_op jit(solution)/shard_map/sums/pallas_call | solution.py:251
  100.5 1.4 collective-permute-start.3
  101.9 1.5 collective-permute-start.5
  103.4 0.0 collective-permute-start.4
  103.4 2.7 %collective-permute-start.6 = (bf16[8,192,128]{2,1,0:T(8,128)(2,1)}, bf16[8,192,128]{2,1,0:T(8,128)(2,1)}, u32[]{:S(2)}, u32[]{:S(2)}) collective-permute-start(bf16[8,192,128]{2,1,0:T(8,128)(2,1)} %get-tuple-element.49.refs_1_), channel_id=1, source_target_pairs={{0,96},{32,0},{64,32},{96,64},{1,97},{33,1},{65,33},{97,65},{2,98}... | collective-permute-start | bytes 1179656 | tf_op jit(solution)/shard_map/ppermute | solution.py:406
  106.1 0.0 copy-done.10
  106.1 0.1 fusion.3
  106.2 0.5 broadcast_maximum_fusion
  106.7 5.8 %collective-permute-done.3.refs_2_ = bf16[8,192,128]{2,1,0:T(8,128)(2,1)S(1)} collective-permute-done((bf16[8,192,128]{2,1,0:T(8,128)(2,1)}, bf16[8,192,128]{2,1,0:T(8,128)(2,1)S(1)}, u32[]{:S(2)}, u32[]{:S(2)}) %collective-permute-start.3) | collective-permute-done | bytes 393248 | tf_op jit(solution)/shard_map/ppermute | solution.py:406
  112.6 0.0 collective-permute-start.7
  112.6 8.2 %collective-permute-done.6.refs_5_ = bf16[8,192,128]{2,1,0:T(8,128)(2,1)} collective-permute-done((bf16[8,192,128]{2,1,0:T(8,128)(2,1)}, bf16[8,192,128]{2,1,0:T(8,128)(2,1)}, u32[]{:S(2)}, u32[]{:S(2)}) %collective-permute-start.6) | collective-permute-done | bytes 393248 | tf_op jit(solution)/shard_map/ppermute | solution.py:406
  120.8 2.9 %collective-permute-start.8 = (bf16[8,192,128]{2,1,0:T(8,128)(2,1)}, bf16[8,192,128]{2,1,0:T(8,128)(2,1)}, u32[]{:S(2)}, u32[]{:S(2)}) collective-permute-start(bf16[8,192,128]{2,1,0:T(8,128)(2,1)} %collective-permute-done.6.refs_5_), channel_id=1, source_target_pairs={{0,96},{32,0},{64,32},{96,64},{1,97},{33,1},{65,33},{97,65},{2,98}... | collective-permute-start | bytes 1179656 | tf_op jit(solution)/shard_map/ppermute | solution.py:406
  123.7 0.0 copy-done.9
  123.7 0.7 broadcast_in_dim.8.scale
  124.3 11.3 %higher.1 = (bf16[45,16,720]{2,1,0:T(8,128)(2,1)}, bf16[45,16,720]{2,1,0:T(8,128)(2,1)}, bf16[45,16,720]{2,1,0:T(8,128)(2,1)}, f32[1,128]{1,0:T(1,128)}) custom-call(s32[128]{0:T(128)} %bins.2, bf16[128,192,128]{2,1,0:T(8,128)(2,1)} %bitcast.17, f32[3088,128]{1,0:T(8,128)} %get-tuple-element.33.mean, f32[16,128]{1,0:T(8,128)} %broadcast_in_dim.8.scale, ...), custom_call_target="tpu_custom_call" | custom-call | flops 440000000 | bytes 11000000 | tf_op jit(solution)/shard_map/higher/pallas_call | solution.py:288
  135.6 0.1 multiply_reduce_fusion
  135.7 0.0 all-to-all-done.1
  135.7 1.4 copy-done
  137.1 5.5 %both.1 = (f32[1168,128]{1,0:T(8,128)}, f32[1168,128]{1,0:T(8,128)}, f32[1168,128]{1,0:T(8,128)}, bf16[16,72,128]{2,1,0:T(8,128)(2,1)}, f32[128,1,128]{2,1,0:T(1,128)}) custom-call(s32[128]{0:T(128)} %bins.2, f32[16]{0:T(128)} %maximum_divide_fusion.inverse, bf16[128,72,128]{2,1,0:T(8,128)(2,1)} %bitcast.19, f32[72,128]{1,0:T(8,128)} %constant.37.clone.weight, ...), custom_call_target="tpu_custom_call" | custom-call | flops 200000000 | bytes 4000000 | tf_op jit(solution)/shard_map/both/pallas_call | solution.py:324
  142.6 8.0 %all-to-all-start.2 = ((f32[128,1,128]{2,1,0:T(1,128)}), f32[128,1,128]{2,1,0:T(1,128)S(1)}, u32[]{:S(2)}, u32[]{:S(2)}) async-start(f32[128,1,128]{2,1,0:T(1,128)} %get-tuple-element.50), calls=%async_computation.2 | async-start | bytes 131072 | tf_op jit(solution)/shard_map/all_to_all | solution.py:451
  150.7 0.6 broadcast_divide_fusion.share
  151.3 0.0 collective-permute-done.4.refs_3_
  151.3 0.0 collective-permute-done.5.refs_4_
  151.3 0.0 collective-permute-done.7.refs_6_
  151.3 0.0 collective-permute-done.8.refs_7_
  151.4 0.7 copy-done.3
  152.1 0.2 copy-done.2
  152.2 7.2 %shard_map.101.refs_4_ = bf16[3,45,16,720]{3,2,1,0:T(8,128)(2,1)} custom-call(f32[3,4]{1,0:T(4,128)} %broadcast_divide_fusion.share, bf16[8,192,128]{2,1,0:T(8,128)(2,1)} %get-tuple-element.48.refs_0_, bf16[8,192,128]{2,1,0:T(8,128)(2,1)} %get-tuple-element.49.refs_1_, bf16[8,192,128]{2,1,0:T(8,128)(2,1)} %copy-done.1, bf16[8,192,128]{2,1,0:T(8,128)(2,1)} %copy-done.3, ...), custom_call_target="tpu_custom_call" | custom-call | flops 110000000 | bytes 5500000 | tf_op jit(solution)/shard_map/pallas_call | solution.py:390
  159.4 1.4 collective-permute-start
  160.9 1.4 collective-permute-start.1
  162.2 1.6 collective-permute-start.2
  163.8 3.3 %unpacked.1 = (bf16[45,16,720]{2,1,0:T(8,128)(2,1)}, bf16[45,16,720]{2,1,0:T(8,128)(2,1)}, bf16[45,16,720]{2,1,0:T(8,128)(2,1)}) custom-call(f32[16,128]{1,0:T(8,128)} %broadcast_in_dim.8.scale, f32[1168,128]{1,0:T(8,128)} %get-tuple-element.37.refs_0_, ...), custom_call_target="tpu_custom_call", output_to_operand_aliasing={{0}: (4, {}), {1}: (5, {}), {2}: (6, {})} | custom-call | flops 12000000 | bytes 2800000 | tf_op jit(solution)/shard_map/unpacked/pallas_call | solution.py:352
  167.1 0.0 all-to-all-done.2
  167.2 0.6 multiply_sqrt_fusion
  167.8 0.4 collective-permute-done.refs_1_
  168.2 0.5 collective-permute-done.1.refs_2_
  168.7 7.6 %collective-permute-done.2.refs_3_ = bf16[16,72,128]{2,1,0:T(8,128)(2,1)S(1)} collective-permute-done((bf16[16,72,128]{2,1,0:T(8,128)(2,1)S(1)}, bf16[16,72,128]{2,1,0:T(8,128)(2,1)S(1)}, u32[]{:S(2)}, u32[]{:S(2)}) %collective-permute-start.2) | collective-permute-done | bytes 294944 | tf_op jit(solution)/shard_map/ppermute | solution.py:406
  176.3 0.0 copy-done.6
  176.3 0.7 copy-done.7
  177.0 3.6 %shard_map.102 = bf16[3,45,16,720]{3,2,1,0:T(8,128)(2,1)} custom-call(f32[3,4]{1,0:T(4,128)} %broadcast_divide_fusion.share, bf16[16,72,128]{2,1,0:T(8,128)(2,1)} %get-tuple-element.47.refs_0_, bf16[16,72,128]{2,1,0:T(8,128)(2,1)} %copy-done.5, bf16[16,72,128]{2,1,0:T(8,128)(2,1)} %copy-done.6, ...), custom_call_target="tpu_custom_call", output_to_operand_aliasing={{}: (5, {})} | custom-call | flops 40000000 | bytes 2000000 | tf_op jit(solution)/shard_map/pallas_call | solution.py:390
  (20 shorter events, 0.1 us)
Async XLA Ops:
  90.4 4.1 %copy-start.12 = (s32[4]{0:T(128)S(1)}, s32[4]{0:T(128)}, u32[]{:S(2)}) copy-start(s32[4]{0:T(128)} %constant.35.clone) | copy-start | bytes 52
  90.4 4.2 %copy-start.8 = (s32[128]{0:T(128)S(1)}, s32[128]{0:T(128)}, u32[]{:S(2)}) copy-start(s32[128]{0:T(128)} %bins.2) | copy-start | bytes 1540
  90.4 45.3 %all-to-all-start.1 = ((bf16[32,4,72,128]{3,2,1,0:T(8,128)(2,1)}), bf16[32,4,72,128]{3,2,1,0:T(8,128)(2,1)S(1)}, u32[]{:S(2)}, u32[]{:S(2)}) async-start(bf16[32,4,72,128]{3,2,1,0:T(8,128)(2,1)} %get-tuple-element.31), calls=%async_computation.1 | async-start | bytes 4718592 | tf_op jit(solution)/shard_map/all_to_all | solution.py:420
  95.2 10.9 %copy-start.10 = (s32[4]{0:T(128)S(1)}, s32[4]{0:T(128)}, u32[]{:S(2)}) copy-start(s32[4]{0:T(128)} %param.8) | copy-start | bytes 52
  95.2 28.5 %copy-start.9 = (f32[16]{0:T(128)S(1)}, f32[16]{0:T(128)}, u32[]{:S(2)}) copy-start(f32[16]{0:T(128)} %maximum_divide_fusion.inverse) | copy-start | bytes 196
  100.5 12.0 %collective-permute-start.3 = (bf16[8,192,128]{2,1,0:T(8,128)(2,1)}, bf16[8,192,128]{2,1,0:T(8,128)(2,1)S(1)}, u32[]{:S(2)}, u32[]{:S(2)}) collective-permute-start(bf16[8,192,128]{2,1,0:T(8,128)(2,1)} %get-tuple-element.48.refs_0_), channel_id=1, source_target_pairs={{0,32},{32,64},{64,96},{96,0},{1,33},{33,65},{65,97},{97,1},{2,34}... | collective-permute-start | bytes 1179656 | tf_op jit(solution)/shard_map/ppermute | solution.py:406
  101.9 49.4 %collective-permute-start.5 = (bf16[8,192,128]{2,1,0:T(8,128)(2,1)}, bf16[8,192,128]{2,1,0:T(8,128)(2,1)S(1)}, u32[]{:S(2)}, u32[]{:S(2)}) collective-permute-start(bf16[8,192,128]{2,1,0:T(8,128)(2,1)} %get-tuple-element.48.refs_0_), channel_id=1, source_target_pairs={{0,96},{32,0},{64,32},{96,64},{1,97},{33,1},{65,33},{97,65},{2,98}... | collective-permute-start | bytes 1179656 | tf_op jit(solution)/shard_map/ppermute | solution.py:406
  103.4 47.9 %collective-permute-start.4 = (bf16[8,192,128]{2,1,0:T(8,128)(2,1)}, bf16[8,192,128]{2,1,0:T(8,128)(2,1)S(1)}, u32[]{:S(2)}, u32[]{:S(2)}) collective-permute-start(bf16[8,192,128]{2,1,0:T(8,128)(2,1)} %get-tuple-element.49.refs_1_), channel_id=1, source_target_pairs={{0,32},{32,64},{64,96},{96,0},{1,33},{33,65},{65,97},{97,1},{2,34}... | collective-permute-start | bytes 1179656 | tf_op jit(solution)/shard_map/ppermute | solution.py:406
  103.4 17.4 %collective-permute-start.6 = (bf16[8,192,128]{2,1,0:T(8,128)(2,1)}, bf16[8,192,128]{2,1,0:T(8,128)(2,1)}, u32[]{:S(2)}, u32[]{:S(2)}) collective-permute-start(bf16[8,192,128]{2,1,0:T(8,128)(2,1)} %get-tuple-element.49.refs_1_), channel_id=1, source_target_pairs={{0,96},{32,0},{64,32},{96,64},{1,97},{33,1},{65,33},{97,65},{2,98}... | collective-permute-start | bytes 1179656 | tf_op jit(solution)/shard_map/ppermute | solution.py:406
  112.6 23.0 %copy-start.1 = (bf16[8,192,128]{2,1,0:T(8,128)(2,1)}, bf16[8,192,128]{2,1,0:T(8,128)(2,1)S(1)}, u32[]{:S(2)}) copy-start(bf16[8,192,128]{2,1,0:T(8,128)(2,1)S(1)} %collective-permute-done.3.refs_2_) | copy-start | bytes 1179652
  112.6 38.8 %collective-permute-start.7 = (bf16[8,192,128]{2,1,0:T(8,128)(2,1)S(1)}, bf16[8,192,128]{2,1,0:T(8,128)(2,1)}, u32[]{:S(2)}, u32[]{:S(2)}) collective-permute-start(bf16[8,192,128]{2,1,0:T(8,128)(2,1)S(1)} %collective-permute-done.3.refs_2_), channel_id=1, source_target_pairs={{0,32},{32,64},{64,96},{96,0},{1,33},{33,65},{65,97},{97,1},{2,34}... | collective-permute-start | bytes 1179656 | tf_op jit(solution)/shard_map/ppermute | solution.py:406
  120.8 30.6 %collective-permute-start.8 = (bf16[8,192,128]{2,1,0:T(8,128)(2,1)}, bf16[8,192,128]{2,1,0:T(8,128)(2,1)}, u32[]{:S(2)}, u32[]{:S(2)}) collective-permute-start(bf16[8,192,128]{2,1,0:T(8,128)(2,1)} %collective-permute-done.6.refs_5_), channel_id=1, source_target_pairs={{0,96},{32,0},{64,32},{96,64},{1,97},{33,1},{65,33},{97,65},{2,98}... | collective-permute-start | bytes 1179656 | tf_op jit(solution)/shard_map/ppermute | solution.py:406
  135.6 15.1 %copy-start.11 = (f32[3]{0:T(128)S(1)}, f32[3]{0:T(128)}, u32[]{:S(2)}) copy-start(f32[3]{0:T(128)} %broadcast_maximum_fusion) | copy-start | bytes 40
  135.7 1.4 copy-start
  142.6 24.5 %all-to-all-start.2 = ((f32[128,1,128]{2,1,0:T(1,128)}), f32[128,1,128]{2,1,0:T(1,128)S(1)}, u32[]{:S(2)}, u32[]{:S(2)}) async-start(f32[128,1,128]{2,1,0:T(1,128)} %get-tuple-element.50), calls=%async_computation.2 | async-start | bytes 131072 | tf_op jit(solution)/shard_map/all_to_all | solution.py:451
  151.3 8.1 %copy-start.4 = (bf16[16,72,128]{2,1,0:T(8,128)(2,1)S(1)}, bf16[16,72,128]{2,1,0:T(8,128)(2,1)}, u32[]{:S(2)}) copy-start(bf16[16,72,128]{2,1,0:T(8,128)(2,1)} %get-tuple-element.47.refs_0_) | copy-start | bytes 884740
  151.3 0.7 copy-start.3
  151.3 0.9 copy-start.2
  159.4 8.8 %collective-permute-start = (bf16[16,72,128]{2,1,0:T(8,128)(2,1)S(1)}, bf16[16,72,128]{2,1,0:T(8,128)(2,1)S(1)}, u32[]{:S(2)}, u32[]{:S(2)}) collective-permute-start(bf16[16,72,128]{2,1,0:T(8,128)(2,1)S(1)} %copy-done.4), channel_id=1, source_target_pairs={{0,32},{32,64},{64,96},{96,0},{1,33},{33,65},{65,97},{97,1},{2,34}... | collective-permute-start | bytes 884744 | tf_op jit(solution)/shard_map/ppermute | solution.py:406
  160.9 7.9 %collective-permute-start.1 = (bf16[16,72,128]{2,1,0:T(8,128)(2,1)S(1)}, bf16[16,72,128]{2,1,0:T(8,128)(2,1)S(1)}, u32[]{:S(2)}, u32[]{:S(2)}) collective-permute-start(bf16[16,72,128]{2,1,0:T(8,128)(2,1)S(1)} %copy-done.4), channel_id=1, source_target_pairs={{0,96},{32,0},{64,32},{96,64},{1,97},{33,1},{65,33},{97,65},{2,98}... | collective-permute-start | bytes 884744 | tf_op jit(solution)/shard_map/ppermute | solution.py:406
  162.2 14.1 %collective-permute-start.2 = (bf16[16,72,128]{2,1,0:T(8,128)(2,1)S(1)}, bf16[16,72,128]{2,1,0:T(8,128)(2,1)S(1)}, u32[]{:S(2)}, u32[]{:S(2)}) collective-permute-start(bf16[16,72,128]{2,1,0:T(8,128)(2,1)S(1)} %copy-done.4), channel_id=1, source_target_pairs={{0,64},{32,96},{64,0},{96,32},{1,65},{33,97},{65,1},{97,33},{2,66}... | collective-permute-start | bytes 884744 | tf_op jit(solution)/shard_map/ppermute | solution.py:406
  168.2 8.1 %copy-start.5 = (bf16[16,72,128]{2,1,0:T(8,128)(2,1)}, bf16[16,72,128]{2,1,0:T(8,128)(2,1)S(1)}, u32[]{:S(2)}) copy-start(bf16[16,72,128]{2,1,0:T(8,128)(2,1)S(1)} %collective-permute-done.refs_1_) | copy-start | bytes 884740
  168.7 7.6 %copy-start.6 = (bf16[16,72,128]{2,1,0:T(8,128)(2,1)}, bf16[16,72,128]{2,1,0:T(8,128)(2,1)S(1)}, u32[]{:S(2)}) copy-start(bf16[16,72,128]{2,1,0:T(8,128)(2,1)S(1)} %collective-permute-done.1.refs_2_) | copy-start | bytes 884740
  176.3 0.7 copy-start.7

commit v5 on v4

--- a/solution.py
+++ b/solution.py
@@ -30,7 +30,6 @@
 VMEM = pl.BlockSpec(memory_space=pltpu.VMEM)
 ANY = pl.BlockSpec(memory_space=pl.ANY)
 STEPS = 8
-SPARE = 94_000
 SPAN = TIME // STEPS
 
 F32 = jnp.float32
@@ -54,6 +53,10 @@
         part[:, :TAIL] = tail
         part[:, TAIL : TAIL + HALF] = tail[half * HALF : (half + 1) * HALF]
     return rows.astype(np.float32), float(weight.sum() * LON)
+
+
+def grant(mebibytes):
+    return pltpu.CompilerParams(vmem_limit_bytes=mebibytes * 2**20)
 
 
 def pack_rows(first, triples, wide, rows, ready):
@@ -128,35 +131,47 @@
     )(x)
 
 
-def unpack(table, scale, out, triples):
-    stride = rows_of(triples) + 1
+def day_rows(table, stride, index):
+    halves = [table[pl.ds(8 * h * stride + index, 8, stride=stride), :] for h in range(DAYS // 8)]
+    return jnp.concatenate(halves, axis=0)
+
+
+def unpack_rows(row, outs, triples):
     count = 3 * triples
     lane = lax.broadcasted_iota(jnp.int32, (DAYS, LANES), 1)
-
-    def row(index):
-        halves = [table[pl.ds(8 * h * stride + index, 8, stride=stride), :] for h in range(DAYS // 8)]
-        value = jnp.concatenate(halves, axis=0)
-        return value if scale is None else value * scale
 
     def whole(lon, carry):
         for j in range(FULL):
-            out[lon, :, j * LANES : (j + 1) * LANES] = row(j * count + lon).astype(BF16)
+            for out, value in zip(outs, row(j * count + lon)):
+                out[lon, :, j * LANES : (j + 1) * LANES] = value.astype(BF16)
         return carry
 
     def tail(lon, carry):
-        out[lon, :, FULL * LANES :] = row(FULL * count + lon)[:, :TAIL].astype(BF16)
+        for out, value in zip(outs, row(FULL * count + lon)):
+            out[lon, :, FULL * LANES :] = value[:, :TAIL].astype(BF16)
         return carry
 
     def last(k, carry):
-        low = pltpu.roll(row(FULL * count + k), LANES - TAIL, 1)
-        high = pltpu.roll(row(FULL * count + triples + k), LANES - TAIL + HALF, 1)
-        joined = jnp.where(lane < HALF, low, high)
-        out[2 * triples + k, :, FULL * LANES :] = joined[:, :TAIL].astype(BF16)
+        for out, low, high in zip(outs, row(FULL * count + k), row(FULL * count + triples + k)):
+            low = pltpu.roll(low, LANES - TAIL, 1)
+            high = pltpu.roll(high, LANES - TAIL + HALF, 1)
+            joined = jnp.where(lane < HALF, low, high)
+            out[2 * triples + k, :, FULL * LANES :] = joined[:, :TAIL].astype(BF16)
         return carry
 
     lax.fori_loop(0, count, whole, 0, unroll=3)
     lax.fori_loop(0, 2 * triples, tail, 0, unroll=2)
     lax.fori_loop(0, triples, last, 0)
+
+
+def unpack(table, scale, out, triples):
+    stride = rows_of(triples) + 1
+
+    def row(index):
+        value = day_rows(table, stride, index)
+        return [value if scale is None else value * scale]
+
+    unpack_rows(row, [out], triples)
 
 
 def zero(table, stride):
@@ -186,14 +201,19 @@
     return pltpu.make_async_copy(x.at[span], held.at[span], got.at[i])
 
 
-def divide(inverse, mean, packed, total):
+def divide(inverse, scale, mean, packed, total):
     stride = total + 1
+    each = total // len(packed)
+
+    def one(k, carry):
+        for p, rows in enumerate(packed):
+            rows[k] = (day_rows(mean, stride, p * each + k) * scale[...]).astype(BF16)
+        return carry
+
+    lax.fori_loop(0, each, one, 0, unroll=4)
     for d in range(DAYS):
         rows = slice(d * stride, d * stride + total)
-        value = mean[rows, :] * inverse[d]
-        mean[rows, :] = value
-        each = DAYS // len(packed)
-        packed[d // each][d % each] = value.astype(BF16)
+        mean[rows, :] = mean[rows, :] * inverse[d]
 
 
 def powers(bins, held, mean, second, third, weight, norm, total, ready=None):
@@ -230,37 +250,37 @@
     return pltpu.make_async_copy(wide.at[i], outs[i].at[pl.ds(first, count)], put.at[i])
 
 
-def sum_kernel(total, bins, inverse, x, mean, low, high, held, got):
+def sum_kernel(total, bins, inverse, scale, x, mean, low, high, held, got):
     for i in range(STEPS):
         enter(x, held, got, i).start()
     zero(mean, total + 1)
     add_up(bins, x, held, got, mean, total)
-    divide(inverse, mean, (low, high), total)
+    divide(inverse, scale, mean, (low, high), total)
 
 
 def table_shape(total):
     return (DAYS * (total + 1), LANES)
 
 
-def half_shape(total):
-    return jax.ShapeDtypeStruct((DAYS // 2, total, LANES), BF16)
-
-
-def sums(bins, inverse, x, triples):
+def row_shape(total):
+    return jax.ShapeDtypeStruct((total, DAYS, LANES), BF16)
+
+
+def sums(bins, inverse, scale, x, triples):
     total = rows_of(triples)
     return pl.pallas_call(
         functools.partial(sum_kernel, total),
-        in_specs=[SMEM, SMEM, ANY],
+        in_specs=[SMEM, SMEM, VMEM, ANY],
         out_specs=[VMEM] * 3,
-        out_shape=[jax.ShapeDtypeStruct(table_shape(total), F32), half_shape(total), half_shape(total)],
+        out_shape=[jax.ShapeDtypeStruct(table_shape(total), F32)] + [row_shape(total // 2)] * 2,
         scratch_shapes=[pltpu.VMEM((TIME, total, LANES), BF16), pltpu.SemaphoreType.DMA((STEPS,))],
         cost_estimate=pl.CostEstimate(flops=10_000_000 * triples, bytes_accessed=700_000 * triples, transcendentals=0),
         name="sums",
-    )(bins, inverse, x)
+    )(bins, inverse, scale, x)
 
 
 def power_kernel(first, triples, bins, x, mean, scale, weight, *refs):
-    outs, (after, held, second, third, norm, wide, got, put, _) = refs[:3], refs[3:]
+    outs, (after, held, second, third, norm, wide, got, put) = refs[:3], refs[3:]
     total = rows_of(triples)
     count = 3 * triples
     for i in range(STEPS):
@@ -298,7 +318,6 @@
             pltpu.VMEM((3, 3 * triples, DAYS, LAT), BF16),
             pltpu.SemaphoreType.DMA((STEPS,)),
             pltpu.SemaphoreType.DMA((3,)),
-            pltpu.VMEM((SPARE, LANES), F32),
         ],
         cost_estimate=pl.CostEstimate(flops=40_000_000 * triples, bytes_accessed=1_000_000 * triples, transcendentals=0),
         name="higher",
@@ -306,82 +325,88 @@
     return result[:3], result[3]
 
 
-def both_kernel(total, bins, inverse, x, weight, before, mean, second, third, packed, after, held, norm, got):
+def both_kernel(first, triples, bins, inverse, scale, x, weight, before, *refs):
+    outs, (packed, after, held, mean, second, third, norm, wide, got, put) = refs[3:6], refs[6:]
+    total = rows_of(triples)
+    count = 3 * triples
     for i in range(STEPS):
         enter(x, held, got, i).start()
     for table in (mean, second, third):
         zero(table, total + 1)
     add_up(bins, x, held, got, mean, total)
-    divide(inverse, mean, (packed,), total)
+    divide(inverse, scale, mean, (packed,), total)
+    unpack(mean, None, wide.at[0], triples)
+    leave(wide, outs, put, first, count, 0).start()
     powers(bins, held, mean, second, third, weight, norm, total)
     row = before[...] + total_norm(norm)
     after[:, 0, :] = jnp.broadcast_to(row, (MODELS * PEERS, TIME))
-
-
-def both(bins, inverse, x, weight, before, triples):
-    total = rows_of(triples)
-    table = jax.ShapeDtypeStruct(table_shape(total), F32)
+    for i, table in ((1, second), (2, third)):
+        unpack(table, scale[...], wide.at[i], triples)
+        leave(wide, outs, put, first, count, i).start()
+    for i in range(3):
+        leave(wide, outs, put, first, count, i).wait()
+
+
+def both(bins, inverse, scale, x, weight, before, outs, first, triples):
+    total = rows_of(triples)
     result = pl.pallas_call(
-        functools.partial(both_kernel, total),
-        in_specs=[SMEM, SMEM, ANY, VMEM, VMEM],
-        out_specs=[VMEM] * 5,
-        out_shape=[table] * 3
-        + [jax.ShapeDtypeStruct((DAYS, total, LANES), BF16)]
-        + [jax.ShapeDtypeStruct((MODELS * PEERS, 1, TIME), F32)],
+        functools.partial(both_kernel, first, triples),
+        in_specs=[SMEM, SMEM, VMEM, ANY, VMEM, VMEM] + [ANY] * 3,
+        out_specs=[ANY] * 3 + [VMEM] * 2,
+        out_shape=[FIELD] * 3 + [row_shape(total), jax.ShapeDtypeStruct((MODELS * PEERS, 1, TIME), F32)],
+        input_output_aliases={6: 0, 7: 1, 8: 2},
         scratch_shapes=[
             pltpu.VMEM((TIME, total, LANES), BF16),
+            pltpu.VMEM(table_shape(total), F32),
+            pltpu.VMEM(table_shape(total), F32),
+            pltpu.VMEM(table_shape(total), F32),
             pltpu.VMEM((TIME, 8, LANES), F32),
+            pltpu.VMEM((3, 3 * triples, DAYS, LAT), BF16),
             pltpu.SemaphoreType.DMA((STEPS,)),
+            pltpu.SemaphoreType.DMA((3,)),
         ],
         cost_estimate=pl.CostEstimate(flops=50_000_000 * triples, bytes_accessed=1_000_000 * triples, transcendentals=0),
         name="both",
-    )(bins, inverse, x, weight, before)
+        compiler_params=grant(24),
+    )(bins, inverse, scale, x, weight, before, *outs)
     return result[:3], result[3], result[4]
-
-
-def unpack_kernel(first, triples, scale, *refs):
-    tables, outs, wide, put = refs[:3], refs[6:9], refs[9], refs[10]
-    for i in range(3):
-        unpack(tables[i], None if i == 0 else scale[...], wide.at[i], triples)
-        leave(wide, outs, put, first, 3 * triples, i).start()
-    for i in range(3):
-        leave(wide, outs, put, first, 3 * triples, i).wait()
-
-
-def unpacked(scale, tables, outs, first, triples):
-    return pl.pallas_call(
-        functools.partial(unpack_kernel, first, triples),
-        in_specs=[VMEM] * 4 + [ANY] * 3,
-        out_specs=[ANY] * 3,
-        out_shape=[FIELD] * 3,
-        input_output_aliases={4: 0, 5: 1, 6: 2},
-        scratch_shapes=[pltpu.VMEM((3, 3 * triples, DAYS, LAT), BF16), pltpu.SemaphoreType.DMA((3,))],
-        cost_estimate=pl.CostEstimate(flops=3_000_000 * triples, bytes_accessed=700_000 * triples, transcendentals=0),
-        name="unpacked",
-    )(scale, *tables, *outs)
 
 
 def family_kernel(first, triples, chained, pieces, share, *refs):
     means, refs = refs[: pieces * MODELS], refs[pieces * MODELS + (1 if chained else 0) :]
-    each = DAYS // pieces
-    out, table, wide, sem = refs
-    total = rows_of(triples)
-    stride = total + 1
-    count = 3 * triples
-    for d in range(DAYS):
-        values = [means[pieces * k + d // each][d % each].astype(F32) for k in range(MODELS)]
+    out, held, wide, got, put = refs
+    total = rows_of(triples)
+    count = 3 * triples
+    each = total // pieces
+
+    def enter(i):
+        k, p = i // pieces, i % pieces
+        return pltpu.make_async_copy(means[i], held.at[k, pl.ds(p * each, each)], got.at[i])
+
+    def leave(f):
+        return pltpu.make_async_copy(wide.at[f], out.at[f, pl.ds(first, count)], put.at[f])
+
+    for i in range(pieces * MODELS):
+        enter(i).start()
+    for i in range(pieces * MODELS):
+        enter(i).wait()
+    shares = [[share[f, k] for k in range(MODELS)] for f in range(FAM)]
+
+    def row(index):
+        values = [held[k, index].astype(F32) for k in range(MODELS)]
+        results = []
         for f in range(FAM):
-            value = values[0] * share[f, 0]
+            value = values[0] * shares[f][0]
             for k in range(1, MODELS):
-                value = value + values[k] * share[f, k]
-            table[f, d * stride : d * stride + total, :] = value
-    copies = []
+                value = value + values[k] * shares[f][k]
+            results.append(value)
+        return results
+
+    unpack_rows(row, [wide.at[f] for f in range(FAM)], triples)
     for f in range(FAM):
-        unpack(table.at[f], None, wide.at[f], triples)
-        copies.append(pltpu.make_async_copy(wide.at[f], out.at[f, pl.ds(first, count)], sem.at[f]))
-        copies[-1].start()
-    for copy in copies:
-        copy.wait()
+        leave(f).start()
+    for f in range(FAM):
+        leave(f).wait()
 
 
 def families(share, means, out, first, triples):
@@ -389,16 +414,18 @@
     chained = out is not None
     return pl.pallas_call(
         functools.partial(family_kernel, first, triples, chained, len(means) // MODELS),
-        in_specs=[SMEM] + [VMEM] * len(means) + [ANY] * (1 if chained else 0),
+        in_specs=[SMEM] + [ANY] * len(means) + [ANY] * (1 if chained else 0),
         out_specs=ANY,
         out_shape=jax.ShapeDtypeStruct((FAM, BAND, DAYS, LAT), BF16),
         input_output_aliases={1 + len(means): 0} if chained else {},
         scratch_shapes=[
-            pltpu.VMEM((FAM, *table_shape(total)), F32),
+            pltpu.VMEM((MODELS, total, DAYS, LANES), BF16),
             pltpu.VMEM((FAM, 3 * triples, DAYS, LAT), BF16),
+            pltpu.SemaphoreType.DMA((len(means),)),
             pltpu.SemaphoreType.DMA((FAM,)),
         ],
         cost_estimate=pl.CostEstimate(flops=10_000_000 * triples, bytes_accessed=500_000 * triples, transcendentals=0),
+        compiler_params=grant(12) if chained else None,
     )(share, *means, *(() if out is None else (out,)))
 
 
@@ -441,15 +468,16 @@
     weight0, total_weight = packed_weight(CHUNKS[0])
     weight1, _ = packed_weight(CHUNKS[1])
     x0 = got0.reshape(TIME, rows_of(CHUNKS[0]), LANES)
-    table0, low0, high0 = sums(day_bins, inverse, x0, CHUNKS[0])
+    table0, low0, high0 = sums(day_bins, inverse, scale, x0, CHUNKS[0])
     means0 = forwarded(low0, high0)
     outs, norm0 = higher(day_bins, x0, table0, scale, jnp.asarray(weight0), STARTS[0], CHUNKS[0])
     got1, norm0 = lax.optimization_barrier((got1, norm0))
     x1 = got1.reshape(TIME, rows_of(CHUNKS[1]), LANES)
-    tables1, mean1, norm = both(day_bins, inverse, x1, jnp.asarray(weight1), norm0, CHUNKS[1])
+    outs, mean1, norm = both(
+        day_bins, inverse, scale, x1, jnp.asarray(weight1), norm0, outs, STARTS[1], CHUNKS[1]
+    )
     means1 = [mean1, *(moved(mean1, by) for by in (1, -1, 2))]
     parts = lax.all_to_all(norm, ("group", "tm"), split_axis=0, concat_axis=0, tiled=True)
-    outs = unpacked(scale, tables1, outs, STARTS[1], CHUNKS[1])
     fam = families(share, means0, None, STARTS[0], CHUNKS[0])
     fam = families(share, means1, fam, STARTS[1], CHUNKS[1])
 

time: 181 us -> 179 us (0.989)
  waiting for transfers between devices: 22.6 us -> 26.5 us
  Pallas kernels: 43.3 us -> 39.7 us
    ppermute x9, waiting for transfers between devices: 22.6 us -> 26.4 us  [moved(): lax.ppermute(array, 'group', [(i, (i + by) % MODELS) for i in range(MODEL...]
    pallas_call x2 -> x1, Pallas kernels: 8.82 us -> 6.55 us  [both(): pl.pallas_call(functools.partial(both_kernel, first, triples), in_specs=[...]
  transfers between devices with their start and end apart: 11 -> 11, of which waited for: 5 -> 5; matrix products, arithmetic and copies ran while one was open for 2% -> 1% of each run, Pallas kernels for 18% -> 17%
where the time goes in v5:
time: 179 us; the launch traced here: 178 us
  blocking collectives  82.6 us (46%)
  Pallas kernels  39.7 us (22%)
  waiting for transfers between devices  26.5 us (15%)
  starting transfers between devices  24.9 us (14%)
  local copies, waits for them, and re-layouts  2.03 us (1%)
    all_to_all x1, blocking collectives, exchange(): return lax.all_to_all(array, 'tm', split_axis=0, concat_axis=0, tiled=True)  82.6 us
    ppermute x9, waiting for transfers between devices, moved(): lax.ppermute(array, 'group', [(i, (i + by) % MODELS) for i in range(MODEL...  26.4 us
    ppermute x9, starting transfers between devices, moved(): lax.ppermute(array, 'group', [(i, (i + by) % MODELS) for i in range(MODEL...  12.8 us
    pallas_call x1, Pallas kernels, higher(): pl.pallas_call(functools.partial(power_kernel, first, triples), in_specs=...  11.3 us
    pallas_call x2, Pallas kernels, families(): pl.pallas_call(functools.partial(family_kernel, first, triples, chained,...  9.2 us
    all_to_all x1, starting transfers between devices, local(): lax.all_to_all(norm, ('group', 'tm'), split_axis=0, concat_axis=0, tiled=...  8.04 us
    pallas_call x1, Pallas kernels, pack(): pl.pallas_call(functools.partial(pack_kernel, steps), in_specs=[ANY], out...  7.15 us
    pallas_call x1, Pallas kernels, both(): pl.pallas_call(functools.partial(both_kernel, first, triples), in_specs=[...  6.55 us
  transfers between devices with their start and end apart: 11, of which 5 were waited for; matrix products, arithmetic and copies ran while one was open for 1% of the time, Pallas kernels for 17%

profile of v5, /device:TPU:1, one launch (start us, length us, event | category | flops | bytes accessed | tf_op | source)
XLA Modules:
  0.0 178.2 jit_solution(595035695387024360)
XLA Ops:
  0.6 7.2 %pack.1 = (bf16[32,4,192,128]{3,2,1,0:T(8,128)(2,1)}, bf16[32,4,72,128]{3,2,1,0:T(8,128)(2,1)}) custom-call(bf16[4,1440,720]{2,1,0:T(8,128)(2,1)} %bitcast.20), custom_call_target="tpu_custom_call" | custom-call | flops 10000000 | bytes 17000000 | tf_op jit(solution)/shard_map/pack/pallas_call | solution.py:119
  7.8 82.6 %all_to_all.15 = bf16[32,4,192,128]{3,2,1,0:T(8,128)(2,1)} all-to-all(bf16[32,4,192,128]{3,2,1,0:T(8,128)(2,1)} %get-tuple-element.25), channel_id=1, replica_groups=mesh['group'=4,'tm'=32] {'tm'}, dimensions={0} | all-to-all | bytes 12582912 | tf_op jit(solution)/shard_map/all_to_all | solution.py:447
  90.4 4.1 %all-to-all-start.1 = ((bf16[32,4,72,128]{3,2,1,0:T(8,128)(2,1)}), bf16[32,4,72,128]{3,2,1,0:T(8,128)(2,1)S(1)}, u32[]{:S(2)}, u32[]{:S(2)}) async-start(bf16[32,4,72,128]{3,2,1,0:T(8,128)(2,1)} %get-tuple-element.28), calls=%async_computation.1 | async-start | bytes 4718592 | tf_op jit(solution)/shard_map/all_to_all | solution.py:447
  94.5 0.0 copy-done.11
  94.5 0.1 fusion.1
  94.6 0.0 copy-done.3
  94.6 0.1 convert_reduce_fusion
  94.7 0.0 copy-start.5
  94.7 0.7 broadcast_in_dim.8.scale
  95.4 0.0 copy-done.5
  95.4 5.5 %sums.1 = (f32[3088,128]{1,0:T(8,128)}, bf16[96,16,128]{2,1,0:T(8,128)(2,1)}, bf16[96,16,128]{2,1,0:T(8,128)(2,1)}) custom-call(s32[128]{0:T(128)} %bins.2, f32[16]{0:T(128)} %copy-done.5, f32[16,128]{1,0:T(8,128)} %broadcast_in_dim.8.scale, bf16[128,192,128]{2,1,0:T(8,128)(2,1)} %bitcast.17), custom_call_target="tpu_custom_call" | custom-call | flops 110000000 | bytes 7700000 | tf_op jit(solution)/shard_map/sums/pallas_call | solution.py:271
  100.9 1.4 collective-permute-start.3
  102.2 1.5 collective-permute-start.5
  103.7 0.0 collective-permute-start.4
  103.7 2.7 %collective-permute-start.6 = (bf16[96,16,128]{2,1,0:T(8,128)(2,1)}, bf16[96,16,128]{2,1,0:T(8,128)(2,1)}, u32[]{:S(2)}, u32[]{:S(2)}) collective-permute-start(bf16[96,16,128]{2,1,0:T(8,128)(2,1)} %get-tuple-element.43.refs_1_), channel_id=1, source_target_pairs={{0,96},{32,0},{64,32},{96,64},{1,97},{33,1},{65,33},{97,65},{2,98}... | collective-permute-start | bytes 1179656 | tf_op jit(solution)/shard_map/ppermute | solution.py:433
  106.4 0.0 copy-done.10
  106.4 0.1 fusion.3
  106.5 6.3 %collective-permute-done.3.refs_2_ = bf16[96,16,128]{2,1,0:T(8,128)(2,1)S(1)} collective-permute-done((bf16[96,16,128]{2,1,0:T(8,128)(2,1)}, bf16[96,16,128]{2,1,0:T(8,128)(2,1)S(1)}, u32[]{:S(2)}, u32[]{:S(2)}) %collective-permute-start.3) | collective-permute-done | bytes 393248 | tf_op jit(solution)/shard_map/ppermute | solution.py:433
  112.9 0.0 collective-permute-start.7
  112.9 8.2 %collective-permute-done.6.refs_5_ = bf16[96,16,128]{2,1,0:T(8,128)(2,1)} collective-permute-done((bf16[96,16,128]{2,1,0:T(8,128)(2,1)}, bf16[96,16,128]{2,1,0:T(8,128)(2,1)}, u32[]{:S(2)}, u32[]{:S(2)}) %collective-permute-start.6) | collective-permute-done | bytes 393248 | tf_op jit(solution)/shard_map/ppermute | solution.py:433
  121.1 2.9 %collective-permute-start.8 = (bf16[96,16,128]{2,1,0:T(8,128)(2,1)}, bf16[96,16,128]{2,1,0:T(8,128)(2,1)}, u32[]{:S(2)}, u32[]{:S(2)}) collective-permute-start(bf16[96,16,128]{2,1,0:T(8,128)(2,1)} %collective-permute-done.6.refs_5_), channel_id=1, source_target_pairs={{0,96},{32,0},{64,32},{96,64},{1,97},{33,1},{65,33},{97,65},{2,98}... | collective-permute-start | bytes 1179656 | tf_op jit(solution)/shard_map/ppermute | solution.py:433
  124.0 11.3 %higher.1 = (bf16[45,16,720]{2,1,0:T(8,128)(2,1)}, bf16[45,16,720]{2,1,0:T(8,128)(2,1)}, bf16[45,16,720]{2,1,0:T(8,128)(2,1)}, f32[1,128]{1,0:T(1,128)}) custom-call(s32[128]{0:T(128)} %bins.2, bf16[128,192,128]{2,1,0:T(8,128)(2,1)} %bitcast.18, f32[3088,128]{1,0:T(8,128)} %get-tuple-element.30.mean, f32[16,128]{1,0:T(8,128)} %broadcast_in_dim.8.scale, ...), custom_call_target="tpu_custom_call" | custom-call | flops 440000000 | bytes 11000000 | tf_op jit(solution)/shard_map/higher/pallas_call | solution.py:308
  135.3 0.0 copy-done.8
  135.3 0.1 multiply_reduce_fusion
  135.4 0.0 all-to-all-done.1
  135.4 0.0 copy-done
  135.4 0.0 copy-done.1
  135.4 0.0 copy-done.4
  135.5 0.6 copy-done.7
  136.1 6.5 %both.1 = (bf16[45,16,720]{2,1,0:T(8,128)(2,1)}, bf16[45,16,720]{2,1,0:T(8,128)(2,1)}, bf16[45,16,720]{2,1,0:T(8,128)(2,1)}, bf16[72,16,128]{2,1,0:T(8,128)(2,1)S(1)}, f32[128,1,128]{2,1,0:T(1,128)}) custom-call(s32[128]{0:T(128)S(1)} %copy-done.4, f32[16]{0:T(128)S(1)} %copy-done.6, ...), custom_call_target="tpu_custom_call", output_to_operand_aliasing={{0}: (6, {}), {1}: (7, {}), {2}: (8, {})} | custom-call | flops 200000000 | bytes 4000000 | tf_op jit(solution)/shard_map/both/pallas_call | solution.py:352
  142.6 8.0 %all-to-all-start.2 = ((f32[128,1,128]{2,1,0:T(1,128)}), f32[128,1,128]{2,1,0:T(1,128)S(1)}, u32[]{:S(2)}, u32[]{:S(2)}) async-start(f32[128,1,128]{2,1,0:T(1,128)} %get-tuple-element.44), calls=%async_computation.2 | async-start | bytes 131072 | tf_op jit(solution)/shard_map/all_to_all | solution.py:480
  150.7 0.7 broadcast_divide_fusion.share
  151.3 0.0 collective-permute-done.4.refs_3_
  151.3 0.0 collective-permute-done.5.refs_4_
  151.3 0.0 copy-start.9
  151.3 0.0 collective-permute-done.7.refs_6_
  151.3 0.0 collective-permute-done.8.refs_7_
  151.4 0.7 copy-done.9
  152.1 6.5 %shard_map.101.refs_4_ = bf16[3,45,16,720]{3,2,1,0:T(8,128)(2,1)} custom-call(f32[3,4]{1,0:T(4,128)} %broadcast_divide_fusion.share, bf16[96,16,128]{2,1,0:T(8,128)(2,1)} %get-tuple-element.42.refs_0_, bf16[96,16,128]{2,1,0:T(8,128)(2,1)} %get-tuple-element.43.refs_1_, bf16[96,16,128]{2,1,0:T(8,128)(2,1)} %copy-done.8, ...), custom_call_target="tpu_custom_call" | custom-call | flops 110000000 | bytes 5500000 | tf_op jit(solution)/shard_map/pallas_call | solution.py:415
  158.6 1.4 collective-permute-start
  160.0 1.4 collective-permute-start.1
  161.4 1.6 collective-permute-start.2
  163.0 0.0 all-to-all-done.2
  163.0 0.6 multiply_sqrt_fusion
  163.6 3.8 %collective-permute-done.refs_1_ = bf16[72,16,128]{2,1,0:T(8,128)(2,1)S(1)} collective-permute-done((bf16[72,16,128]{2,1,0:T(8,128)(2,1)S(1)}, bf16[72,16,128]{2,1,0:T(8,128)(2,1)S(1)}, u32[]{:S(2)}, u32[]{:S(2)}) %collective-permute-start) | collective-permute-done | bytes 294944 | tf_op jit(solution)/shard_map/ppermute | solution.py:433
  167.4 0.5 collective-permute-done.1.refs_2_
  167.9 7.6 %collective-permute-done.2.refs_3_ = bf16[72,16,128]{2,1,0:T(8,128)(2,1)S(1)} collective-permute-done((bf16[72,16,128]{2,1,0:T(8,128)(2,1)S(1)}, bf16[72,16,128]{2,1,0:T(8,128)(2,1)S(1)}, u32[]{:S(2)}, u32[]{:S(2)}) %collective-permute-start.2) | collective-permute-done | bytes 294944 | tf_op jit(solution)/shard_map/ppermute | solution.py:433
  175.5 2.7 %shard_map.102 = bf16[3,45,16,720]{3,2,1,0:T(8,128)(2,1)} custom-call(f32[3,4]{1,0:T(4,128)S(1)} %copy-done.2, bf16[72,16,128]{2,1,0:T(8,128)(2,1)S(1)} %get-tuple-element.41.refs_0_, bf16[72,16,128]{2,1,0:T(8,128)(2,1)S(1)} %collective-permute-done.refs_1_, bf16[72,16,128]{2,1,0:T(8,128)(2,1)S(1)} %collective-permute-done.1.refs_2_, ...), custom_call_target="tpu_custom_call", output_to_operand_aliasing={{}: (5, {})} | custom-call | flops 40000000 | bytes 2000000 | tf_op jit(solution)/shard_map/pallas_call | solution.py:415
  (17 shorter events, 0.1 us)
Async XLA Ops:
  90.4 4.1 %copy-start.11 = (s32[4]{0:T(128)S(1)}, s32[4]{0:T(128)}, u32[]{:S(2)}) copy-start(s32[4]{0:T(128)} %constant.35.clone) | copy-start | bytes 52
  90.4 4.2 %copy-start.3 = (s32[128]{0:T(128)S(1)}, s32[128]{0:T(128)}, u32[]{:S(2)}) copy-start(s32[128]{0:T(128)} %bins.2) | copy-start | bytes 1540
  90.4 45.0 %all-to-all-start.1 = ((bf16[32,4,72,128]{3,2,1,0:T(8,128)(2,1)}), bf16[32,4,72,128]{3,2,1,0:T(8,128)(2,1)S(1)}, u32[]{:S(2)}, u32[]{:S(2)}) async-start(bf16[32,4,72,128]{3,2,1,0:T(8,128)(2,1)} %get-tuple-element.28), calls=%async_computation.1 | async-start | bytes 4718592 | tf_op jit(solution)/shard_map/all_to_all | solution.py:447
  94.7 0.7 copy-start.5
  95.4 11.0 %copy-start.10 = (s32[4]{0:T(128)S(1)}, s32[4]{0:T(128)}, u32[]{:S(2)}) copy-start(s32[4]{0:T(128)} %param.8) | copy-start | bytes 52
  100.9 12.0 %collective-permute-start.3 = (bf16[96,16,128]{2,1,0:T(8,128)(2,1)}, bf16[96,16,128]{2,1,0:T(8,128)(2,1)S(1)}, u32[]{:S(2)}, u32[]{:S(2)}) collective-permute-start(bf16[96,16,128]{2,1,0:T(8,128)(2,1)} %get-tuple-element.42.refs_0_), channel_id=1, source_target_pairs={{0,32},{32,64},{64,96},{96,0},{1,33},{33,65},{65,97},{97,1},{2,34}... | collective-permute-start | bytes 1179656 | tf_op jit(solution)/shard_map/ppermute | solution.py:433
  102.2 49.1 %collective-permute-start.5 = (bf16[96,16,128]{2,1,0:T(8,128)(2,1)}, bf16[96,16,128]{2,1,0:T(8,128)(2,1)S(1)}, u32[]{:S(2)}, u32[]{:S(2)}) collective-permute-start(bf16[96,16,128]{2,1,0:T(8,128)(2,1)} %get-tuple-element.42.refs_0_), channel_id=1, source_target_pairs={{0,96},{32,0},{64,32},{96,64},{1,97},{33,1},{65,33},{97,65},{2,98}... | collective-permute-start | bytes 1179656 | tf_op jit(solution)/shard_map/ppermute | solution.py:433
  103.7 47.6 %collective-permute-start.4 = (bf16[96,16,128]{2,1,0:T(8,128)(2,1)}, bf16[96,16,128]{2,1,0:T(8,128)(2,1)}, u32[]{:S(2)}, u32[]{:S(2)}) collective-permute-start(bf16[96,16,128]{2,1,0:T(8,128)(2,1)} %get-tuple-element.43.refs_1_), channel_id=1, source_target_pairs={{0,32},{32,64},{64,96},{96,0},{1,33},{33,65},{65,97},{97,1},{2,34}... | collective-permute-start | bytes 1179656 | tf_op jit(solution)/shard_map/ppermute | solution.py:433
  103.7 17.4 %collective-permute-start.6 = (bf16[96,16,128]{2,1,0:T(8,128)(2,1)}, bf16[96,16,128]{2,1,0:T(8,128)(2,1)}, u32[]{:S(2)}, u32[]{:S(2)}) collective-permute-start(bf16[96,16,128]{2,1,0:T(8,128)(2,1)} %get-tuple-element.43.refs_1_), channel_id=1, source_target_pairs={{0,96},{32,0},{64,32},{96,64},{1,97},{33,1},{65,33},{97,65},{2,98}... | collective-permute-start | bytes 1179656 | tf_op jit(solution)/shard_map/ppermute | solution.py:433
  112.9 22.4 %copy-start.8 = (bf16[96,16,128]{2,1,0:T(8,128)(2,1)}, bf16[96,16,128]{2,1,0:T(8,128)(2,1)S(1)}, u32[]{:S(2)}) copy-start(bf16[96,16,128]{2,1,0:T(8,128)(2,1)S(1)} %collective-permute-done.3.refs_2_) | copy-start | bytes 1179652
  112.9 38.4 %collective-permute-start.7 = (bf16[96,16,128]{2,1,0:T(8,128)(2,1)S(1)}, bf16[96,16,128]{2,1,0:T(8,128)(2,1)}, u32[]{:S(2)}, u32[]{:S(2)}) collective-permute-start(bf16[96,16,128]{2,1,0:T(8,128)(2,1)S(1)} %collective-permute-done.3.refs_2_), channel_id=1, source_target_pairs={{0,32},{32,64},{64,96},{96,0},{1,33},{33,65},{65,97},{97,1},{2,34}... | collective-permute-start | bytes 1179656 | tf_op jit(solution)/shard_map/ppermute | solution.py:433
  121.1 30.2 %collective-permute-start.8 = (bf16[96,16,128]{2,1,0:T(8,128)(2,1)}, bf16[96,16,128]{2,1,0:T(8,128)(2,1)}, u32[]{:S(2)}, u32[]{:S(2)}) collective-permute-start(bf16[96,16,128]{2,1,0:T(8,128)(2,1)} %collective-permute-done.6.refs_5_), channel_id=1, source_target_pairs={{0,96},{32,0},{64,32},{96,64},{1,97},{33,1},{65,33},{97,65},{2,98}... | collective-permute-start | bytes 1179656 | tf_op jit(solution)/shard_map/ppermute | solution.py:433
  124.0 11.5 %copy-start = (f32[16,128]{1,0:T(8,128)S(1)}, f32[16,128]{1,0:T(8,128)}, u32[]{:S(2)}) copy-start(f32[16,128]{1,0:T(8,128)} %broadcast_in_dim.8.scale) | copy-start | bytes 24580
  124.0 11.5 %copy-start.1 = (f32[72,128]{1,0:T(8,128)S(1)}, f32[72,128]{1,0:T(8,128)}, u32[]{:S(2)}) copy-start(f32[72,128]{1,0:T(8,128)} %constant.37.clone.weight) | copy-start | bytes 110596
  124.0 11.5 %copy-start.4 = (s32[128]{0:T(128)S(1)}, s32[128]{0:T(128)}, u32[]{:S(2)}) copy-start(s32[128]{0:T(128)} %bins.2) | copy-start | bytes 1540
  124.0 11.5 %copy-start.6 = (f32[16]{0:T(128)S(1)}, f32[16]{0:T(128)}, u32[]{:S(2)}) copy-start(f32[16]{0:T(128)} %copy-done.5) | copy-start | bytes 196
  135.5 0.6 copy-start.7
  142.6 20.4 %all-to-all-start.2 = ((f32[128,1,128]{2,1,0:T(1,128)}), f32[128,1,128]{2,1,0:T(1,128)S(1)}, u32[]{:S(2)}, u32[]{:S(2)}) async-start(f32[128,1,128]{2,1,0:T(1,128)} %get-tuple-element.44), calls=%async_computation.2 | async-start | bytes 131072 | tf_op jit(solution)/shard_map/all_to_all | solution.py:480
  151.3 24.2 %copy-start.2 = (f32[3,4]{1,0:T(4,128)S(1)}, f32[3,4]{1,0:T(4,128)}, u32[]{:S(2)}) copy-start(f32[3,4]{1,0:T(4,128)} %broadcast_divide_fusion.share) | copy-start | bytes 148
  151.3 0.8 copy-start.9
  158.6 8.8 %collective-permute-start = (bf16[72,16,128]{2,1,0:T(8,128)(2,1)S(1)}, bf16[72,16,128]{2,1,0:T(8,128)(2,1)S(1)}, u32[]{:S(2)}, u32[]{:S(2)}) collective-permute-start(bf16[72,16,128]{2,1,0:T(8,128)(2,1)S(1)} %get-tuple-element.41.refs_0_), channel_id=1, source_target_pairs={{0,32},{32,64},{64,96},{96,0},{1,33},{33,65},{65,97},{97,1},{2,34}... | collective-permute-start | bytes 884744 | tf_op jit(solution)/shard_map/ppermute | solution.py:433
  160.0 7.9 %collective-permute-start.1 = (bf16[72,16,128]{2,1,0:T(8,128)(2,1)S(1)}, bf16[72,16,128]{2,1,0:T(8,128)(2,1)S(1)}, u32[]{:S(2)}, u32[]{:S(2)}) collective-permute-start(bf16[72,16,128]{2,1,0:T(8,128)(2,1)S(1)} %get-tuple-element.41.refs_0_), channel_id=1, source_target_pairs={{0,96},{32,0},{64,32},{96,64},{1,97},{33,1},{65,33},{97,65},{2,98}... | collective-permute-start | bytes 884744 | tf_op jit(solution)/shard_map/ppermute | solution.py:433
  161.4 14.1 %collective-permute-start.2 = (bf16[72,16,128]{2,1,0:T(8,128)(2,1)S(1)}, bf16[72,16,128]{2,1,0:T(8,128)(2,1)S(1)}, u32[]{:S(2)}, u32[]{:S(2)}) collective-permute-start(bf16[72,16,128]{2,1,0:T(8,128)(2,1)S(1)} %get-tuple-element.41.refs_0_), channel_id=1, source_target_pairs={{0,64},{32,96},{64,0},{96,32},{1,65},{33,97},{65,1},{97,33},{2,66}... | collective-permute-start | bytes 884744 | tf_op jit(solution)/shard_map/ppermute | solution.py:433

commit v6 on v5

v6 whole, which is shorter than its diff:
```python
import functools
import math

import jax
import jax.numpy as jnp
import numpy as np
from jax import lax
from jax.experimental import pallas as pl
from jax.experimental.pallas import tpu as pltpu
from jax.sharding import PartitionSpec as P


LON = 1440
LAT = 720
DAYS = 16
FAM = 3
MODELS = 4
TIME = 128
LANES = 128
FULL = LAT // LANES
TAIL = LAT - FULL * LANES
HALF = TAIL // 2
PEERS = 32
BAND = LON // PEERS
BLOCK = 8 * BAND
CHUNKS = ((15, 16), (14,))
STARTS = tuple(sum(map(sum, CHUNKS[:c])) for c in range(len(CHUNKS)))

SMEM = pl.BlockSpec(memory_space=pltpu.SMEM)
VMEM = pl.BlockSpec(memory_space=pltpu.VMEM)
ANY = pl.BlockSpec(memory_space=pl.ANY)
STEPS = 8
LIMITS = (None, None, 12)
SPAN = TIME // STEPS

F32 = jnp.float32
BF16 = jnp.bfloat16


def tails_of(count):
    return -(-2 * count // 3)


def block_rows(count):
    return FULL * count + tails_of(count)


def rows_of(chunk):
    return -(-sum(map(block_rows, chunk)) // 8) * 8


def blocks_of(chunk):
    lon = row = 0
    for count in chunk:
        yield lon, row, count, tails_of(count), count - tails_of(count)
        lon += count
        row += block_rows(count)


def packed_weight(chunk):
    lat = np.arange(LAT, dtype=np.float64)
    weight = np.cos((-90.0 + (lat + 0.5) * 180.0 / LAT) * (math.pi / 180.0))
    rows = np.zeros((rows_of(chunk), LANES))
    left = weight[FULL * LANES :]
    for _, base, count, tails, split in blocks_of(chunk):
        for j in range(FULL):
            rows[base + j * count : base + (j + 1) * count] = weight[j * LANES : (j + 1) * LANES]
        at = base + FULL * count
        rows[at : at + tails, :TAIL] = left
        for half in range(2):
            part = rows[at + half * split : at + (half + 1) * split]
            part[:, TAIL : TAIL + HALF] = left[half * HALF : (half + 1) * HALF]
    return rows.astype(np.float32), float(weight.sum() * LON)


def loop(length, body, unroll):
    def some(k, carry):
        for i in range(unroll):
            body(k * unroll + i)
        return carry

    lax.fori_loop(0, length // unroll, some, 0)
    for i in range(length - length % unroll, length):
        body(i)


def grant(mebibytes):
    return pltpu.CompilerParams(vmem_limit_bytes=mebibytes * 2**20)


def pack_rows(first, chunk, wide, rows, ready):
    for r in range(8):
        for lon, base, count, tails, split in blocks_of(chunk):
            s = BAND * r + first + lon
            for j in range(FULL):
                rows[base + j * count : base + (j + 1) * count, :] = wide[j, s : s + count, :]
            at = base + FULL * count
            lane = lax.broadcasted_iota(jnp.int32, (split, LANES), 1)
            third = wide[FULL, s + tails : s + count, :]
            for half in range(2):
                own = wide[FULL, s + half * split : s + (half + 1) * split, :]
                moved = pltpu.roll(third, TAIL - half * HALF, 1)
                rows[at + half * split : at + (half + 1) * split, :] = jnp.where(
                    lane < TAIL, own, jnp.where(lane < TAIL + HALF, moved, 0.0)
                )
            if tails > 2 * split:
                own = wide[FULL, s + 2 * split : s + tails, :]
                lane = lax.broadcasted_iota(jnp.int32, own.shape, 1)
                rows[at + 2 * split : at + tails, :] = jnp.where(lane < TAIL, own, 0.0)
        ready[r] = rows[...].astype(BF16)


def pack_kernel(steps, x, *refs):
    n = len(CHUNKS)
    outs, held, ready, wide = refs[:n], refs[n], refs[n + 1 : 2 * n + 1], refs[2 * n + 1]
    rows, got, put = refs[2 * n + 2 : 3 * n + 2], refs[3 * n + 2], refs[3 * n + 3]
    pieces = LON // BLOCK * steps

    def enter(i):
        q, t = i // steps, i % steps
        return pltpu.make_async_copy(x.at[t, pl.ds(pl.multiple_of(q * BLOCK, 8), BLOCK)], held.at[i], got.at[i])

    def leave(c, i):
        q, t = i // steps, i % steps
        return pltpu.make_async_copy(ready[c].at[i], outs[c].at[pl.ds(q * 8, 8), t], put.at[c, i])

    for i in range(pieces):
        enter(i).start()
    for c, chunk in enumerate(CHUNKS):
        total = rows_of(chunk)
        rows[c][total - 8 :, :] = jnp.zeros((8, LANES), F32)

    def piece(i, carry):
        enter(i).wait()
        for j in range(FULL):
            wide[j] = held[i, :, j * LANES : (j + 1) * LANES].astype(F32)
        wide[FULL, :, :TAIL] = held[i, :, FULL * LANES :].astype(F32)
        for c, chunk in enumerate(CHUNKS):
            pack_rows(STARTS[c], chunk, wide, rows[c], ready[c].at[i])
            leave(c, i).start()
        return carry

    lax.fori_loop(0, pieces, piece, 0)
    for c in range(n):
        for i in range(pieces):
            leave(c, i).wait()


def pack(x):
    steps = x.shape[0]
    totals = [rows_of(n) for n in CHUNKS]
    pieces = LON // BLOCK * steps
    return pl.pallas_call(
        functools.partial(pack_kernel, steps),
        in_specs=[ANY],
        out_specs=[ANY] * len(CHUNKS),
        out_shape=[jax.ShapeDtypeStruct((PEERS, steps, total, LANES), BF16) for total in totals],
        scratch_shapes=[pltpu.VMEM((pieces, BLOCK, LAT), BF16)]
        + [pltpu.VMEM((pieces, 8, total, LANES), BF16) for total in totals]
        + [pltpu.VMEM((FULL + 1, BLOCK, LANES), F32)]
        + [pltpu.VMEM((total, LANES), F32) for total in totals]
        + [pltpu.SemaphoreType.DMA((pieces,)), pltpu.SemaphoreType.DMA((len(CHUNKS), pieces))],
        cost_estimate=pl.CostEstimate(flops=10_000_000, bytes_accessed=17_000_000, transcendentals=0),
        name="pack",
    )(x)


def day_rows(table, stride, index):
    halves = [table[pl.ds(8 * h * stride + index, 8, stride=stride), :] for h in range(DAYS // 8)]
    return jnp.concatenate(halves, axis=0)


def unpack_rows(row, outs, block):
    first, base, count, tails, split = block
    lane = lax.broadcasted_iota(jnp.int32, (DAYS, LANES), 1)
    at = base + FULL * count

    def whole(lon):
        for j in range(FULL):
            for out, value in zip(outs, row(base + j * count + lon)):
                out[first + lon, :, j * LANES : (j + 1) * LANES] = value.astype(BF16)

    def tail(lon):
        for out, value in zip(outs, row(at + lon)):
            out[first + lon, :, FULL * LANES :] = value[:, :TAIL].astype(BF16)

    def last(k):
        for out, low, high in zip(outs, row(at + k), row(at + split + k)):
            low = pltpu.roll(low, LANES - TAIL, 1)
            high = pltpu.roll(high, LANES - TAIL + HALF, 1)
            joined = jnp.where(lane < HALF, low, high)
            out[first + tails + k, :, FULL * LANES :] = joined[:, :TAIL].astype(BF16)

    loop(count, whole, 3)
    loop(tails, tail, 2)
    loop(split, last, 1)


def unpack(table, scale, out, chunk):
    stride = rows_of(chunk) + 1

    def row(index):
        value = day_rows(table, stride, index)
        return [value if scale is None else value * scale]

    for block in blocks_of(chunk):
        unpack_rows(row, [out], block)


def zero(table, stride):
    for d in range(DAYS):
        table[d * stride : (d + 1) * stride, :] = jnp.zeros((stride, LANES), F32)


def add_up(bins, x, held, got, mean, total):
    stride = total + 1

    def add(t, carry):
        at = bins[t] * stride
        for k in range(total // 8):
            rows = pl.ds(at + 8 * k, 8)
            mean[rows, :] = mean[rows, :] + held[t, 8 * k : 8 * k + 8].astype(F32)
        return carry

    def adds(i, carry):
        enter(x, held, got, i).wait()
        return lax.fori_loop(0, SPAN, lambda t, c: add(i * SPAN + t, c), carry, unroll=4)

    lax.fori_loop(0, STEPS, adds, 0)


def enter(x, held, got, i):
    span = pl.ds(i * SPAN, SPAN)
    return pltpu.make_async_copy(x.at[span], held.at[span], got.at[i])


def divide(inverse, scale, mean, packed, total):
    stride = total + 1
    base = 0
    for rows in packed:

        def one(k, rows=rows, base=base):
            rows[k] = (day_rows(mean, stride, base + k) * scale[...]).astype(BF16)

        loop(rows.shape[0], one, 4)
        base += rows.shape[0]
    for d in range(DAYS):
        rows = slice(d * stride, d * stride + total)
        mean[rows, :] = mean[rows, :] * inverse[d]


def powers(bins, held, mean, second, third, weight, norm, total, ready=None):
    stride = total + 1

    def one(t, carry):
        at = bins[t] * stride
        sums = None
        for k in range(total // 8):
            rows = pl.ds(at + 8 * k, 8)
            tile = slice(8 * k, 8 * k + 8)
            a = held[t, tile].astype(F32) - mean[rows, :]
            q = a * a
            second[rows, :] = second[rows, :] + q
            third[rows, :] = third[rows, :] + q * a
            w = q * weight[tile, :]
            sums = w if sums is None else sums + w
        norm[t] = sums
        return carry

    def some(i, carry):
        if ready is not None:
            ready(i)
        return lax.fori_loop(0, SPAN, lambda t, c: one(i * SPAN + t, c), carry, unroll=2 if total > 100 else 4)

    lax.fori_loop(0, STEPS, some, 0)


def total_norm(norm):
    return jnp.sum(jnp.sum(norm[...], axis=1).T, axis=0, keepdims=True)


def leave(wide, outs, put, first, count, i):
    return pltpu.make_async_copy(wide.at[i], outs[i].at[pl.ds(first, count)], put.at[i])


def sum_kernel(total, bins, inverse, scale, x, mean, *refs):
    packed, held, got = refs[:-2], refs[-2], refs[-1]
    for i in range(STEPS):
        enter(x, held, got, i).start()
    zero(mean, total + 1)
    add_up(bins, x, held, got, mean, total)
    divide(inverse, scale, mean, packed, total)


def table_shape(total):
    return (DAYS * (total + 1), LANES)


def row_shape(total):
    return jax.ShapeDtypeStruct((total, DAYS, LANES), BF16)


def sums(bins, inverse, scale, x, chunk):
    total = rows_of(chunk)
    return pl.pallas_call(
        functools.partial(sum_kernel, total),
        in_specs=[SMEM, SMEM, VMEM, ANY],
        out_specs=[VMEM] * (1 + len(chunk)),
        out_shape=[jax.ShapeDtypeStruct(table_shape(total), F32)] + [row_shape(block_rows(n)) for n in chunk],
        scratch_shapes=[pltpu.VMEM((TIME, total, LANES), BF16), pltpu.SemaphoreType.DMA((STEPS,))],
        cost_estimate=pl.CostEstimate(flops=3_000_000 * sum(chunk), bytes_accessed=230_000 * sum(chunk), transcendentals=0),
        name="sums",
    )(bins, inverse, scale, x)


def power_kernel(first, chunk, bins, x, mean, scale, weight, *refs):
    outs, (after, held, second, third, norm, wide, got, put) = refs[:3], refs[3:]
    total = rows_of(chunk)
    count = sum(chunk)
    for i in range(STEPS):
        enter(x, held, got, i).start()
    zero(second, total + 1)
    zero(third, total + 1)
    unpack(mean, None, wide.at[0], chunk)
    leave(wide, outs, put, first, count, 0).start()
    powers(
        bins, held, mean, second, third, weight, norm, total, lambda i: enter(x, held, got, i).wait()
    )
    after[...] = total_norm(norm)
    for i, table in ((1, second), (2, third)):
        unpack(table, scale[...], wide.at[i], chunk)
        leave(wide, outs, put, first, count, i).start()
    for i in range(3):
        leave(wide, outs, put, first, count, i).wait()


FIELD = jax.ShapeDtypeStruct((BAND, DAYS, LAT), BF16)


def higher(bins, x, mean, scale, weight, first, chunk):
    total = rows_of(chunk)
    result = pl.pallas_call(
        functools.partial(power_kernel, first, chunk),
        in_specs=[SMEM, ANY] + [VMEM] * 3,
        out_specs=[ANY] * 3 + [VMEM],
        out_shape=[FIELD] * 3 + [jax.ShapeDtypeStruct((1, TIME), F32)],
        scratch_shapes=[
            pltpu.VMEM((TIME, total, LANES), BF16),
            pltpu.VMEM(table_shape(total), F32),
            pltpu.VMEM(table_shape(total), F32),
            pltpu.VMEM((TIME, 8, LANES), F32),
            pltpu.VMEM((3, sum(chunk), DAYS, LAT), BF16),
            pltpu.SemaphoreType.DMA((STEPS,)),
            pltpu.SemaphoreType.DMA((3,)),
        ],
        cost_estimate=pl.CostEstimate(flops=13_000_000 * sum(chunk), bytes_accessed=330_000 * sum(chunk), transcendentals=0),
        name="higher",
    )(bins, x, mean, scale, weight)
    return result[:3], result[3]


def both_kernel(first, chunk, bins, inverse, scale, x, weight, before, *refs):
    outs, (packed, after, held, mean, second, third, norm, wide, got, put) = refs[3:6], refs[6:]
    total = rows_of(chunk)
    count = sum(chunk)
    for i in range(STEPS):
        enter(x, held, got, i).start()
    for table in (mean, second, third):
        zero(table, total + 1)
    add_up(bins, x, held, got, mean, total)
    divide(inverse, scale, mean, (packed,), total)
    unpack(mean, None, wide.at[0], chunk)
    leave(wide, outs, put, first, count, 0).start()
    powers(bins, held, mean, second, third, weight, norm, total)
    row = before[...] + total_norm(norm)
    after[:, 0, :] = jnp.broadcast_to(row, (MODELS * PEERS, TIME))
    for i, table in ((1, second), (2, third)):
        unpack(table, scale[...], wide.at[i], chunk)
        leave(wide, outs, put, first, count, i).start()
    for i in range(3):
        leave(wide, outs, put, first, count, i).wait()


def both(bins, inverse, scale, x, weight, before, outs, first, chunk):
    total = rows_of(chunk)
    result = pl.pallas_call(
        functools.partial(both_kernel, first, chunk),
        in_specs=[SMEM, SMEM, VMEM, ANY, VMEM, VMEM] + [ANY] * 3,
        out_specs=[ANY] * 3 + [VMEM] * 2,
        out_shape=[FIELD] * 3 + [row_shape(block_rows(*chunk)), jax.ShapeDtypeStruct((MODELS * PEERS, 1, TIME), F32)],
        input_output_aliases={6: 0, 7: 1, 8: 2},
        scratch_shapes=[
            pltpu.VMEM((TIME, total, LANES), BF16),
            pltpu.VMEM(table_shape(total), F32),
            pltpu.VMEM(table_shape(total), F32),
            pltpu.VMEM(table_shape(total), F32),
            pltpu.VMEM((TIME, 8, LANES), F32),
            pltpu.VMEM((3, sum(chunk), DAYS, LAT), BF16),
            pltpu.SemaphoreType.DMA((STEPS,)),
            pltpu.SemaphoreType.DMA((3,)),
        ],
        cost_estimate=pl.CostEstimate(flops=16_000_000 * sum(chunk), bytes_accessed=330_000 * sum(chunk), transcendentals=0),
        name="both",
        compiler_params=grant(24),
    )(bins, inverse, scale, x, weight, before, *outs)
    return result[:3], result[3], result[4]


def family_kernel(first, count, chained, share, *refs):
    means = refs[:MODELS]
    out, held, wide, got, put = refs[MODELS + (1 if chained else 0) :]

    def enter(k):
        return pltpu.make_async_copy(means[k], held.at[k], got.at[k])

    def leave(f):
        return pltpu.make_async_copy(wide.at[f], out.at[f, pl.ds(first, count)], put.at[f])

    for k in range(MODELS):
        enter(k).start()
    for k in range(MODELS):
        enter(k).wait()
    shares = [[share[f, k] for k in range(MODELS)] for f in range(FAM)]

    def row(index):
        values = [held[k, index].astype(F32) for k in range(MODELS)]
        results = []
        for f in range(FAM):
            value = values[0] * shares[f][0]
            for k in range(1, MODELS):
                value = value + values[k] * shares[f][k]
            results.append(value)
        return results

    (block,) = blocks_of((count,))
    unpack_rows(row, [wide.at[f] for f in range(FAM)], block)
    for f in range(FAM):
        leave(f).start()
    for f in range(FAM):
        leave(f).wait()


def families(share, means, out, first, count, limit=None):
    chained = out is not None
    return pl.pallas_call(
        functools.partial(family_kernel, first, count, chained),
        in_specs=[SMEM] + [ANY] * MODELS + [ANY] * (1 if chained else 0),
        out_specs=ANY,
        out_shape=jax.ShapeDtypeStruct((FAM, BAND, DAYS, LAT), BF16),
        input_output_aliases={1 + MODELS: 0} if chained else {},
        scratch_shapes=[
            pltpu.VMEM((MODELS, block_rows(count), DAYS, LANES), BF16),
            pltpu.VMEM((FAM, count, DAYS, LAT), BF16),
            pltpu.SemaphoreType.DMA((MODELS,)),
            pltpu.SemaphoreType.DMA((FAM,)),
        ],
        cost_estimate=pl.CostEstimate(flops=3_000_000 * count, bytes_accessed=170_000 * count, transcendentals=0),
        compiler_params=None if limit is None else grant(limit),
    )(share, *means, *(() if out is None else (out,)))


def moved(array, by):
    return lax.ppermute(array, "group", [(i, (i + by) % MODELS) for i in range(MODELS)])


def from_others(mean):
    return [mean, *(moved(mean, by) for by in (1, -1, 2))]


def exchange(array):
    return lax.all_to_all(array, "tm", split_axis=0, concat_axis=0, tiled=True)


def local(precip, day_bins, family_of):
    sent = pack(precip[0])
    got0, later, day_bins, family_of = lax.optimization_barrier((exchange(sent[0]), sent[1], day_bins, family_of))
    got1 = exchange(later)

    days = jnp.arange(DAYS, dtype=jnp.int32)
    counts = jnp.sum((day_bins[None, :] == days[:, None]).astype(F32), axis=1)
    inverse = 1.0 / jnp.maximum(counts, 1.0)
    scale = jnp.broadcast_to(inverse[:, None], (DAYS, LANES))

    group = lax.axis_index("group")
    turned = (group + jnp.array([0, MODELS - 1, 1, 2], dtype=jnp.int32)) % MODELS
    models = jnp.arange(MODELS, dtype=jnp.int32)
    hot = (family_of[None, :] == jnp.arange(FAM, dtype=jnp.int32)[:, None]).astype(F32)
    members = jnp.maximum(jnp.sum(hot, axis=1), 1.0)
    at = (turned[:, None] == models[None, :]).astype(F32)
    share = jnp.sum(hot[:, None, :] * at[None], axis=2) / members[:, None]

    weight0, total_weight = packed_weight(CHUNKS[0])
    weight1, _ = packed_weight(CHUNKS[1])
    x0 = got0.reshape(TIME, rows_of(CHUNKS[0]), LANES)
    table0, *mean0 = sums(day_bins, inverse, scale, x0, CHUNKS[0])
    means0a = from_others(mean0[0])
    means0b = from_others(mean0[1])
    outs, norm0 = higher(day_bins, x0, table0, scale, jnp.asarray(weight0), STARTS[0], CHUNKS[0])
    first_block, second_block = CHUNKS[0]
    fam = families(share, means0a, None, 0, first_block, LIMITS[0])
    got1, norm0, fam = lax.optimization_barrier((got1, norm0, fam))
    x1 = got1.reshape(TIME, rows_of(CHUNKS[1]), LANES)
    outs, mean1, norm = both(
        day_bins, inverse, scale, x1, jnp.asarray(weight1), norm0, outs, STARTS[1], CHUNKS[1]
    )
    means1 = from_others(mean1)
    parts = lax.all_to_all(norm, ("group", "tm"), split_axis=0, concat_axis=0, tiled=True)
    fam = families(share, means0b, fam, first_block, second_block, LIMITS[1])
    fam = families(share, means1, fam, STARTS[1], CHUNKS[1][0], LIMITS[2])
    parts, fam = lax.optimization_barrier((parts, fam))

    anomaly_norm = jnp.sqrt(jnp.sum(parts.reshape(MODELS, PEERS, TIME), axis=1) / total_weight)
    fields = [o[None].transpose(0, 2, 1, 3) for o in outs]
    return (*fields, fam.transpose(0, 2, 1, 3), anomaly_norm)


def solution(mesh):
    in_specs = (P("group", "tm", None, None), P(), P())
    out_specs = (
        P("group", None, "tm", None),
        P("group", None, "tm", None),
        P("group", None, "tm", None),
        P(None, None, "tm", None),
        P(),
    )
    return jax.shard_map(local, mesh=mesh, in_specs=in_specs, out_specs=out_specs, check_vma=False)
```

time: 179 us -> 163 us (0.911)
  waiting for transfers between devices: 26.5 us -> 5.48 us
  starting transfers between devices: 24.9 us -> 34.6 us
  blocking collectives: 82.6 us -> 77.3 us
    ppermute x9, waiting for transfers between devices: 26.4 us -> 3.43 us  [moved(): lax.ppermute(array, 'group', [(i, (i + by) % MODELS) for i in range(MODEL...]
    all_to_all x1, starting transfers between devices: 8.04 us -> 17.6 us  [local(): lax.all_to_all(norm, ('group', 'tm'), split_axis=0, concat_axis=0, tiled=...]
    all_to_all x1, blocking collectives: 82.6 us -> 77.3 us  [exchange(): return lax.all_to_all(array, 'tm', split_axis=0, concat_axis=0, tiled=True)]
    all_to_all x1, waiting for transfers between devices: 0.01 us -> 2.05 us  [local(): lax.all_to_all(norm, ('group', 'tm'), split_axis=0, concat_axis=0, tiled=...]
    pallas_call x4 -> x5, Pallas kernels: 27.1 us -> 28.9 us  [the longest x3 11.4 us: families(): pl.pallas_call(functools.partial(family_kernel, first, count, chained), i...]
  transfers between devices with their start and end apart: 11 -> 11, of which waited for: 5 -> 2; matrix products, arithmetic and copies ran while one was open for 1% -> 1% of each run, Pallas kernels for 17% -> 21%
where the time goes in v6:
time: 163 us; the launch traced here: 162 us
  blocking collectives  77.3 us (47%)
  Pallas kernels  41.3 us (25%)
  starting transfers between devices  34.6 us (21%)
  waiting for transfers between devices  5.48 us (3%)
  other arithmetic  1.68 us (1%)
    all_to_all x1, blocking collectives, exchange(): return lax.all_to_all(array, 'tm', split_axis=0, concat_axis=0, tiled=True)  77.3 us
    all_to_all x1, starting transfers between devices, local(): lax.all_to_all(norm, ('group', 'tm'), split_axis=0, concat_axis=0, tiled=...  17.6 us
    ppermute x9, starting transfers between devices, moved(): lax.ppermute(array, 'group', [(i, (i + by) % MODELS) for i in range(MODEL...  13 us
    pallas_call x3, Pallas kernels, families(): pl.pallas_call(functools.partial(family_kernel, first, count, chained), i...  11.4 us
    pallas_call x1, Pallas kernels, higher(): pl.pallas_call(functools.partial(power_kernel, first, chunk), in_specs=[S...  10.4 us
    pallas_call x1, Pallas kernels, pack(): pl.pallas_call(functools.partial(pack_kernel, steps), in_specs=[ANY], out...  7.13 us
    pallas_call x1, Pallas kernels, both(): pl.pallas_call(functools.partial(both_kernel, first, chunk), in_specs=[SM...  7.06 us
    pallas_call x1, Pallas kernels, sums(): pl.pallas_call(functools.partial(sum_kernel, total), in_specs=[SMEM, SMEM...  5.32 us
  transfers between devices with their start and end apart: 11, of which 2 were waited for; matrix products, arithmetic and copies ran while one was open for 1% of the time, Pallas kernels for 21%

profile of v6, /device:TPU:1, one launch (start us, length us, event | category | flops | bytes accessed | tf_op | source)
XLA Modules:
  0.0 162.0 jit_solution(14768105592185894991)
XLA Ops:
  0.6 7.1 %pack.1 = (bf16[32,4,176,128]{3,2,1,0:T(8,128)(2,1)}, bf16[32,4,80,128]{3,2,1,0:T(8,128)(2,1)}) custom-call(bf16[4,1440,720]{2,1,0:T(8,128)(2,1)} %bitcast.20), custom_call_target="tpu_custom_call" | custom-call | flops 10000000 | bytes 17000000 | tf_op jit(solution)/shard_map/pack/pallas_call | solution.py:153
  7.8 77.3 %all_to_all.15 = bf16[32,4,176,128]{3,2,1,0:T(8,128)(2,1)} all-to-all(bf16[32,4,176,128]{3,2,1,0:T(8,128)(2,1)} %get-tuple-element.28), channel_id=1, replica_groups=mesh['group'=4,'tm'=32] {'tm'}, dimensions={0} | all-to-all | bytes 11534336 | tf_op jit(solution)/shard_map/all_to_all | solution.py:471
  85.1 4.0 %all-to-all-start.1 = ((bf16[32,4,80,128]{3,2,1,0:T(8,128)(2,1)}), bf16[32,4,80,128]{3,2,1,0:T(8,128)(2,1)S(1)}, u32[]{:S(2)}, u32[]{:S(2)}) async-start(bf16[32,4,80,128]{3,2,1,0:T(8,128)(2,1)} %get-tuple-element.31), calls=%async_computation.1 | async-start | bytes 5242880 | tf_op jit(solution)/shard_map/all_to_all | solution.py:471
  89.1 0.0 copy-done.10
  89.1 0.1 fusion.1
  89.2 0.0 copy-done.3
  89.2 0.1 convert_reduce_fusion
  89.3 0.7 broadcast_in_dim.8.scale
  90.0 0.0 copy-done.5
  90.0 5.3 %sums.1 = (f32[2832,128]{1,0:T(8,128)}, bf16[85,16,128]{2,1,0:T(8,128)(2,1)}, bf16[91,16,128]{2,1,0:T(8,128)(2,1)}) custom-call(s32[128]{0:T(128)} %bins.2, f32[16]{0:T(128)} %copy-done.5, f32[16,128]{1,0:T(8,128)} %broadcast_in_dim.8.scale, bf16[128,176,128]{2,1,0:T(8,128)(2,1)} %bitcast.17), custom_call_target="tpu_custom_call" | custom-call | flops 93000000 | bytes 7130000 | tf_op jit(solution)/shard_map/sums/pallas_call | solution.py:305
  95.3 1.4 collective-permute-start
  96.7 1.5 collective-permute-start.1
  98.2 1.6 collective-permute-start.2
  99.8 0.4 collective-permute-start.6
  100.2 2.3 %collective-permute-start.7 = (bf16[91,16,128]{2,1,0:T(8,128)(2,1)}, bf16[91,16,128]{2,1,0:T(8,128)(2,1)}, u32[]{:S(2)}, u32[]{:S(2)}) collective-permute-start(bf16[91,16,128]{2,1,0:T(8,128)(2,1)} %get-tuple-element.47.refs_0_), channel_id=1, source_target_pairs={{0,96},{32,0},{64,32},{96,64},{1,97},{33,1},{65,33},{97,65},{2,98}... | collective-permute-start | bytes 1118216 | tf_op jit(solution)/shard_map/ppermute | solution.py:463
  102.4 0.0 copy-done.9
  102.4 0.1 fusion.3
  102.6 0.1 multiply_reduce_fusion
  102.7 0.7 broadcast_divide_fusion.share
  103.3 3.4 %collective-permute-done.refs_1_ = bf16[85,16,128]{2,1,0:T(8,128)(2,1)} collective-permute-done((bf16[85,16,128]{2,1,0:T(8,128)(2,1)}, bf16[85,16,128]{2,1,0:T(8,128)(2,1)}, u32[]{:S(2)}, u32[]{:S(2)}) %collective-permute-start) | collective-permute-done | bytes 348192 | tf_op jit(solution)/shard_map/ppermute | solution.py:463
  106.7 1.7 %collective-permute-start.8 = (bf16[91,16,128]{2,1,0:T(8,128)(2,1)}, bf16[91,16,128]{2,1,0:T(8,128)(2,1)}, u32[]{:S(2)}, u32[]{:S(2)}) collective-permute-start(bf16[91,16,128]{2,1,0:T(8,128)(2,1)} %get-tuple-element.47.refs_0_), channel_id=1, source_target_pairs={{0,64},{32,96},{64,0},{96,32},{1,65},{33,97},{65,1},{97,33},{2,66}... | collective-permute-start | bytes 1118216 | tf_op jit(solution)/shard_map/ppermute | solution.py:463
  108.4 10.4 %higher.1 = (bf16[45,16,720]{2,1,0:T(8,128)(2,1)}, bf16[45,16,720]{2,1,0:T(8,128)(2,1)}, bf16[45,16,720]{2,1,0:T(8,128)(2,1)}, f32[1,128]{1,0:T(1,128)}) custom-call(s32[128]{0:T(128)} %bins.2, bf16[128,176,128]{2,1,0:T(8,128)(2,1)} %bitcast.18, f32[2832,128]{1,0:T(8,128)} %get-tuple-element.33.mean, f32[16,128]{1,0:T(8,128)} %broadcast_in_dim.8.scale, ...), custom_call_target="tpu_custom_call" | custom-call | flops 403000000 | bytes 10230000 | tf_op jit(solution)/shard_map/higher/pallas_call | solution.py:342
  118.8 0.0 copy-start
  118.8 0.0 copy-start.1
  118.8 0.0 copy-start.4
  118.8 0.0 copy-start.6
  118.8 0.0 copy-start.7
  118.8 0.0 collective-permute-done.1.refs_2_
  118.8 0.0 collective-permute-done.2.refs_3_
  118.8 4.2 %shard_map.101.refs_4_ = bf16[3,45,16,720]{3,2,1,0:T(8,128)(2,1)} custom-call(f32[3,4]{1,0:T(4,128)} %broadcast_divide_fusion.share, bf16[85,16,128]{2,1,0:T(8,128)(2,1)} %get-tuple-element.36.refs_0_, bf16[85,16,128]{2,1,0:T(8,128)(2,1)} %collective-permute-done.refs_1_, bf16[85,16,128]{2,1,0:T(8,128)(2,1)} %collective-permute-done.1.refs_2_, ...), custom_call_target="tpu_custom_call" | custom-call | flops 45000000 | bytes 2550000 | tf_op jit(solution)/shard_map/pallas_call | solution.py:445
  123.0 0.0 all-to-all-done.1
  123.1 7.1 %both.1 = (bf16[45,16,720]{2,1,0:T(8,128)(2,1)}, bf16[45,16,720]{2,1,0:T(8,128)(2,1)}, bf16[45,16,720]{2,1,0:T(8,128)(2,1)}, bf16[80,16,128]{2,1,0:T(8,128)(2,1)S(1)}, f32[128,1,128]{2,1,0:T(1,128)}) custom-call(s32[128]{0:T(128)S(1)} %copy-done.4, f32[16]{0:T(128)S(1)} %copy-done.6, ...), custom_call_target="tpu_custom_call", output_to_operand_aliasing={{0}: (6, {}), {1}: (7, {}), {2}: (8, {})} | custom-call | flops 224000000 | bytes 4620000 | tf_op jit(solution)/shard_map/both/pallas_call | solution.py:386
  130.1 1.1 collective-permute-start.3
  131.2 1.7 %collective-permute-start.4 = (bf16[80,16,128]{2,1,0:T(8,128)(2,1)S(1)}, bf16[80,16,128]{2,1,0:T(8,128)(2,1)S(1)}, u32[]{:S(2)}, u32[]{:S(2)}) collective-permute-start(bf16[80,16,128]{2,1,0:T(8,128)(2,1)S(1)} %get-tuple-element.46.refs_0_), channel_id=1, source_target_pairs={{0,96},{32,0},{64,32},{96,64},{1,97},{33,1},{65,33},{97,65},{2,98}... | collective-permute-start | bytes 983048 | tf_op jit(solution)/shard_map/ppermute | solution.py:463
  132.9 0.0 collective-permute-done.6.refs_1_
  132.9 1.4 collective-permute-start.5
  134.3 17.6 %all-to-all-start.2 = ((f32[128,1,128]{2,1,0:T(1,128)}), f32[128,1,128]{2,1,0:T(1,128)S(1)}, u32[]{:S(2)}, u32[]{:S(2)}) async-start(f32[128,1,128]{2,1,0:T(1,128)} %get-tuple-element.45), calls=%async_computation.2 | async-start | bytes 131072 | tf_op jit(solution)/shard_map/all_to_all | solution.py:507
  152.0 0.0 copy-start.2
  152.0 0.0 collective-permute-done.7.refs_2_
  152.0 0.0 collective-permute-done.8.refs_3_
  152.0 0.0 copy-done.8
  152.0 4.3 %shard_map.102.refs_4_ = bf16[3,45,16,720]{3,2,1,0:T(8,128)(2,1)} custom-call(f32[3,4]{1,0:T(4,128)} %broadcast_divide_fusion.share, bf16[91,16,128]{2,1,0:T(8,128)(2,1)} %get-tuple-element.47.refs_0_, bf16[91,16,128]{2,1,0:T(8,128)(2,1)} %copy-done.8, bf16[91,16,128]{2,1,0:T(8,128)(2,1)} %collective-permute-done.7.refs_2_, ...), custom_call_target="tpu_custom_call", output_to_operand_aliasing={{}: (5, {})} | custom-call | flops 48000000 | bytes 2720000 | tf_op jit(solution)/shard_map/pallas_call | solution.py:445
  156.3 0.0 collective-permute-done.3.refs_1_
  156.3 0.0 collective-permute-done.4.refs_2_
  156.3 0.0 collective-permute-done.5.refs_3_
  156.3 3.0 %shard_map.103 = bf16[3,45,16,720]{3,2,1,0:T(8,128)(2,1)} custom-call(f32[3,4]{1,0:T(4,128)S(1)} %copy-done.2, bf16[80,16,128]{2,1,0:T(8,128)(2,1)S(1)} %get-tuple-element.46.refs_0_, bf16[80,16,128]{2,1,0:T(8,128)(2,1)S(1)} %collective-permute-done.3.refs_1_, ...), custom_call_target="tpu_custom_call", output_to_operand_aliasing={{}: (5, {})} | custom-call | flops 42000000 | bytes 2380000 | tf_op jit(solution)/shard_map/pallas_call | solution.py:445
  159.4 2.0 %all-to-all-done.2 = f32[128,1,128]{2,1,0:T(1,128)S(1)} async-done(((f32[128,1,128]{2,1,0:T(1,128)}), f32[128,1,128]{2,1,0:T(1,128)S(1)}, u32[]{:S(2)}, u32[]{:S(2)}) %all-to-all-start.2) | async-done | bytes 65568 | tf_op jit(solution)/shard_map/all_to_all | solution.py:507
  161.4 0.6 multiply_sqrt_fusion
  (16 shorter events, 0.1 us)
Async XLA Ops:
  85.1 4.0 %copy-start.10 = (s32[4]{0:T(128)S(1)}, s32[4]{0:T(128)}, u32[]{:S(2)}) copy-start(s32[4]{0:T(128)} %constant.35.clone) | copy-start | bytes 52
  85.1 4.1 %copy-start.3 = (s32[128]{0:T(128)S(1)}, s32[128]{0:T(128)}, u32[]{:S(2)}) copy-start(s32[128]{0:T(128)} %bins.2) | copy-start | bytes 1540
  85.1 37.9 %all-to-all-start.1 = ((bf16[32,4,80,128]{3,2,1,0:T(8,128)(2,1)}), bf16[32,4,80,128]{3,2,1,0:T(8,128)(2,1)S(1)}, u32[]{:S(2)}, u32[]{:S(2)}) async-start(bf16[32,4,80,128]{3,2,1,0:T(8,128)(2,1)} %get-tuple-element.31), calls=%async_computation.1 | async-start | bytes 5242880 | tf_op jit(solution)/shard_map/all_to_all | solution.py:471
  89.3 0.7 copy-start.5
  90.0 12.5 %copy-start.9 = (s32[4]{0:T(128)S(1)}, s32[4]{0:T(128)}, u32[]{:S(2)}) copy-start(s32[4]{0:T(128)} %param.8) | copy-start | bytes 52
  95.3 11.4 %collective-permute-start = (bf16[85,16,128]{2,1,0:T(8,128)(2,1)}, bf16[85,16,128]{2,1,0:T(8,128)(2,1)}, u32[]{:S(2)}, u32[]{:S(2)}) collective-permute-start(bf16[85,16,128]{2,1,0:T(8,128)(2,1)} %get-tuple-element.36.refs_0_), channel_id=1, source_target_pairs={{0,32},{32,64},{64,96},{96,0},{1,33},{33,65},{65,97},{97,1},{2,34}... | collective-permute-start | bytes 1044488 | tf_op jit(solution)/shard_map/ppermute | solution.py:463
  96.7 22.2 %collective-permute-start.1 = (bf16[85,16,128]{2,1,0:T(8,128)(2,1)}, bf16[85,16,128]{2,1,0:T(8,128)(2,1)}, u32[]{:S(2)}, u32[]{:S(2)}) collective-permute-start(bf16[85,16,128]{2,1,0:T(8,128)(2,1)} %get-tuple-element.36.refs_0_), channel_id=1, source_target_pairs={{0,96},{32,0},{64,32},{96,64},{1,97},{33,1},{65,33},{97,65},{2,98}... | collective-permute-start | bytes 1044488 | tf_op jit(solution)/shard_map/ppermute | solution.py:463
  98.2 20.6 %collective-permute-start.2 = (bf16[85,16,128]{2,1,0:T(8,128)(2,1)}, bf16[85,16,128]{2,1,0:T(8,128)(2,1)}, u32[]{:S(2)}, u32[]{:S(2)}) collective-permute-start(bf16[85,16,128]{2,1,0:T(8,128)(2,1)} %get-tuple-element.36.refs_0_), channel_id=1, source_target_pairs={{0,64},{32,96},{64,0},{96,32},{1,65},{33,97},{65,1},{97,33},{2,66}... | collective-permute-start | bytes 1044488 | tf_op jit(solution)/shard_map/ppermute | solution.py:463
  99.8 33.1 %collective-permute-start.6 = (bf16[91,16,128]{2,1,0:T(8,128)(2,1)}, bf16[91,16,128]{2,1,0:T(8,128)(2,1)S(1)}, u32[]{:S(2)}, u32[]{:S(2)}) collective-permute-start(bf16[91,16,128]{2,1,0:T(8,128)(2,1)} %get-tuple-element.47.refs_0_), channel_id=1, source_target_pairs={{0,32},{32,64},{64,96},{96,0},{1,33},{33,65},{65,97},{97,1},{2,34}... | collective-permute-start | bytes 1118216 | tf_op jit(solution)/shard_map/ppermute | solution.py:463
  100.2 51.8 %collective-permute-start.7 = (bf16[91,16,128]{2,1,0:T(8,128)(2,1)}, bf16[91,16,128]{2,1,0:T(8,128)(2,1)}, u32[]{:S(2)}, u32[]{:S(2)}) collective-permute-start(bf16[91,16,128]{2,1,0:T(8,128)(2,1)} %get-tuple-element.47.refs_0_), channel_id=1, source_target_pairs={{0,96},{32,0},{64,32},{96,64},{1,97},{33,1},{65,33},{97,65},{2,98}... | collective-permute-start | bytes 1118216 | tf_op jit(solution)/shard_map/ppermute | solution.py:463
  106.7 45.3 %collective-permute-start.8 = (bf16[91,16,128]{2,1,0:T(8,128)(2,1)}, bf16[91,16,128]{2,1,0:T(8,128)(2,1)}, u32[]{:S(2)}, u32[]{:S(2)}) collective-permute-start(bf16[91,16,128]{2,1,0:T(8,128)(2,1)} %get-tuple-element.47.refs_0_), channel_id=1, source_target_pairs={{0,64},{32,96},{64,0},{96,32},{1,65},{33,97},{65,1},{97,33},{2,66}... | collective-permute-start | bytes 1118216 | tf_op jit(solution)/shard_map/ppermute | solution.py:463
  118.8 4.3 %copy-start = (f32[16,128]{1,0:T(8,128)S(1)}, f32[16,128]{1,0:T(8,128)}, u32[]{:S(2)}) copy-start(f32[16,128]{1,0:T(8,128)} %broadcast_in_dim.8.scale) | copy-start | bytes 24580
  118.8 4.3 %copy-start.1 = (f32[80,128]{1,0:T(8,128)S(1)}, f32[80,128]{1,0:T(8,128)}, u32[]{:S(2)}) copy-start(f32[80,128]{1,0:T(8,128)} %constant.37.clone.weight) | copy-start | bytes 122884
  118.8 4.2 %copy-start.4 = (s32[128]{0:T(128)S(1)}, s32[128]{0:T(128)}, u32[]{:S(2)}) copy-start(s32[128]{0:T(128)} %bins.2) | copy-start | bytes 1540
  118.8 4.2 %copy-start.6 = (f32[16]{0:T(128)S(1)}, f32[16]{0:T(128)}, u32[]{:S(2)}) copy-start(f32[16]{0:T(128)} %copy-done.5) | copy-start | bytes 196
  118.8 4.2 %copy-start.7 = (f32[1,128]{1,0:T(1,128)S(1)}, f32[1,128]{1,0:T(1,128)}, u32[]{:S(2)}) copy-start(f32[1,128]{1,0:T(1,128)} %get-tuple-element.38.before) | copy-start | bytes 1540
  130.1 26.2 %collective-permute-start.3 = (bf16[80,16,128]{2,1,0:T(8,128)(2,1)S(1)}, bf16[80,16,128]{2,1,0:T(8,128)(2,1)S(1)}, u32[]{:S(2)}, u32[]{:S(2)}) collective-permute-start(bf16[80,16,128]{2,1,0:T(8,128)(2,1)S(1)} %get-tuple-element.46.refs_0_), channel_id=1, source_target_pairs={{0,32},{32,64},{64,96},{96,0},{1,33},{33,65},{65,97},{97,1},{2,34}... | collective-permute-start | bytes 983048 | tf_op jit(solution)/shard_map/ppermute | solution.py:463
  131.2 25.1 %collective-permute-start.4 = (bf16[80,16,128]{2,1,0:T(8,128)(2,1)S(1)}, bf16[80,16,128]{2,1,0:T(8,128)(2,1)S(1)}, u32[]{:S(2)}, u32[]{:S(2)}) collective-permute-start(bf16[80,16,128]{2,1,0:T(8,128)(2,1)S(1)} %get-tuple-element.46.refs_0_), channel_id=1, source_target_pairs={{0,96},{32,0},{64,32},{96,64},{1,97},{33,1},{65,33},{97,65},{2,98}... | collective-permute-start | bytes 983048 | tf_op jit(solution)/shard_map/ppermute | solution.py:463
  132.9 19.1 %copy-start.8 = (bf16[91,16,128]{2,1,0:T(8,128)(2,1)}, bf16[91,16,128]{2,1,0:T(8,128)(2,1)S(1)}, u32[]{:S(2)}) copy-start(bf16[91,16,128]{2,1,0:T(8,128)(2,1)S(1)} %collective-permute-done.6.refs_1_) | copy-start | bytes 1118212
  132.9 23.4 %collective-permute-start.5 = (bf16[80,16,128]{2,1,0:T(8,128)(2,1)S(1)}, bf16[80,16,128]{2,1,0:T(8,128)(2,1)S(1)}, u32[]{:S(2)}, u32[]{:S(2)}) collective-permute-start(bf16[80,16,128]{2,1,0:T(8,128)(2,1)S(1)} %get-tuple-element.46.refs_0_), channel_id=1, source_target_pairs={{0,64},{32,96},{64,0},{96,32},{1,65},{33,97},{65,1},{97,33},{2,66}... | collective-permute-start | bytes 983048 | tf_op jit(solution)/shard_map/ppermute | solution.py:463
  134.3 27.1 %all-to-all-start.2 = ((f32[128,1,128]{2,1,0:T(1,128)}), f32[128,1,128]{2,1,0:T(1,128)S(1)}, u32[]{:S(2)}, u32[]{:S(2)}) async-start(f32[128,1,128]{2,1,0:T(1,128)} %get-tuple-element.45), calls=%async_computation.2 | async-start | bytes 131072 | tf_op jit(solution)/shard_map/all_to_all | solution.py:507
  152.0 4.4 %copy-start.2 = (f32[3,4]{1,0:T(4,128)S(1)}, f32[3,4]{1,0:T(4,128)}, u32[]{:S(2)}) copy-start(f32[3,4]{1,0:T(4,128)} %broadcast_divide_fusion.share) | copy-start | bytes 148
